TPU v7x, 128 devices: a whole 4x4x4 slice. The times are simulated.
128 devices in a mesh: energy: 16 (over y, x), kpt: 8 (over z, core).
Axes of the slice: x: 4, y: 4, z: 4, core: 2. Of those that a mesh axis runs over, the one named last changes fastest.
Arguments:
- density: bfloat16 [64, 8, 128, 3072], P('energy', 'kpt'), may hold values from -6 to 6
- quad_weights: float32 [64, 8], P('energy', 'kpt'), may hold values from 0.022097087 to 0.088388346
- orbital_cells: int32 [128, 3072], replicated, may hold values from 0 to 262143
- fixed_charge: float32 [1024, 128, 256], P('energy', 'kpt'), may hold values from -16 to 16
- gate_mask: int32 [1024, 128, 256], P('energy', 'kpt'), may hold values 0 or 1
- gate_voltage: float32 [1024], P('energy'), may hold values from -1 to 1
Outputs:
- potential: float32 [1024, 128, 256], P('energy', 'kpt')
- band_shift: float32 [64, 8, 128], P('energy', 'kpt')
Inputs may be any that keep to these rules, and one draw needn't show every extreme that they name: `orbital_cells`: each entry is s * 128 * 256 + y * 256 + z, a cell of one of the layer's 8 planes.
All inputs are finite; a program needn't handle non-finite values. No bound on the sum of `gate_mask` on one device may be relied on, other than what follows from the above.
Results may differ from a plain program's by a relative error of at most 0.0003.
Values sent between devices are 32-bit elements; how exact they have to be, the bound alone decides.
No kernel may reach another device: no remote copies, remote signals or barrier semaphores. Data moves between devices by JAX's collectives and lax.ppermute only.
A program may use at most 64 MiB of HBM per device.

v0:
```python
import jax
import jax.numpy as jnp
from jax import lax
from jax.sharding import Mesh
from jax.sharding import PartitionSpec as P

LAYER_DEV = 8
SUB = 8
ITERS = 2
ENERGY_KPT = ("energy_0", "energy_1", "kpt_0", "kpt_1")
ENERGY = ("energy_0", "energy_1")
KPT = ("kpt_0", "kpt_1")


PENALTY = 4.0


def extended(x, sides, width):
    edges = {}
    for axis, dim in sides:
        peers, length = (lax.axis_size(axis), x.shape[dim])
        up = [(i, (i + 1) % peers) for i in range(peers - 1)]
        last = lax.slice_in_dim(x, length - width, length, axis=dim)
        first = lax.slice_in_dim(x, 0, width, axis=dim)
        edges[dim] = (
            lax.ppermute(last, axis, up),
            lax.ppermute(first, axis, [(b, a) for a, b in up]),
        )
    done = []
    for _, dim in sides:
        low, high = edges[dim]
        around = [(width, width) if d in done else (0, 0) for d in range(x.ndim)]
        x = jnp.concatenate([jnp.pad(low, around), x, jnp.pad(high, around)], axis=dim)
        done.append(dim)
    return x


def one_axis_at_a_time(x, axes):
    for axis in axes:
        x = lax.psum(x, axis)
    return x


def cut_along(x, dim, peers):
    lengths = x.shape
    tiles = x.reshape(*lengths[:dim], peers, lengths[dim] // peers, *lengths[dim + 1 :])
    return jnp.moveaxis(tiles, dim, 0)


def scatter_pairs(x, chips, core, dim):
    sizes = (lax.axis_size(chips), lax.axis_size(core))
    tiles = cut_along(x, dim, sizes[0] * sizes[1])
    inside = tiles.shape[1:]
    tiles = tiles.reshape(*sizes, *inside).swapaxes(0, 1).reshape(-1, *inside)
    tiles = lax.psum_scatter(tiles, core, scatter_dimension=0, tiled=True)
    return lax.psum_scatter(tiles, chips, scatter_dimension=0, tiled=True)[0]


def from_everyone(x, axis):
    copies = jnp.broadcast_to(x, (lax.axis_size(axis), *x.shape))
    return lax.all_to_all(copies, axis, split_axis=0, concat_axis=0, tiled=True)


def laid_out(tiles, dim):
    lengths = list(tiles.shape[1:])
    lengths[dim] *= tiles.shape[0]
    return jnp.moveaxis(tiles, 0, dim).reshape(lengths)


def gather_directly(x, axis, dim):
    tiles = from_everyone(x, axis)
    return laid_out(tiles, dim)


def over_copies(x, axis):
    return from_everyone(x, axis).sum(axis=0)


def operate(values_field, diagonal):
    padded = extended(values_field, ((ENERGY, 0), (KPT, 1)), 1)
    padded = jnp.pad(padded, ((0, 0), (0, 0), (1, 1)))
    beside = padded[2:, 1:-1, 1:-1] + padded[:-2, 1:-1, 1:-1]
    beside = beside + padded[1:-1, 2:, 1:-1] + padded[1:-1, :-2, 1:-1]
    beside = beside + padded[1:-1, 1:-1, 2:] + padded[1:-1, 1:-1, :-2]
    return diagonal * values_field - beside


def paired_sums(residual, image):
    return (
        one_axis_at_a_time(jnp.sum(residual * residual), ENERGY_KPT),
        one_axis_at_a_time(jnp.sum(residual * image), ENERGY_KPT),
    )


def window_index(map_rows, kpt_index, planes, cross_y, width_y, depth_z):
    section = cross_y * depth_z
    within = map_rows % section
    column = within // depth_z - kpt_index * width_y
    inside = (column >= 0) & (column < width_y)
    layer_rows = lax.broadcasted_iota(jnp.int32, map_rows.shape, 0)
    flat_cell = (
        (layer_rows * planes + map_rows // section) * width_y + jnp.clip(column, 0, width_y - 1)
    ) * depth_z + within % depth_z
    return (flat_cell, inside)


def per_device(density, quad_weights, orbital_cells, fixed_charge, gate_mask, gate_voltage):
    planes_dev, width_y, depth_z = fixed_charge.shape
    kpt_index = lax.axis_index(KPT)
    cross_y = width_y * lax.axis_size(KPT)
    occupancy = jnp.einsum(
        "ek,eklo->lo", quad_weights, density.astype(jnp.float32), precision=lax.Precision.HIGHEST
    )
    partial_rows = scatter_pairs(occupancy, ("energy_0", "energy_1", "kpt_0"), "kpt_1", 0)
    slab_occupancy = gather_directly(partial_rows, KPT, 0)
    slab_cells = lax.dynamic_slice_in_dim(
        orbital_cells, lax.axis_index(ENERGY) * LAYER_DEV, LAYER_DEV, 0
    )
    flat_cell, inside = window_index(slab_cells, kpt_index, SUB, cross_y, width_y, depth_z)
    deposit = jax.ops.segment_sum(
        jnp.where(inside, slab_occupancy, 0.0).reshape(-1),
        flat_cell.reshape(-1),
        num_segments=planes_dev * width_y * depth_z,
    )
    charge = deposit.reshape(planes_dev, width_y, depth_z)
    gated = gate_mask.astype(jnp.float32)
    diagonal = 6.0 + PENALTY * gated
    right_side = fixed_charge - charge + PENALTY * gated * gate_voltage[:, None, None]
    potential = jnp.zeros_like(right_side)
    residual = right_side
    image = operate(residual, diagonal)
    norm_now, product = paired_sums(residual, image)
    alpha = norm_now / product
    direction = residual
    along = image
    for sweep_index in range(ITERS):
        potential = potential + alpha * direction
        residual = residual - alpha * along
        if sweep_index + 1 < ITERS:
            image = operate(residual, diagonal)
            norm_next, product = paired_sums(residual, image)
            ratio = norm_next / norm_now
            alpha = norm_next / (product - ratio * norm_next / alpha)
            direction = residual + ratio * direction
            along = image + ratio * along
            norm_now = norm_next
    local_values = jnp.where(inside, jnp.take(potential.reshape(-1), flat_cell), 0.0)
    orbital_potential = over_copies(local_values, KPT)
    factor = density.shape[3] ** (-0.5)
    block = density.astype(jnp.float32)
    band_shift = (
        jnp.einsum(
            "eklo,lo->ekl",
            block,
            gather_directly(orbital_potential, ENERGY, 0),
            precision=lax.Precision.HIGHEST,
        )
        * factor
    )
    return (potential, band_shift)


def solution(mesh):
    split = Mesh(mesh.devices.reshape(4, 4, 4, 2), ("energy_0", "energy_1", "kpt_0", "kpt_1"))
    in_specs = (
        P(ENERGY, KPT, None, None),
        P(ENERGY, KPT),
        P(),
        P(ENERGY, KPT, None),
        P(ENERGY, KPT, None),
        P(ENERGY),
    )
    out_specs = (P(ENERGY, KPT, None), P(ENERGY, KPT, None))
    return jax.shard_map(
        per_device, mesh=split, in_specs=in_specs, out_specs=out_specs, check_vma=False
    )
```

profile of v0, /device:TPU:0, one launch (start us, length us, event | category | flops | bytes accessed | tf_op | source)
XLA Modules:
  0.0 621.8 jit_solution(6941981207994598572)
XLA Ops:
  7.2 4.3 copy.14
  11.6 5.2 fusion.27
  16.8 1.6 copy.10
  18.5 14.4 %reduce-scatter.3.cloned.1.call-done = f32[64,1,3072]{2,0,1:T(8,128)} async-done(((f32[128,1,3072]{2,0,1:T(8,128)}), f32[64,1,3072]{2,0,1:T(8,128)}) %reduce-scatter.3.cloned.1.call-update) | async-done | bytes 786448 | tf_op jit(solution)/shard_map/reduce_scatter | solution.py:55
  34.7 133.9 %all-reduce.17.cloned.1.call-done = f32[64,1,3072]{2,0,1:T(8,128)} async-done(((f32[64,1,3072]{2,0,1:T(8,128)}), f32[64,1,3072]{2,0,1:T(8,128)}) %all-reduce.17.cloned.1.call-update) | async-done | bytes 786448
  168.6 1.5 constant_dynamic-slice_fusion
  170.8 3.4 all-to-all-start
  174.3 5.7 all-to-all-done
  181.0 128.7 %scatter_custom_fusion = f32[262144]{0:T(1024)S(1)} fusion(s32[24576]{0:T(1024)S(1)} %bitcast.51, f32[24576]{0:T(1024)S(1)} %bitcast.52, f32[]{:T(128)} %constant.80.clone.1), kind=kCustom, calls=%fused_computation.53 | custom fusion | flops 24576 | bytes 1048580 | tf_op jit(solution)/shard_map/scatter-add | solution.py:120
  310.0 1.5 multiply_add_fusion.2
  311.6 1.3 collective-permute-start.2
  312.9 3.0 collective-permute-start.3
  316.0 1.3 collective-permute-start
  317.3 4.5 collective-permute-start.1
  324.5 2.6 multiply_reduce_fusion.1
  327.2 14.4 %all-reduce.12 = (f32[]{:T(128)}, f32[]{:T(128)}) all-reduce(f32[]{:T(128)} %get-tuple-element.5, f32[]{:T(128)} %get-tuple-element.4), channel_id=1, replica_groups=mesh['energy_0'=4,'energy_1'=4,'kpt_0'=4,'kpt_1'=2] {'energy_0'}, use_global_device_ids=true, to_apply=%region_4.5 | all-reduce | flops 2 | bytes 16 | tf_op jit(solution)/shard_map/psum | solution.py:40
  341.5 8.3 %all-reduce.10 = (f32[]{:T(128)}, f32[]{:T(128)}) all-reduce(f32[]{:T(128)} %get-tuple-element.16, f32[]{:T(128)} %get-tuple-element.17), channel_id=1, replica_groups=mesh['energy_0'=4,'energy_1'=4,'kpt_0'=4,'kpt_1'=2] {'energy_1'}, use_global_device_ids=true, to_apply=%region_5.6 | all-reduce | flops 2 | bytes 16 | tf_op jit(solution)/shard_map/psum | solution.py:40
  349.9 9.5 %all-reduce.8 = (f32[]{:T(128)}, f32[]{:T(128)}) all-reduce(f32[]{:T(128)} %get-tuple-element.12, f32[]{:T(128)} %get-tuple-element.13), channel_id=1, replica_groups=mesh['energy_0'=4,'energy_1'=4,'kpt_0'=4,'kpt_1'=2] {'kpt_0'}, use_global_device_ids=true, to_apply=%region_6.7 | all-reduce | flops 2 | bytes 16 | tf_op jit(solution)/shard_map/psum | solution.py:40
  359.4 3.3 all-reduce.14
  364.1 1.5 multiply_subtract_fusion
  365.7 1.3 collective-permute-start.6
  367.0 3.0 collective-permute-start.7
  371.4 4.5 collective-permute-start.5
  378.6 1.7 fusion.6
  380.3 14.2 %all-reduce.11 = (f32[]{:T(128)}, f32[]{:T(128)}) all-reduce(f32[]{:T(128)} %get-tuple-element.3, f32[]{:T(128)} %get-tuple-element.2), channel_id=1, replica_groups=mesh['energy_0'=4,'energy_1'=4,'kpt_0'=4,'kpt_1'=2] {'energy_0'}, use_global_device_ids=true, to_apply=%region_14.15 | all-reduce | flops 2 | bytes 16 | tf_op jit(solution)/shard_map/psum | solution.py:40
  394.5 8.4 %all-reduce.9 = (f32[]{:T(128)}, f32[]{:T(128)}) all-reduce(f32[]{:T(128)} %get-tuple-element.14, f32[]{:T(128)} %get-tuple-element.15), channel_id=1, replica_groups=mesh['energy_0'=4,'energy_1'=4,'kpt_0'=4,'kpt_1'=2] {'energy_1'}, use_global_device_ids=true, to_apply=%region_15.16 | all-reduce | flops 2 | bytes 16 | tf_op jit(solution)/shard_map/psum | solution.py:40
  402.9 9.6 %all-reduce.7 = (f32[]{:T(128)}, f32[]{:T(128)}) all-reduce(f32[]{:T(128)} %get-tuple-element.10, f32[]{:T(128)} %get-tuple-element.11), channel_id=1, replica_groups=mesh['energy_0'=4,'energy_1'=4,'kpt_0'=4,'kpt_1'=2] {'kpt_0'}, use_global_device_ids=true, to_apply=%region_16.17 | all-reduce | flops 2 | bytes 16 | tf_op jit(solution)/shard_map/psum | solution.py:40
  412.5 3.1 all-reduce.13
  422.1 135.5 %gather_fusion = f32[24576]{0:T(1024)S(1)} fusion(f32[262144]{0:T(1024)S(1)} %bitcast.42, s32[24576]{0:T(1024)S(1)} %broadcast_clamp_fusion), kind=kCustom, calls=%fused_computation | custom fusion | bytes 294912 | tf_op jit(solution)/shard_map/jit(_take)/gather | solution.py:147
  557.8 15.6 %all_to_all.15 = f32[8,8,3072]{2,1,0:T(8,128)S(1)} all-to-all(f32[8,8,3072]{2,1,0:T(8,128)S(1)} %broadcast_in_dim.31), channel_id=1, replica_groups=mesh['energy_0'=4,'energy_1'=4,'kpt_0'=4,'kpt_1'=2] {'kpt_0','kpt_1'}, dimensions={0} | all-to-all | bytes 1572864 | tf_op jit(solution)/shard_map/all_to_all | solution.py:61
  573.5 26.1 %all_to_all.16 = f32[16,8,3072]{2,1,0:T(8,128)S(1)} all-to-all(f32[16,8,3072]{2,1,0:T(8,128)S(1)} %broadcast_in_dim.32), channel_id=1, replica_groups=mesh['energy_0'=4,'energy_1'=4,'kpt_0'=4,'kpt_1'=2] {'energy_0','energy_1'}, dimensions={0} | all-to-all | bytes 3145728 | tf_op jit(solution)/shard_map/all_to_all | solution.py:61
  599.7 14.6 %fusion = f32[128,1,4]{2,1,0:T(1,128)S(1)} fusion(bf16[4,128,3072]{2,1,0:T(8,128)(2,1)S(1)} %bitcast.46, f32[128,3072,1]{1,0,2:T(8,128)S(1)} %bitcast.48), kind=kOutput, calls=%fused_computation.4 | convolution fusion | flops 18874368 | bytes 4720640 | tf_op jit(solution)/shard_map/eklo,lo->ekl/dot_general | solution.py:152
  (55 shorter events, 13.4 us)
Async XLA Ops:
  7.2 4.4 copy-start
  7.2 25.8 %reduce-scatter.3.cloned.1.call-start = ((), (), s32[]{:S(2)}) async-start(), calls=%async_computation.4 | async-start | bytes 2359296 | tf_op jit(solution)/shard_map/reduce_scatter | solution.py:55
  16.8 16.2 %copy-start.5 = (u32[128]{0:T(128)S(1)}, u32[128]{0:T(128)}, u32[]{:S(2)}) copy-start(u32[128]{0:T(128)} %constant.119) | copy-start | bytes 1540
  16.8 157.4 %copy-start.4 = (f32[64]{0:T(128)S(1)}, f32[64]{0:T(128)}, u32[]{:S(2)}) copy-start(f32[64]{0:T(128)} %param.11) | copy-start | bytes 772
  18.5 150.1 %all-reduce.17.cloned.1.call-start = ((), (), s32[]{:S(2)}) async-start(), calls=%async_computation.5 | async-start | bytes 1572864
  33.0 277.0 %copy-start.1 = (s32[64,16,256]{2,1,0:T(8,128)S(1)}, s32[64,16,256]{2,1,0:T(8,128)}, u32[]{:S(2)}) copy-start(s32[64,16,256]{2,1,0:T(8,128)} %param.10) | copy-start | bytes 3145732
  170.8 9.1 %all-to-all-start = ((f32[8,1,3072]{2,1,0:T(1,128)}), f32[8,1,3072]{2,1,0:T(1,128)S(1)}, u32[]{:S(2)}, u32[]{:S(2)}) async-start(f32[8,1,3072]{2,1,0:T(1,128)} %broadcast_in_dim.27), calls=%async_computation.1 | async-start | bytes 196608 | tf_op jit(solution)/shard_map/all_to_all | solution.py:61
  311.6 10.2 %collective-permute-start.2 = (f32[64,1,256]{2,1,0:T(1,128)S(1)}, f32[64,1,256]{2,1,0:T(1,128)S(1)}, u32[]{:S(2)}, u32[]{:S(2)}) collective-permute-start(f32[64,1,256]{2,1,0:T(1,128)S(1)} %get-tuple-element.35), channel_id=1, source_target_pairs={{1,0},{2,1},{3,2},{4,3},{5,4},{6,5},{7,6},{9,8},{10,9},{11,10},{12... | collective-permute-start | bytes 196616 | tf_op jit(solution)/shard_map/ppermute | solution.py:27
  312.9 9.0 %collective-permute-start.3 = (f32[64,1,256]{2,1,0:T(1,128)S(1)}, f32[64,1,256]{2,1,0:T(1,128)S(1)}, u32[]{:S(2)}, u32[]{:S(2)}) collective-permute-start(f32[64,1,256]{2,1,0:T(1,128)S(1)} %get-tuple-element.34), channel_id=1, source_target_pairs={{0,1},{1,2},{2,3},{3,4},{4,5},{5,6},{6,7},{8,9},{9,10},{10,11},{11... | collective-permute-start | bytes 196616 | tf_op jit(solution)/shard_map/ppermute | solution.py:26
  316.0 6.0 collective-permute-start
  317.3 6.0 collective-permute-start.1
  365.7 10.2 %collective-permute-start.6 = (f32[64,1,256]{2,1,0:T(1,128)S(1)}, f32[64,1,256]{2,1,0:T(1,128)S(1)}, u32[]{:S(2)}, u32[]{:S(2)}) collective-permute-start(f32[64,1,256]{2,1,0:T(1,128)S(1)} %get-tuple-element.31), channel_id=1, source_target_pairs={{1,0},{2,1},{3,2},{4,3},{5,4},{6,5},{7,6},{9,8},{10,9},{11,10},{12... | collective-permute-start | bytes 196616 | tf_op jit(solution)/shard_map/ppermute | solution.py:27
  367.0 9.0 %collective-permute-start.7 = (f32[64,1,256]{2,1,0:T(1,128)S(1)}, f32[64,1,256]{2,1,0:T(1,128)S(1)}, u32[]{:S(2)}, u32[]{:S(2)}) collective-permute-start(f32[64,1,256]{2,1,0:T(1,128)S(1)} %get-tuple-element.30), channel_id=1, source_target_pairs={{0,1},{1,2},{2,3},{3,4},{4,5},{5,6},{6,7},{8,9},{9,10},{10,11},{11... | collective-permute-start | bytes 196616 | tf_op jit(solution)/shard_map/ppermute | solution.py:26
  370.1 6.0 collective-permute-start.4
  371.4 6.0 collective-permute-start.5
  420.6 1.0 copy-start.2
  573.4 26.3 %copy-start.3 = (bf16[4,1,128,3072]{3,2,1,0:T(8,128)(2,1)S(1)}, bf16[4,1,128,3072]{3,2,1,0:T(8,128)(2,1)}, u32[]{:S(2)}) copy-start(bf16[4,1,128,3072]{3,2,1,0:T(8,128)(2,1)} %param.6) | copy-start | bytes 9437188
Sparse Core Ops, SparseCore 0:
  18.6 14.3 reduce-scatter.2
  37.6 130.9 all-reduce.16
where the time goes:
time: 623 us; the launch traced here: 622 us
  waiting for transfers between devices  157 us (25%)
  local copies, waits for them, and re-layouts  147 us (24%)
  other arithmetic  142 us (23%)
  blocking collectives  113 us (18%)
  starting transfers between devices  23.8 us (4%)
  between operations  20.5 us (3%)
  matrix products  19.8 us (3%)
    gather x2, local copies, waits for them, and re-layouts, per_device(): jnp.take(potential.reshape(-1), flat_cell)  136 us
    unnamed x3, waiting for transfers between devices  134 us
    scatter-add x1, other arithmetic, per_device(): jax.ops.segment_sum(jnp.where(inside, slab_occupancy, 0.0).reshape(-1), f...  129 us
    psum x8, blocking collectives, one_axis_at_a_time(): x = lax.psum(x, axis)  70.9 us
    all_to_all x2, blocking collectives, from_everyone(): return lax.all_to_all(copies, axis, split_axis=0, concat_axis=0, tiled=True)  41.7 us
    ppermute x4, starting transfers between devices, extended(): lax.ppermute(last, axis, up)  15.2 us
    dot_general x1, matrix products, per_device(): jnp.einsum('eklo,lo->ekl', block, gather_directly(orbital_potential, ENER...  14.6 us
    reduce_scatter x1, waiting for transfers between devices, scatter_pairs(): tiles = lax.psum_scatter(tiles, core, scatter_dimension=0, tiled=True)  14.4 us
  transfers between devices with their start and end apart: 11, of which 5 were waited for; matrix products, arithmetic and copies ran while one was open for 0% of the time, Pallas kernels for 0%

commit v1 on v0

v1 whole, which is shorter than its diff:
```python
import jax
import jax.numpy as jnp
from jax import lax
from jax.experimental import pallas as pl
from jax.experimental.pallas import tpu as pltpu
from jax.sharding import Mesh
from jax.sharding import PartitionSpec as P

ENERGY = ("energy_0", "energy_1")
KPT = ("kpt_0", "kpt_1")
CHIPS = ("energy_0", "energy_1", "kpt_0")
CORE = "kpt_1"
EVERY = ("energy_0", "energy_1", "kpt_0", "kpt_1")

NE = 16
NK = 8
NZC = 4
SUB = 8
LAYERS = 128
LD = 8
ORB = 3072
CY = 16
NY = 128
NZ = 256
PLANES = 64
EL = 4
W = 24
COL = ORB // NK
TL = COL // 128
PENALTY = 4.0
VMEM = 60 * 1024 * 1024


def swap_cores(x):
    return lax.ppermute(x, CORE, [(0, 1), (1, 0)])


def exchange(x, axis):
    return lax.all_to_all(x, axis, split_axis=0, concat_axis=0, tiled=True)


def params():
    return pltpu.CompilerParams(vmem_limit_bytes=VMEM)


def occupancy_body(core, weights, density, own, other):
    for half, out in ((0, own), (1, other)):
        which = core[0] if half == 0 else 1 - core[0]
        start = pl.multiple_of(which * COL, 128)
        zero = jnp.zeros((3, 128), jnp.float32)
        for e in range(0, NE, 2):
            total = None
            for i in range(EL):
                part = density[i, 8 * e : 8 * e + 16, pl.ds(start, COL)].astype(jnp.float32) * weights[i]
                total = part if total is None else total + part
            for h in range(2):
                at = e + h
                for t in range(TL):
                    tile = total[8 * h : 8 * h + 8, 128 * t : 128 * (t + 1)]
                    out[at, 0, 8 * t : 8 * t + 8, :] = tile
                    if at + 1 < NE:
                        out[at + 1, 0, 24 + t : 25 + t, :] = tile[7:8]
                    if at > 0:
                        out[at - 1, 0, 27 + t : 28 + t, :] = tile[0:1]
        out[0, 0, 24:27, :] = zero
        out[NE - 1, 0, 27:30, :] = zero
        for e in range(NE):
            out[e, 0, 30:32, :] = zero[:2]


def occupancy_parts(core, weights, density):
    shape = jax.ShapeDtypeStruct((NE, NZC, 32, 128), jnp.float32)
    block = pl.BlockSpec((NE, 1, 32, 128), lambda z, *_: (0, z, 0, 0))
    return pl.pallas_call(
        occupancy_body,
        grid_spec=pltpu.PrefetchScalarGridSpec(
            num_scalar_prefetch=2,
            grid=(NZC,),
            in_specs=[pl.BlockSpec((EL, LAYERS, 2 * COL), lambda z, *_: (0, 0, z))],
            out_specs=[block, block],
        ),
        out_shape=[shape, shape],
        compiler_params=params(),
        name="occupancy_parts",
    )(core, weights, density)


def collect_body(parts, out):
    total = parts[0]
    for i in range(1, NE * NZC):
        total = total + parts[i]
    for k in range(NK):
        out[k] = total


def collect(parts):
    return pl.pallas_call(
        collect_body,
        out_shape=jax.ShapeDtypeStruct((NK, 32, 128), jnp.float32),
        compiler_params=params(),
        name="collect",
    )(parts)


def split_parts(x):
    high = x.astype(jnp.bfloat16)
    low = (x - high.astype(jnp.float32)).astype(jnp.bfloat16)
    return high, low


def charge_of(cells, values, first_plane, planes, y0):
    count = cells.shape[1]
    plane = (cells >> 15) - first_plane
    dy = ((cells >> 8) & (NY - 1)) - y0
    near = (dy >= -2) & (dy < CY + 2) & (plane >= 0) & (plane < planes)
    row = jnp.where(near, plane * W + jnp.where(dy >= 0, dy, dy + W), -1)
    z = cells & (NZ - 1)
    rows = planes * W
    hit = lax.broadcasted_iota(jnp.int32, (rows, count), 0) == row
    high = values.astype(jnp.bfloat16).astype(jnp.float32)
    low = values - high
    left = jnp.concatenate(
        [jnp.where(hit, high, 0.0).astype(jnp.bfloat16), jnp.where(hit, low, 0.0).astype(jnp.bfloat16)], axis=0
    )
    right = jnp.where(lax.broadcasted_iota(jnp.int32, (NZ, count), 0) == z, 1.0, 0.0).astype(jnp.bfloat16)
    both = lax.dot_general(left, right, (((1,), (1,)), ((), ())), preferred_element_type=jnp.float32)
    return both[:rows] + both[rows:]


def beside(field, plane):
    here = field[plane]
    lane = lax.broadcasted_iota(jnp.int32, (W, NZ), 1)
    total = field[plane + 1] + field[plane - 1]
    total = total + pltpu.roll(here, 1, 0) + pltpu.roll(here, W - 1, 0)
    total = total + jnp.where(lane == 0, 0.0, pltpu.roll(here, 1, 1))
    return here, total + jnp.where(lane == NZ - 1, 0.0, pltpu.roll(here, NZ - 1, 1))


def field_body(where, volts, occ, below, mine, above, fixed, gate, xlow, xhigh, ylow, yhigh,
               sums, r_out, w_out, r_ext, w_ext, g_ext):
    e = where[0]
    k = where[1]
    y0 = k * CY
    row = lax.broadcasted_iota(jnp.int32, (W, NZ), 0)
    y = jnp.where(row < CY + 4, row, row - W) + y0
    valid = jnp.where((y >= 0) & (y < NY), 1.0, 0.0)
    r_ext[:, 16:24, :] = jnp.zeros((PLANES + 4, 8, NZ), jnp.float32)
    g_ext[:, 16:24, :] = jnp.zeros((PLANES + 4, 8, NZ), jnp.float32)

    def load_plane(p, carry):
        g = gate[p].astype(jnp.float32)
        g_ext[p + 2, 0:CY, :] = g
        r_ext[p + 2, 0:CY, :] = fixed[p] + PENALTY * g * volts[p]
        return carry

    lax.fori_loop(0, PLANES, load_plane, 0, unroll=4)
    for i in range(2):
        r_ext[i, 0:CY, :] = xlow[0, i]
        g_ext[i, 0:CY, :] = xlow[1, i]
        r_ext[PLANES + 2 + i, 0:CY, :] = xhigh[0, i]
        g_ext[PLANES + 2 + i, 0:CY, :] = xhigh[1, i]

    def load_halo(p, carry):
        r_ext[p, CY : CY + 2, :] = yhigh[0, p]
        g_ext[p, CY : CY + 2, :] = yhigh[1, p]
        r_ext[p, W - 2 : W, :] = ylow[0, p]
        g_ext[p, W - 2 : W, :] = ylow[1, p]
        return carry

    lax.fori_loop(0, PLANES + 4, load_halo, 0, unroll=4)

    def values_of(index):
        return jnp.concatenate(
            [occ[c, pl.ds(index(t), 1), :] for c in range(NK) for t in range(TL)], axis=1
        )

    def one_layer(j, carry):
        charge = charge_of(mine[pl.ds(j, 1), :], values_of(lambda t: 8 * t + j), 0, SUB, y0)
        at = pl.ds(2 + SUB * j, SUB)
        r_ext[at] = r_ext[at] - charge.reshape(SUB, W, NZ)
        return carry

    lax.fori_loop(0, LD, one_layer, 0)
    charge = charge_of(below[7:8, :], values_of(lambda t: 24 + t), SUB - 2, 2, y0)
    r_ext[0:2] = r_ext[0:2] - charge.reshape(2, W, NZ)
    charge = charge_of(above[0:1, :], values_of(lambda t: 27 + t), 0, 2, y0)
    r_ext[PLANES + 2 : PLANES + 4] = r_ext[PLANES + 2 : PLANES + 4] - charge.reshape(2, W, NZ)

    def image_plane(p, carry):
        here, around = beside(r_ext, p + 1)
        x = e * PLANES + p - 1
        inside = jnp.where((x >= 0) & (x < NE * PLANES), 1.0, 0.0)
        w_ext[p] = ((6.0 + PENALTY * g_ext[p + 1]) * here - around) * (valid * inside)
        return carry

    lax.fori_loop(0, PLANES + 2, image_plane, 0, unroll=2)

    def sum_plane(p, carry):
        rr, rw, ww, waw = carry
        r = r_ext[p + 2, 0:CY, :]
        here, around = beside(w_ext, p + 1)
        image = (6.0 + PENALTY * g_ext[p + 2]) * here - around
        w = here[0:CY]
        r_out[p] = r
        w_out[p] = w
        return rr + r * r, rw + r * w, ww + w * w, waw + w * image[0:CY]

    zero = jnp.zeros((CY, NZ), jnp.float32)
    totals = lax.fori_loop(0, PLANES, sum_plane, (zero,) * 4, unroll=2)
    lane = lax.broadcasted_iota(jnp.int32, (1, 128), 1)
    line = jnp.zeros((1, 128), jnp.float32)
    for i, total in enumerate(totals):
        line = line + jnp.where(lane == i, jnp.sum(total), 0.0)
    for d in range(NE * NK):
        sums[d] = line


def fields(where, volts, occ, cells, fixed, gate, xlow, xhigh, ylow, yhigh):
    whole = lambda x: pl.BlockSpec(x.shape, lambda i, *_: (0,) * x.ndim)
    near = lambda shift: pl.BlockSpec(
        (LD, ORB), lambda i, where, *_: (jnp.clip(where[0] + shift, 0, NE - 1), 0)
    )
    shapes = [
        jax.ShapeDtypeStruct((NE * NK, 1, 128), jnp.float32),
        jax.ShapeDtypeStruct((PLANES, CY, NZ), jnp.float32),
        jax.ShapeDtypeStruct((PLANES, CY, NZ), jnp.float32),
    ]
    return pl.pallas_call(
        field_body,
        grid_spec=pltpu.PrefetchScalarGridSpec(
            num_scalar_prefetch=2,
            grid=(1,),
            in_specs=[whole(occ), near(-1), near(0), near(1)]
            + [whole(x) for x in (fixed, gate, xlow, xhigh, ylow, yhigh)],
            out_specs=[whole(x) for x in shapes],
            scratch_shapes=[
                pltpu.VMEM((PLANES + 4, W, NZ), jnp.float32),
                pltpu.VMEM((PLANES + 2, W, NZ), jnp.float32),
                pltpu.VMEM((PLANES + 4, W, NZ), jnp.float32),
            ],
        ),
        out_shape=shapes,
        compiler_params=params(),
        name="fields",
    )(where, volts, occ, cells, cells, cells, fixed, gate, xlow, xhigh, ylow, yhigh)


def pick_body(where, mine, r, w, out):
    y0 = where[1] * CY
    wide = 2 * COL

    def one_layer(j, carry):
        at = pl.ds(SUB * j, SUB)
        both = jnp.concatenate([r[at].reshape(SUB * CY, NZ), w[at].reshape(SUB * CY, NZ)], axis=0)
        high, low = split_parts(both)
        for n in range(ORB // wide):
            cells = mine[pl.ds(j, 1), n * wide : (n + 1) * wide]
            dy = ((cells >> 8) & (NY - 1)) - y0
            row = jnp.where((dy >= 0) & (dy < CY), (cells >> 15) * CY + dy, -1)
            z = cells & (NZ - 1)
            right = jnp.where(lax.broadcasted_iota(jnp.int32, (NZ, wide), 0) == z, 1.0, 0.0).astype(jnp.bfloat16)
            lines = jnp.dot(high, right, preferred_element_type=jnp.float32)
            lines = lines + jnp.dot(low, right, preferred_element_type=jnp.float32)
            hit = lax.broadcasted_iota(jnp.int32, (SUB * CY, wide), 0) == row
            for f in range(2):
                part = lines[f * SUB * CY : (f + 1) * SUB * CY]
                value = jnp.sum(jnp.where(hit, part, 0.0), axis=0, keepdims=True)
                for h in range(2):
                    out[2 * n + h, pl.ds(f * LD + j, 1), :] = value[:, h * COL : (h + 1) * COL]
        return carry

    lax.fori_loop(0, LD, one_layer, 0)


def pick(where, cells, r, w):
    whole = lambda x: pl.BlockSpec(x.shape, lambda i, *_: (0,) * x.ndim)
    shape = jax.ShapeDtypeStruct((NK, 2 * LD, COL), jnp.float32)
    return pl.pallas_call(
        pick_body,
        grid_spec=pltpu.PrefetchScalarGridSpec(
            num_scalar_prefetch=1,
            grid=(1,),
            in_specs=[pl.BlockSpec((LD, ORB), lambda i, where: (where[0], 0)), whole(r), whole(w)],
            out_specs=whole(shape),
        ),
        out_shape=shape,
        compiler_params=params(),
        name="pick",
    )(where, cells, r, w)


def mix_body(sums, picked, scalars, out):
    line = jnp.sum(sums[...].reshape(NE * NK, 128), axis=0, keepdims=True)
    lane = lax.broadcasted_iota(jnp.int32, (1, 128), 1)
    rr, rw, ww, waw = [
        jnp.broadcast_to(jnp.sum(jnp.where(lane == i, line, 0.0), axis=1, keepdims=True), (1, 128)) for i in range(4)
    ]
    alpha = rr / rw
    norm = alpha * alpha * ww - rr
    ratio = norm / rr
    ahead = 1.0 + ratio
    curve = ahead * ahead * rw - 2.0 * ahead * alpha * ww + alpha * alpha * waw
    small = (norm <= 1e-9 * rr) | (curve <= 0.0)
    step = jnp.where(small, alpha, norm / curve)
    ahead = jnp.where(small, 1.0, ahead)
    c_r = alpha + step * ahead
    c_w = -alpha * step
    scalars[...] = jnp.where(lane == 0, c_r, c_w)
    total = picked[0]
    for i in range(1, NK):
        total = total + picked[i]
    c_r = jnp.concatenate([c_r] * TL, axis=1)
    c_w = jnp.concatenate([c_w] * TL, axis=1)
    value = c_r * total[:LD] + c_w * total[LD:]
    for d in range(NE * NZC):
        out[d] = value


def mix(sums, picked):
    return pl.pallas_call(
        mix_body,
        out_shape=[
            jax.ShapeDtypeStruct((1, 128), jnp.float32),
            jax.ShapeDtypeStruct((NE * NZC, LD, COL), jnp.float32),
        ],
        compiler_params=params(),
        name="mix",
    )(sums, picked)


def band_body(core, density, same, cross, out, acc):
    z = pl.program_id(0)

    @pl.when(z == 0)
    def _():
        acc[...] = jnp.zeros_like(acc)

    for half, values in ((0, same), (1, cross)):
        which = core[0] if half == 0 else 1 - core[0]
        start = pl.multiple_of(which * COL, 128)
        for m in range(0, NE, 2):
            v = values[m : m + 2, 0].reshape(16, COL)
            for i in range(EL):
                part = density[i, 8 * m : 8 * m + 16, pl.ds(start, COL)].astype(jnp.float32) * v
                total = part[:, :128]
                for t in range(1, TL):
                    total = total + part[:, 128 * t : 128 * (t + 1)]
                acc[i, 8 * m : 8 * m + 16] = acc[i, 8 * m : 8 * m + 16] + total

    @pl.when(z == NZC - 1)
    def _():
        for i in range(EL):
            out[i : i + 1, :] = jnp.sum(acc[i].T, axis=0, keepdims=True) * ORB**-0.5


def band(core, density, same, cross):
    values = pl.BlockSpec((NE, 1, LD, COL), lambda z, *_: (0, z, 0, 0))
    return pl.pallas_call(
        band_body,
        grid_spec=pltpu.PrefetchScalarGridSpec(
            num_scalar_prefetch=1,
            grid=(NZC,),
            in_specs=[pl.BlockSpec((EL, LAYERS, 2 * COL), lambda z, *_: (0, 0, z)), values, values],
            out_specs=pl.BlockSpec((EL, LAYERS), lambda z, *_: (0, 0)),
            scratch_shapes=[pltpu.VMEM((EL, LAYERS, 128), jnp.float32)],
        ),
        out_shape=jax.ShapeDtypeStruct((EL, LAYERS), jnp.float32),
        compiler_params=params(),
        name="band",
    )(core, density, same, cross)


def edges(x, axis, dim):
    peers = lax.axis_size(axis)
    up = [(i, i + 1) for i in range(peers - 1)]
    first = lax.slice_in_dim(x, 0, 2, axis=dim)
    last = lax.slice_in_dim(x, x.shape[dim] - 2, x.shape[dim], axis=dim)
    return lax.ppermute(last, axis, up), lax.ppermute(first, axis, [(b, a) for a, b in up])


def per_device(density, quad_weights, orbital_cells, fixed_charge, gate_mask, gate_voltage):
    e = lax.axis_index(ENERGY).astype(jnp.int32)
    k = lax.axis_index(KPT).astype(jnp.int32)
    core = lax.axis_index(CORE).astype(jnp.int32)[None]
    where = jnp.stack([e, k])
    density = density.reshape(EL, LAYERS, ORB)

    own, other = occupancy_parts(core, quad_weights.reshape(EL), density)
    chips = NE * NZC
    pair = own.reshape(chips, 32, 128) + swap_cores(other.reshape(chips, 32, 128))
    parts = exchange(pair, CHIPS)

    gated = gate_mask.astype(jnp.float32)
    known = jnp.stack([fixed_charge + PENALTY * gated * gate_voltage[:, None, None], gated])
    xlow, xhigh = edges(known, ENERGY, 1)
    first = jnp.concatenate([xlow[:, :, :2], known[:, :, :2], xhigh[:, :, :2]], axis=1)
    last = jnp.concatenate([xlow[:, :, -2:], known[:, :, -2:], xhigh[:, :, -2:]], axis=1)
    up = [(i, i + 1) for i in range(NK - 1)]
    ylow = lax.ppermute(last, KPT, up)
    yhigh = lax.ppermute(first, KPT, [(b, a) for a, b in up])

    occ = exchange(collect(parts), KPT)
    sums, r, w = fields(
        where, gate_voltage, occ, orbital_cells, fixed_charge, gate_mask, xlow, xhigh, ylow, yhigh
    )
    all_sums = exchange(sums, EVERY)
    picked = exchange(pick(where, orbital_cells, r, w), KPT)
    scalars, values = mix(all_sums, picked)
    same = exchange(values, CHIPS)
    potential = scalars[0, 0] * r + scalars[0, 1] * w
    cross = swap_cores(same)
    shape = (NE, NZC, LD, COL)
    shift = band(core, density, same.reshape(shape), cross.reshape(shape))
    return potential, shift.reshape(EL, 1, LAYERS)


def solution(mesh):
    split = Mesh(mesh.devices.reshape(4, 4, 4, 2), ("energy_0", "energy_1", "kpt_0", "kpt_1"))
    in_specs = (
        P(ENERGY, KPT, None, None),
        P(ENERGY, KPT),
        P(),
        P(ENERGY, KPT, None),
        P(ENERGY, KPT, None),
        P(ENERGY),
    )
    out_specs = (P(ENERGY, KPT, None), P(ENERGY, KPT, None))
    return jax.shard_map(per_device, mesh=split, in_specs=in_specs, out_specs=out_specs, check_vma=False)
```

time: 623 us -> 144 us (0.23)
  local copies, waits for them, and re-layouts: 147 us -> 3.97 us
  other arithmetic: 142 us -> 4.76 us
  waiting for transfers between devices: 157 us -> 20 us
  blocking collectives: 113 us -> 35.2 us
  Pallas kernels: 0 us -> 45.6 us
  matrix products: 19.8 us -> 0 us
  between operations: 20.5 us -> 0.82 us
  starting transfers between devices: 23.8 us -> 31.5 us
    gather x2 -> x0, local copies, waits for them, and re-layouts: 136 us -> none  [per_device(): jnp.take(potential.reshape(-1), flat_cell)]
    unnamed x3 -> x0, waiting for transfers between devices: 134 us -> none
    scatter-add x1 -> x0, other arithmetic: 129 us -> none  [per_device(): jax.ops.segment_sum(jnp.where(inside, slab_occupancy, 0.0).reshape(-1), f...]
    psum x8 -> x0, blocking collectives: 70.9 us -> none  [one_axis_at_a_time(): x = lax.psum(x, axis)]
    pallas_call x0 -> x6, Pallas kernels: none -> 45.6 us  [the longest x1 19.3 us: fields(): pl.pallas_call(field_body, grid_spec=pltpu.PrefetchScalarGridSpec(num_sca...]
    all_to_all x1 -> x3, starting transfers between devices: 3.36 us -> 24.1 us  [exchange(): return lax.all_to_all(x, axis, split_axis=0, concat_axis=0, tiled=True)]
    dot_general x2 -> x0, matrix products: 19.8 us -> none  [the longest x1 14.6 us: per_device(): jnp.einsum('eklo,lo->ekl', block, gather_directly(orbital_potential, ENER...]
    reduce_scatter x1 -> x0, waiting for transfers between devices: 14.4 us -> none  [scatter_pairs(): tiles = lax.psum_scatter(tiles, core, scatter_dimension=0, tiled=True)]
  transfers between devices with their start and end apart: 11 -> 9, of which waited for: 5 -> 5; matrix products, arithmetic and copies ran while one was open for 0% -> 4% of each run, Pallas kernels for 0% -> 11%
where the time goes in v1:
time: 144 us; the launch traced here: 142 us
  Pallas kernels  45.6 us (32%)
  blocking collectives  35.2 us (24%)
  starting transfers between devices  31.5 us (22%)
  waiting for transfers between devices  20 us (14%)
  other arithmetic  4.76 us (3%)
  local copies, waits for them, and re-layouts  3.97 us (3%)
    all_to_all x2, blocking collectives, exchange(): return lax.all_to_all(x, axis, split_axis=0, concat_axis=0, tiled=True)  35.2 us
    all_to_all x3, starting transfers between devices, exchange(): return lax.all_to_all(x, axis, split_axis=0, concat_axis=0, tiled=True)  24.1 us
    pallas_call x1, Pallas kernels, fields(): pl.pallas_call(field_body, grid_spec=pltpu.PrefetchScalarGridSpec(num_sca...  19.3 us
    pallas_call x1, Pallas kernels, pick(): pl.pallas_call(pick_body, grid_spec=pltpu.PrefetchScalarGridSpec(num_scal...  13.2 us
    all_to_all x3, waiting for transfers between devices, exchange(): return lax.all_to_all(x, axis, split_axis=0, concat_axis=0, tiled=True)  7.82 us
    ppermute x1, waiting for transfers between devices, edges(): lax.ppermute(last, axis, up)  7.7 us
    pallas_call x1, Pallas kernels, occupancy_parts(): pl.pallas_call(occupancy_body, grid_spec=pltpu.PrefetchScalarGridSpec(num...  5.07 us
    pallas_call x1, Pallas kernels, band(): pl.pallas_call(band_body, grid_spec=pltpu.PrefetchScalarGridSpec(num_scal...  4.02 us
  transfers between devices with their start and end apart: 9, of which 5 were waited for; matrix products, arithmetic and copies ran while one was open for 4% of the time, Pallas kernels for 11%

profile of v1, /device:TPU:0, one launch (start us, length us, event | category | flops | bytes accessed | tf_op | source)
XLA Modules:
  0.0 142.0 jit_solution(8721713712203072385)
XLA Ops:
  0.6 0.0 copy-start.14
  0.6 0.0 copy-start
  0.7 5.1 %occupancy_parts.1 = (f32[16,4,32,128]{3,2,1,0:T(8,128)}, f32[16,4,32,128]{3,2,1,0:T(8,128)}) custom-call(s32[1]{0:T(128)} %bitcast.2.core, f32[4]{0:T(128)} %bitcast.24, bf16[4,128,3072]{2,1,0:T(8,128)(2,1)} %bitcast.19), custom_call_target="tpu_custom_call" | custom-call | tf_op jit(solution)/shard_map/occupancy_parts/pallas_call | solution.py:74
  5.8 0.2 add_bitcast_fusion
  6.0 2.7 %collective-permute-done = f32[64,32,128]{2,1,0:T(8,128)S(1)} collective-permute-done((f32[64,32,128]{2,1,0:T(8,128)}, f32[64,32,128]{2,1,0:T(8,128)S(1)}, u32[]{:S(2)}, u32[]{:S(2)}) %collective-permute-start) | collective-permute-done | bytes 1048608 | tf_op jit(solution)/shard_map/ppermute | solution.py:35
  8.6 1.2 bitcast_add_fusion
  9.8 11.5 %all-to-all-start = ((f32[64,32,128]{2,1,0:T(8,128)}), f32[64,32,128]{2,1,0:T(8,128)S(1)}, u32[]{:S(2)}, u32[]{:S(2)}) async-start(f32[64,32,128]{2,1,0:T(8,128)} %bitcast_add_fusion), calls=%async_computation | async-start | bytes 2097152 | tf_op jit(solution)/shard_map/all_to_all | solution.py:39
  21.3 0.1 convert_bitcast_fusion
  21.5 3.5 %collective-permute-start.1 = (f32[2,2,16,256]{3,2,1,0:T(8,128)S(1)}, f32[2,2,16,256]{3,2,1,0:T(8,128)S(1)}, u32[]{:S(2)}, u32[]{:S(2)}) collective-permute-start(f32[2,2,16,256]{3,2,1,0:T(8,128)S(1)} %get-tuple-element.21), channel_id=1, source_target_pairs={{0,8},{8,16},{16,24},{24,32},{32,40},{40,48},{48,56},{56,64},{64,7... | collective-permute-start | bytes 196616 | tf_op jit(solution)/shard_map/ppermute | solution.py:378
  24.9 1.3 collective-permute-start.2
  26.2 7.7 %collective-permute-done.1.xlow = f32[2,2,16,256]{3,2,1,0:T(8,128)S(1)} collective-permute-done((f32[2,2,16,256]{3,2,1,0:T(8,128)S(1)}, f32[2,2,16,256]{3,2,1,0:T(8,128)S(1)}, u32[]{:S(2)}, u32[]{:S(2)}) %collective-permute-start.1) | collective-permute-done | bytes 65568 | tf_op jit(solution)/shard_map/ppermute | solution.py:378
  34.0 1.9 %collective-permute-done.2.xhigh = f32[2,2,16,256]{3,2,1,0:T(8,128)S(1)} collective-permute-done((f32[2,2,16,256]{3,2,1,0:T(8,128)S(1)}, f32[2,2,16,256]{3,2,1,0:T(8,128)S(1)}, u32[]{:S(2)}, u32[]{:S(2)}) %collective-permute-start.2) | collective-permute-done | bytes 65568 | tf_op jit(solution)/shard_map/ppermute | solution.py:378
  35.8 0.2 fusion.1
  36.0 1.3 collective-permute-start.3
  37.4 1.3 collective-permute-start.4
  38.7 2.4 %all-to-all-done.parts = f32[64,32,128]{2,1,0:T(8,128)S(1)} async-done(((f32[64,32,128]{2,1,0:T(8,128)}), f32[64,32,128]{2,1,0:T(8,128)S(1)}, u32[]{:S(2)}, u32[]{:S(2)}) %all-to-all-start) | async-done | bytes 1048608 | tf_op jit(solution)/shard_map/all_to_all | solution.py:39
  41.1 1.0 copy-done.1
  42.0 2.0 %collect.1 = f32[8,32,128]{2,1,0:T(8,128)} custom-call(f32[64,32,128]{2,1,0:T(8,128)} %copy-done.1), custom_call_target="tpu_custom_call" | custom-call | tf_op jit(solution)/shard_map/collect/pallas_call | solution.py:97
  44.0 4.8 %all-to-all-start.1 = ((f32[8,32,128]{2,1,0:T(8,128)}), f32[8,32,128]{2,1,0:T(8,128)S(1)}, u32[]{:S(2)}, u32[]{:S(2)}) async-start(f32[8,32,128]{2,1,0:T(8,128)} %collect.1), calls=%async_computation.1 | async-start | bytes 262144 | tf_op jit(solution)/shard_map/all_to_all | solution.py:39
  48.8 0.7 pad_add_fusion.where
  49.5 5.4 %all-to-all-done.1.occ = f32[8,32,128]{2,1,0:T(8,128)S(1)} async-done(((f32[8,32,128]{2,1,0:T(8,128)}), f32[8,32,128]{2,1,0:T(8,128)S(1)}, u32[]{:S(2)}, u32[]{:S(2)}) %all-to-all-start.1) | async-done | bytes 131104 | tf_op jit(solution)/shard_map/all_to_all | solution.py:39
  54.9 0.6 copy-done.8
  55.6 19.3 %fields.1 = (f32[128,1,128]{2,1,0:T(1,128)}, f32[64,16,256]{2,1,0:T(8,128)}, f32[64,16,256]{2,1,0:T(8,128)}) custom-call(s32[2]{0:T(128)} %pad_add_fusion.where, f32[64]{0:T(128)} %volts.1, f32[8,32,128]{2,1,0:T(8,128)} %copy-done.8, s32[128,3072]{1,0:T(8,128)} %mine.3, s32[128,3072]{1,0:T(8,128)} %mine.3, s32[128,3072]{1,0:T(8,128)} %mine.3, ...), custom_call_target="tpu_custom_call" | custom-call | tf_op jit(solution)/shard_map/fields/pallas_call | solution.py:228
  74.9 7.8 %all-to-all-start.2 = ((f32[128,1,128]{2,1,0:T(1,128)}), f32[128,1,128]{2,1,0:T(1,128)S(1)}, u32[]{:S(2)}, u32[]{:S(2)}) async-start(f32[128,1,128]{2,1,0:T(1,128)} %get-tuple-element.11), calls=%async_computation.2 | async-start | bytes 131072 | tf_op jit(solution)/shard_map/all_to_all | solution.py:39
  82.7 13.2 %pick.1 = f32[8,16,384]{2,1,0:T(8,128)} custom-call(s32[2]{0:T(128)} %pad_add_fusion.where, s32[128,3072]{1,0:T(8,128)} %mine.3, f32[64,16,256]{2,1,0:T(8,128)} %get-tuple-element.12.r, f32[64,16,256]{2,1,0:T(8,128)} %get-tuple-element.13.w), custom_call_target="tpu_custom_call" | custom-call | tf_op jit(solution)/shard_map/pick/pallas_call | solution.py:278
  95.9 11.0 %all_to_all.25.picked = f32[8,16,384]{2,1,0:T(8,128)} all-to-all(f32[8,16,384]{2,1,0:T(8,128)} %pick.1), channel_id=1, replica_groups=mesh['energy_0'=4,'energy_1'=4,'kpt_0'=4,'kpt_1'=2] {'kpt_0','kpt_1'}, dimensions={0} | all-to-all | bytes 393216 | tf_op jit(solution)/shard_map/all_to_all | solution.py:39
  107.0 2.1 %mix.1 = (f32[1,128]{1,0:T(1,128)}, f32[64,8,384]{2,1,0:T(8,128)}) custom-call(f32[128,1,128]{2,1,0:T(1,128)} %copy-done.11, f32[8,16,384]{2,1,0:T(8,128)} %all_to_all.25.picked), custom_call_target="tpu_custom_call" | custom-call | tf_op jit(solution)/shard_map/mix/pallas_call | solution.py:320
  109.1 24.1 %all_to_all.26 = f32[64,8,384]{2,1,0:T(8,128)S(1)} all-to-all(f32[64,8,384]{2,1,0:T(8,128)} %get-tuple-element.15), channel_id=1, replica_groups=mesh['energy_0'=4,'energy_1'=4,'kpt_0'=4,'kpt_1'=2] {'energy_0','energy_..., dimensions={0} | all-to-all | bytes 1572864 | tf_op jit(solution)/shard_map/all_to_all | solution.py:39
  133.2 1.4 fusion.6
  134.6 2.4 %multiply_add_fusion = f32[64,16,256]{2,1,0:T(8,128)} fusion(f32[64,16,256]{2,1,0:T(8,128)S(1)} %copy-done.4, f32[64,16,256]{2,1,0:T(8,128)S(1)} %copy-done.3, f32[]{:T(128)} %bitcast.10, f32[]{:T(128)} %bitcast.9), kind=kLoop, calls=%fused_computation.1 | loop fusion | flops 786432 | bytes 3145736 | tf_op jit(solution)/shard_map/add | solution.py:410
  137.0 0.9 copy-done.7
  137.9 4.0 %band.1 = f32[4,128]{1,0:T(4,128)} custom-call(s32[1]{0:T(128)} %bitcast.2.core, bf16[4,128,3072]{2,1,0:T(8,128)(2,1)} %bitcast.20, f32[16,4,8,384]{3,2,1,0:T(8,128)} %bitcast.21, f32[16,4,8,384]{3,2,1,0:T(8,128)} %bitcast.22), custom_call_target="tpu_custom_call" | custom-call | tf_op jit(solution)/shard_map/band/pallas_call | solution.py:358
  (35 shorter events, 0.1 us)
Async XLA Ops:
  0.6 5.1 %copy-start.14 = (f32[64]{0:T(128)S(1)}, f32[64]{0:T(128)}, u32[]{:S(2)}) copy-start(f32[64]{0:T(128)} %volts.1) | copy-start | bytes 772
  0.6 5.1 %copy-start = (s32[64,16,256]{2,1,0:T(8,128)S(1)}, s32[64,16,256]{2,1,0:T(8,128)}, u32[]{:S(2)}) copy-start(s32[64,16,256]{2,1,0:T(8,128)} %gate.1) | copy-start | bytes 3145732
  0.7 5.1 %copy-start.2 = (f32[64,16,256]{2,1,0:T(8,128)S(1)}, f32[64,16,256]{2,1,0:T(8,128)}, u32[]{:S(2)}) copy-start(f32[64,16,256]{2,1,0:T(8,128)} %fixed.1) | copy-start | bytes 3145732
  5.7 2.9 %copy-start.6 = (f32[16,4,32,128]{3,2,1,0:T(8,128)S(1)}, f32[16,4,32,128]{3,2,1,0:T(8,128)}, u32[]{:S(2)}) copy-start(f32[16,4,32,128]{3,2,1,0:T(8,128)} %get-tuple-element.9) | copy-start | bytes 3145732
  5.7 2.9 %collective-permute-start = (f32[64,32,128]{2,1,0:T(8,128)}, f32[64,32,128]{2,1,0:T(8,128)S(1)}, u32[]{:S(2)}, u32[]{:S(2)}) collective-permute-start(f32[64,32,128]{2,1,0:T(8,128)} %bitcast.25), channel_id=1, source_target_pairs={{0,1},{1,0},{2,3},{3,2},{4,5},{5,4},{6,7},{7,6},{8,9},{9,8},{10,11... | collective-permute-start | bytes 3145736 | tf_op jit(solution)/shard_map/ppermute | solution.py:35
  9.8 31.3 %all-to-all-start = ((f32[64,32,128]{2,1,0:T(8,128)}), f32[64,32,128]{2,1,0:T(8,128)S(1)}, u32[]{:S(2)}, u32[]{:S(2)}) async-start(f32[64,32,128]{2,1,0:T(8,128)} %bitcast_add_fusion), calls=%async_computation | async-start | bytes 2097152 | tf_op jit(solution)/shard_map/all_to_all | solution.py:39
  21.5 12.5 %collective-permute-start.1 = (f32[2,2,16,256]{3,2,1,0:T(8,128)S(1)}, f32[2,2,16,256]{3,2,1,0:T(8,128)S(1)}, u32[]{:S(2)}, u32[]{:S(2)}) collective-permute-start(f32[2,2,16,256]{3,2,1,0:T(8,128)S(1)} %get-tuple-element.21), channel_id=1, source_target_pairs={{0,8},{8,16},{16,24},{24,32},{32,40},{40,48},{48,56},{56,64},{64,7... | collective-permute-start | bytes 196616 | tf_op jit(solution)/shard_map/ppermute | solution.py:378
  24.9 10.9 %collective-permute-start.2 = (f32[2,2,16,256]{3,2,1,0:T(8,128)S(1)}, f32[2,2,16,256]{3,2,1,0:T(8,128)S(1)}, u32[]{:S(2)}, u32[]{:S(2)}) collective-permute-start(f32[2,2,16,256]{3,2,1,0:T(8,128)S(1)} %get-tuple-element.20), channel_id=1, source_target_pairs={{8,0},{16,8},{24,16},{32,24},{40,32},{48,40},{56,48},{64,56},{72,6... | collective-permute-start | bytes 196616 | tf_op jit(solution)/shard_map/ppermute | solution.py:378
  33.9 21.0 %copy-start.12 = (f32[2,2,16,256]{3,2,1,0:T(8,128)}, f32[2,2,16,256]{3,2,1,0:T(8,128)S(1)}, u32[]{:S(2)}) copy-start(f32[2,2,16,256]{3,2,1,0:T(8,128)S(1)} %collective-permute-done.1.xlow) | copy-start | bytes 196612
  35.8 19.1 %copy-start.13 = (f32[2,2,16,256]{3,2,1,0:T(8,128)}, f32[2,2,16,256]{3,2,1,0:T(8,128)S(1)}, u32[]{:S(2)}) copy-start(f32[2,2,16,256]{3,2,1,0:T(8,128)S(1)} %collective-permute-done.2.xhigh) | copy-start | bytes 196612
  36.0 13.4 %collective-permute-start.3 = (f32[2,68,2,256]{3,2,1,0:T(2,128)S(1)}, f32[2,68,2,256]{3,2,1,0:T(2,128)S(1)}, u32[]{:S(2)}, u32[]{:S(2)}) collective-permute-start(f32[2,68,2,256]{3,2,1,0:T(2,128)S(1)} %get-tuple-element.19), channel_id=1, source_target_pairs={{0,1},{1,2},{2,3},{3,4},{4,5},{5,6},{6,7},{8,9},{9,10},{10,11},{11... | collective-permute-start | bytes 835592 | tf_op jit(solution)/shard_map/ppermute | solution.py:399
  37.4 12.1 %collective-permute-start.4 = (f32[2,68,2,256]{3,2,1,0:T(2,128)S(1)}, f32[2,68,2,256]{3,2,1,0:T(2,128)S(1)}, u32[]{:S(2)}, u32[]{:S(2)}) collective-permute-start(f32[2,68,2,256]{3,2,1,0:T(2,128)S(1)} %get-tuple-element.18), channel_id=1, source_target_pairs={{1,0},{2,1},{3,2},{4,3},{5,4},{6,5},{7,6},{9,8},{10,9},{11,10},{12... | collective-permute-start | bytes 835592 | tf_op jit(solution)/shard_map/ppermute | solution.py:400
  41.1 1.0 copy-start.1
  44.0 10.9 %all-to-all-start.1 = ((f32[8,32,128]{2,1,0:T(8,128)}), f32[8,32,128]{2,1,0:T(8,128)S(1)}, u32[]{:S(2)}, u32[]{:S(2)}) async-start(f32[8,32,128]{2,1,0:T(8,128)} %collect.1), calls=%async_computation.1 | async-start | bytes 262144 | tf_op jit(solution)/shard_map/all_to_all | solution.py:39
  49.5 5.4 %copy-start.9 = (f32[2,68,2,256]{3,2,1,0:T(2,128)}, f32[2,68,2,256]{3,2,1,0:T(2,128)S(1)}, u32[]{:S(2)}) copy-start(f32[2,68,2,256]{3,2,1,0:T(2,128)S(1)} %collective-permute-done.3.ylow) | copy-start | bytes 835588
  49.5 5.4 %copy-start.10 = (f32[2,68,2,256]{3,2,1,0:T(2,128)}, f32[2,68,2,256]{3,2,1,0:T(2,128)S(1)}, u32[]{:S(2)}) copy-start(f32[2,68,2,256]{3,2,1,0:T(2,128)S(1)} %collective-permute-done.4.yhigh) | copy-start | bytes 835588
  54.9 0.7 copy-start.8
  74.9 59.7 %copy-start.3 = (f32[64,16,256]{2,1,0:T(8,128)S(1)}, f32[64,16,256]{2,1,0:T(8,128)}, u32[]{:S(2)}) copy-start(f32[64,16,256]{2,1,0:T(8,128)} %get-tuple-element.12.r) | copy-start | bytes 3145732
  74.9 59.7 %copy-start.4 = (f32[64,16,256]{2,1,0:T(8,128)S(1)}, f32[64,16,256]{2,1,0:T(8,128)}, u32[]{:S(2)}) copy-start(f32[64,16,256]{2,1,0:T(8,128)} %get-tuple-element.13.w) | copy-start | bytes 3145732
  74.9 21.0 %all-to-all-start.2 = ((f32[128,1,128]{2,1,0:T(1,128)}), f32[128,1,128]{2,1,0:T(1,128)S(1)}, u32[]{:S(2)}, u32[]{:S(2)}) async-start(f32[128,1,128]{2,1,0:T(1,128)} %get-tuple-element.11), calls=%async_computation.2 | async-start | bytes 131072 | tf_op jit(solution)/shard_map/all_to_all | solution.py:39
  95.9 11.1 %copy-start.11 = (f32[128,1,128]{2,1,0:T(1,128)}, f32[128,1,128]{2,1,0:T(1,128)S(1)}, u32[]{:S(2)}) copy-start(f32[128,1,128]{2,1,0:T(1,128)S(1)} %all-to-all-done.2.sums) | copy-start | bytes 196612
  133.2 4.7 %copy-start.5 = (f32[64,8,384]{2,1,0:T(8,128)}, f32[64,8,384]{2,1,0:T(8,128)S(1)}, u32[]{:S(2)}) copy-start(f32[64,8,384]{2,1,0:T(8,128)S(1)} %all_to_all.26) | copy-start | bytes 2359300
  133.2 3.8 %collective-permute-start.5 = (f32[64,8,384]{2,1,0:T(8,128)S(1)}, f32[64,8,384]{2,1,0:T(8,128)S(1)}, u32[]{:S(2)}, u32[]{:S(2)}) collective-permute-start(f32[64,8,384]{2,1,0:T(8,128)S(1)} %all_to_all.26), channel_id=1, source_target_pairs={{0,1},{1,0},{2,3},{3,2},{4,5},{5,4},{6,7},{7,6},{8,9},{9,8},{10,11... | collective-permute-start | bytes 2359304 | tf_op jit(solution)/shard_map/ppermute | solution.py:35
  137.0 0.9 copy-start.7

commit v2 on v1

v2 whole, which is shorter than its diff:
```python
import jax
import jax.numpy as jnp
from jax import lax
from jax.experimental import pallas as pl
from jax.experimental.pallas import tpu as pltpu
from jax.sharding import Mesh
from jax.sharding import PartitionSpec as P

ENERGY = ("energy_0", "energy_1")
KPT = ("kpt_0", "kpt_1")
CHIPS = ("energy_0", "energy_1", "kpt_0")
CORE = "kpt_1"
EVERY = ("energy_0", "energy_1", "kpt_0", "kpt_1")

NE = 16
NK = 8
NZC = 4
SUB = 8
LAYERS = 128
LD = 8
ORB = 3072
CY = 16
NY = 128
NZ = 256
PLANES = 64
EL = 4
W = 24
COL = ORB // NK
TL = COL // 128
PENALTY = 4.0


def swap_cores(x):
    return lax.ppermute(x, CORE, [(0, 1), (1, 0)])


def exchange(x, axis):
    return lax.all_to_all(x, axis, split_axis=0, concat_axis=0, tiled=True)


def in_hbm(x):
    return pltpu.with_memory_space_constraint(x, pltpu.HBM)


def params(mib):
    return pltpu.CompilerParams(vmem_limit_bytes=mib * 1024 * 1024)


def occupancy_body(energy, kpt, volts, weights, density, fixed, gate, own, other, xup, xdown, yup, ydown,
                   fixed_here, gate_here, fixed_ends, gate_ends, arrivals):
    z = pl.program_id(0)
    e = energy[0]
    k = kpt[0]
    core = k % 2
    whole = [
        pltpu.make_async_copy(fixed, fixed_here, arrivals.at[0]),
        pltpu.make_async_copy(gate, gate_here, arrivals.at[1]),
    ]
    ends = []
    for i, plane in enumerate((0, PLANES - 1)):
        ends.append(pltpu.make_async_copy(fixed.at[plane], fixed_ends.at[i], arrivals.at[2 + 2 * i]))
        ends.append(pltpu.make_async_copy(gate.at[plane], gate_ends.at[i], arrivals.at[3 + 2 * i]))

    @pl.when(z == 0)
    def _():
        for copy in ends + whole:
            copy.start()

    for half, out in ((0, own), (1, other)):
        which = core if half == 0 else 1 - core
        start = pl.multiple_of(which * COL, 128)
        zero = jnp.zeros((3, 128), jnp.float32)
        for i in range(0, NE, 2):
            total = None
            for n in range(EL):
                weight = jnp.broadcast_to(weights[0:1, n : n + 1], (16, COL))
                part = density[n, 8 * i : 8 * i + 16, pl.ds(start, COL)].astype(jnp.float32) * weight
                total = part if total is None else total + part
            for h in range(2):
                at = i + h
                for t in range(TL):
                    tile = total[8 * h : 8 * h + 8, 128 * t : 128 * (t + 1)]
                    out[at, 0, 8 * t : 8 * t + 8, :] = tile
                    if at + 1 < NE:
                        out[at + 1, 0, 24 + t : 25 + t, :] = tile[7:8]
                    if at > 0:
                        out[at - 1, 0, 27 + t : 28 + t, :] = tile[0:1]
        out[0, 0, 24:27, :] = zero
        out[NE - 1, 0, 27:30, :] = zero
        for i in range(NE):
            out[i, 0, 30:32, :] = zero[:2]

    @pl.when(z == 0)
    def _():
        for copy in ends:
            copy.wait()

    for dx in (-1, 1):
        for dy in (-1, 1):
            to_e = e + dx
            to_k = k + dy

            @pl.when((to_e >= 0) & (to_e < NE) & (to_k >= 0) & (to_k < NK) & (to_k // 2 == z))
            def _(dx=dx, dy=dy, to_e=to_e):
                i = 1 if dx == 1 else 0
                y = CY - 1 if dy == 1 else 0
                g = gate_ends[i, y : y + 1, :].astype(jnp.float32)
                line = fixed_ends[i, y : y + 1, :] + PENALTY * g * volts[(PLANES - 1) * i]
                other[to_e, 0, 30:31, :] = line[:, :128]
                other[to_e, 0, 31:32, :] = line[:, 128:]

    @pl.when(z == NZC - 1)
    def _():
        for copy in whole:
            copy.wait()
        for out, planes in ((xup, (PLANES - 2, PLANES - 1)), (xdown, (0, 1))):
            for i, p in enumerate(planes):
                g = gate_here[p].astype(jnp.float32)
                out[i] = fixed_here[p] + PENALTY * g * volts[p]
                if p in (0, PLANES - 1):
                    out[2] = g

        def one_plane(p, carry):
            volt = PENALTY * volts[p]
            for out, rows in ((yup, (CY - 2, CY - 1)), (ydown, (0, 1))):
                for i, y in enumerate(rows):
                    g = gate_here[p, y : y + 1, :].astype(jnp.float32)
                    out[i, pl.ds(p, 1), :] = fixed_here[p, y : y + 1, :] + volt * g
                    if y in (0, CY - 1):
                        out[2, pl.ds(p, 1), :] = g
            return carry

        lax.fori_loop(0, PLANES, one_plane, 0, unroll=8)


def occupancy_parts(e, k, volts, weights, density, fixed, gate):
    shape = jax.ShapeDtypeStruct((NE, NZC, 32, 128), jnp.float32)
    block = pl.BlockSpec((NE, 1, 32, 128), lambda z, *_: (0, z, 0, 0))
    xedge = jax.ShapeDtypeStruct((3, CY, NZ), jnp.float32)
    yedge = jax.ShapeDtypeStruct((3, PLANES, NZ), jnp.float32)
    whole = lambda x: pl.BlockSpec(x.shape, lambda z, *_: (0, 0, 0))
    hbm = pl.BlockSpec(memory_space=pltpu.HBM)
    return pl.pallas_call(
        occupancy_body,
        grid_spec=pltpu.PrefetchScalarGridSpec(
            num_scalar_prefetch=3,
            grid=(NZC,),
            in_specs=[
                pl.BlockSpec((1, EL), lambda z, *_: (0, 0)),
                pl.BlockSpec((EL, LAYERS, 2 * COL), lambda z, *_: (0, 0, z)),
                hbm,
                hbm,
            ],
            out_specs=[block, block, whole(xedge), whole(xedge), whole(yedge), whole(yedge)],
            scratch_shapes=[
                pltpu.VMEM((PLANES, CY, NZ), jnp.float32),
                pltpu.VMEM((PLANES, CY, NZ), jnp.int32),
                pltpu.VMEM((2, CY, NZ), jnp.float32),
                pltpu.VMEM((2, CY, NZ), jnp.int32),
                pltpu.SemaphoreType.DMA((6,)),
            ],
        ),
        out_shape=[shape, shape, xedge, xedge, yedge, yedge],
        compiler_params=params(12),
        name="occupancy_parts",
    )(e[None], k[None], in_hbm(volts), in_hbm(weights), in_hbm(density), in_hbm(fixed), in_hbm(gate))


def collect_body(where, parts, out, corners):
    e = where[0]
    k = where[1]
    total = parts[0]
    for i in range(1, NE * NZC):
        total = total + parts[i]
    for n in range(NK):
        out[n] = total
    for i, dx in enumerate((-1, 1)):
        for j, dy in enumerate((-1, 1)):
            from_e = e + dx
            from_k = k + dy
            there = (from_e >= 0) & (from_e < NE) & (from_k >= 0) & (from_k < NK)
            source = jnp.where(there, from_e * NZC + from_k // 2, 0)
            lines = parts[source, 30:32, :]
            corners[i, j : j + 1, 0:128] = jnp.where(there, lines[0:1], 0.0)
            corners[i, j : j + 1, 128:256] = jnp.where(there, lines[1:2], 0.0)


def collect(where, parts):
    whole = lambda shape: pl.BlockSpec(shape, lambda i, *_: (0, 0, 0))
    shapes = [(NK, 32, 128), (2, 2, NZ)]
    return pl.pallas_call(
        collect_body,
        grid_spec=pltpu.PrefetchScalarGridSpec(
            num_scalar_prefetch=1,
            grid=(1,),
            in_specs=[whole((NE * NZC, 32, 128))],
            out_specs=[whole(x) for x in shapes],
        ),
        out_shape=[jax.ShapeDtypeStruct(x, jnp.float32) for x in shapes],
        compiler_params=params(4),
        name="collect",
    )(where, parts)


def split_parts(x):
    high = x.astype(jnp.bfloat16)
    low = (x - high.astype(jnp.float32)).astype(jnp.bfloat16)
    return high, low


def spread(line, rows):
    block = jnp.broadcast_to(line, (16, 128)).astype(jnp.bfloat16)
    return jnp.concatenate([block] * (rows // 16), axis=0)


def counting(rows):
    return lax.broadcasted_iota(jnp.int32, (rows, 128), 0).astype(jnp.float32).astype(jnp.bfloat16)


def tiles_of(line):
    return [line[:, 128 * t : 128 * (t + 1)] for t in range(line.shape[1] // 128)]


def marks(index, rows, counts):
    one = jnp.ones((), jnp.bfloat16)
    zero = jnp.zeros((), jnp.bfloat16)
    return jnp.concatenate([jnp.where(counts[:rows] == spread(t, rows), one, zero) for t in tiles_of(index)], axis=1)


def charge_of(cells, values, first_plane, planes, y0):
    plane = (cells >> 15) - first_plane
    dy = ((cells >> 8) & (NY - 1)) - y0
    near = (dy >= -2) & (dy < CY + 2) & (plane >= 0) & (plane < planes)
    row = jnp.where(near, plane * W + jnp.where(dy >= 0, dy, dy + W), -1).astype(jnp.float32)
    z = (cells & (NZ - 1)).astype(jnp.float32)
    rows = planes * W
    counts = counting(NZ)
    high = values.astype(jnp.bfloat16).astype(jnp.float32)
    low = values - high
    zero = jnp.zeros((), jnp.bfloat16)
    tops, bottoms = [], []
    for t, h, l in zip(tiles_of(row), tiles_of(high), tiles_of(low)):
        hit = counts[:rows] == spread(t, rows)
        tops.append(jnp.where(hit, spread(h, rows), zero))
        bottoms.append(jnp.where(hit, spread(l, rows), zero))
    left = jnp.concatenate([jnp.concatenate(tops, axis=1), jnp.concatenate(bottoms, axis=1)], axis=0)
    right = marks(z, NZ, counts)
    both = lax.dot_general(left, right, (((1,), (1,)), ((), ())), preferred_element_type=jnp.float32)
    return both[:rows] + both[rows:]


def beside(field, plane):
    here = field[plane]
    lane = lax.broadcasted_iota(jnp.int32, (W, NZ), 1)
    total = field[plane + 1] + field[plane - 1]
    total = total + pltpu.roll(here, 1, 0) + pltpu.roll(here, W - 1, 0)
    total = total + jnp.where(lane == 0, 0.0, pltpu.roll(here, 1, 1))
    return here, total + jnp.where(lane == NZ - 1, 0.0, pltpu.roll(here, NZ - 1, 1))


def field_body(where, volts, occ, below, mine, above, corners, xlow, xhigh, ylow, yhigh, fixed, gate,
               sums, kept_out, fields_here, r_ext, w_ext, g_ext, fixed_here, gate_here, arrivals, leaving):
    e = where[0]
    k = where[1]
    y0 = k * CY
    copies = [
        pltpu.make_async_copy(fixed, fixed_here, arrivals.at[0]),
        pltpu.make_async_copy(gate, gate_here, arrivals.at[1]),
    ]
    for copy in copies:
        copy.start()
    row = lax.broadcasted_iota(jnp.int32, (W, NZ), 0)
    y = jnp.where(row < CY + 4, row, row - W) + y0
    valid = jnp.where((y >= 0) & (y < NY), 1.0, 0.0)

    def values_of(index):
        return jnp.concatenate(
            [occ[c, pl.ds(index(t), 1), :] for c in range(NK) for t in range(TL)], axis=1
        )

    def one_layer(j, carry):
        charge = charge_of(mine[pl.ds(j, 1), :], values_of(lambda t: 8 * t + j), 0, SUB, y0)
        r_ext[pl.ds(2 + SUB * j, SUB)] = -charge.reshape(SUB, W, NZ)
        return carry

    lax.fori_loop(0, LD, one_layer, 0, unroll=LD)
    charge = charge_of(below[7:8, :], values_of(lambda t: 24 + t), SUB - 2, 2, y0)
    r_ext[0:2] = -charge.reshape(2, W, NZ)
    charge = charge_of(above[0:1, :], values_of(lambda t: 27 + t), 0, 2, y0)
    r_ext[PLANES + 2 : PLANES + 4] = -charge.reshape(2, W, NZ)

    for at, halo in ((0, xlow), (PLANES + 2, xhigh)):
        for i in range(2):
            r_ext[at + i, 0:CY, :] = r_ext[at + i, 0:CY, :] + halo[i]
    g_ext[1, 0:CY, :] = xlow[2]
    g_ext[PLANES + 2, 0:CY, :] = xhigh[2]
    sub = lax.broadcasted_iota(jnp.int32, (8, NZ), 0)
    none = jnp.zeros((8, NZ), jnp.float32)
    line = lambda x: jnp.broadcast_to(x, (8, NZ))
    for at, i in ((1, 0), (PLANES + 2, 1)):
        tile = jnp.where(sub == 0, line(corners[i, 1:2, :]), jnp.where(sub == 7, line(corners[i, 0:1, :]), none))
        r_ext[at, CY:W, :] = r_ext[at, CY:W, :] + tile
        g_ext[at, CY:W, :] = none
    for copy in copies:
        copy.wait()

    def load_plane(p, carry):
        at = pl.ds(p, 1)
        g = gate_here[p].astype(jnp.float32)
        g_ext[p + 2, 0:CY, :] = g
        r_ext[p + 2, 0:CY, :] = r_ext[p + 2, 0:CY, :] + (fixed_here[p] + PENALTY * g * volts[p])
        tile = jnp.where(sub == 0, line(yhigh[0, at, :]), jnp.where(sub == 1, line(yhigh[1, at, :]), none))
        tile = jnp.where(sub == 6, line(ylow[0, at, :]), jnp.where(sub == 7, line(ylow[1, at, :]), tile))
        r_ext[p + 2, CY:W, :] = r_ext[p + 2, CY:W, :] + tile
        tile = jnp.where(sub == 0, line(yhigh[2, at, :]), jnp.where(sub == 7, line(ylow[2, at, :]), none))
        g_ext[p + 2, CY:W, :] = tile
        return carry

    lax.fori_loop(0, PLANES, load_plane, 0, unroll=8)

    def image_plane(p, carry):
        here, around = beside(r_ext, p + 1)
        x = e * PLANES + p - 1
        inside = jnp.where((x >= 0) & (x < NE * PLANES), 1.0, 0.0)
        w_ext[p] = ((6.0 + PENALTY * g_ext[p + 1]) * here - around) * (valid * inside)
        return carry

    lax.fori_loop(0, PLANES + 2, image_plane, 0, unroll=11)

    def sum_plane(p, carry):
        rr, rw, ww, waw = carry
        r = r_ext[p + 2, 0:CY, :]
        here, around = beside(w_ext, p + 1)
        image = (6.0 + PENALTY * g_ext[p + 2]) * here - around
        w = here[0:CY]
        fields_here[0, p] = r
        fields_here[1, p] = w
        return rr + r * r, rw + r * w, ww + w * w, waw + w * image[0:CY]

    zero = jnp.zeros((CY, NZ), jnp.float32)
    totals = (zero,) * 4
    kept = []
    for j in range(LD):
        totals = lax.fori_loop(SUB * j, SUB * (j + 1), sum_plane, totals, unroll=SUB)
        at = pl.ds(SUB * j, SUB)
        kept.append(pltpu.make_async_copy(fields_here.at[:, at], kept_out.at[:, at], leaving.at[j]))
        kept[-1].start()
    lane = lax.broadcasted_iota(jnp.int32, (1, 128), 1)
    line = jnp.zeros((1, 128), jnp.float32)
    for i, total in enumerate(totals):
        line = line + jnp.where(lane == i, jnp.sum(total), 0.0)
    for d in range(NE * NK):
        sums[d] = line
    for copy in kept:
        copy.wait()


def fields(where, volts, occ, cells, corners, fixed, gate, xlow, xhigh, ylow, yhigh):
    whole = lambda x: pl.BlockSpec(x.shape, lambda i, *_: (0,) * x.ndim)
    near = lambda shift: pl.BlockSpec(
        (LD, ORB), lambda i, where, *_: (jnp.clip(where[0] + shift, 0, NE - 1), 0)
    )
    shapes = [
        jax.ShapeDtypeStruct((NE * NK, 1, 128), jnp.float32),
        pltpu.HBM((2, PLANES, CY, NZ), jnp.float32),
    ]
    return pl.pallas_call(
        field_body,
        grid_spec=pltpu.PrefetchScalarGridSpec(
            num_scalar_prefetch=2,
            grid=(1,),
            in_specs=[whole(occ), near(-1), near(0), near(1)]
            + [whole(x) for x in (corners, xlow, xhigh, ylow, yhigh)]
            + [pl.BlockSpec(memory_space=pltpu.HBM)] * 2,
            out_specs=[
                pl.BlockSpec((NE * NK, 1, 128), lambda i, *_: (0, 0, 0)),
                pl.BlockSpec(memory_space=pltpu.HBM),
            ],
            scratch_shapes=[
                pltpu.VMEM((2, PLANES, CY, NZ), jnp.float32),
                pltpu.VMEM((PLANES + 4, W, NZ), jnp.float32),
                pltpu.VMEM((PLANES + 2, W, NZ), jnp.float32),
                pltpu.VMEM((PLANES + 4, W, NZ), jnp.float32),
                pltpu.VMEM((PLANES, CY, NZ), jnp.float32),
                pltpu.VMEM((PLANES, CY, NZ), jnp.int32),
                pltpu.SemaphoreType.DMA((2,)),
                pltpu.SemaphoreType.DMA((LD,)),
            ],
        ),
        out_shape=shapes,
        compiler_params=params(16),
        name="fields",
    )(where, volts, occ, cells, cells, cells, corners, xlow, xhigh, ylow, yhigh, in_hbm(fixed), in_hbm(gate))


def pick_body(where, mine, rw_kept, out, rw, arrivals):
    copies = []
    for j in range(LD):
        at = pl.ds(SUB * j, SUB)
        copies.append(pltpu.make_async_copy(rw_kept.at[:, at], rw.at[:, at], arrivals.at[j]))
        copies[-1].start()
    y0 = where[1] * CY
    wide = 2 * COL
    counts = counting(NZ)

    def one_layer(j, carry):
        at = pl.ds(SUB * j, SUB)
        both = jnp.concatenate([rw[0, at].reshape(SUB * CY, NZ), rw[1, at].reshape(SUB * CY, NZ)], axis=0)
        high, low = split_parts(both)
        for n in range(ORB // wide):
            cells = mine[pl.ds(j, 1), n * wide : (n + 1) * wide]
            dy = ((cells >> 8) & (NY - 1)) - y0
            row = jnp.where((dy >= 0) & (dy < CY), (cells >> 15) * CY + dy, -1)
            z = cells & (NZ - 1)
            right = marks(z.astype(jnp.float32), NZ, counts)
            lines = jnp.dot(high, right, preferred_element_type=jnp.float32)
            lines = lines + jnp.dot(low, right, preferred_element_type=jnp.float32)
            hit = lax.broadcasted_iota(jnp.int32, (SUB * CY, wide), 0) == row
            for f in range(2):
                part = lines[f * SUB * CY : (f + 1) * SUB * CY]
                value = jnp.sum(jnp.where(hit, part, 0.0), axis=0, keepdims=True)
                for h in range(2):
                    out[2 * n + h, pl.ds(f * LD + j, 1), :] = value[:, h * COL : (h + 1) * COL]
        return carry

    for j in range(LD):
        copies[j].wait()
        one_layer(j, 0)


def pick(where, cells, rw):
    whole = lambda x: pl.BlockSpec(x.shape, lambda i, *_: (0,) * x.ndim)
    shape = jax.ShapeDtypeStruct((NK, 2 * LD, COL), jnp.float32)
    return pl.pallas_call(
        pick_body,
        grid_spec=pltpu.PrefetchScalarGridSpec(
            num_scalar_prefetch=1,
            grid=(1,),
            in_specs=[pl.BlockSpec((LD, ORB), lambda i, where: (where[0], 0)), pl.BlockSpec(memory_space=pltpu.HBM)],
            out_specs=whole(shape),
            scratch_shapes=[pltpu.VMEM(rw.shape, jnp.float32), pltpu.SemaphoreType.DMA((LD,))],
        ),
        out_shape=shape,
        compiler_params=params(12),
        name="pick",
    )(where, cells, in_hbm(rw))


def mix_body(sums, picked, scalars, out):
    line = jnp.sum(sums[...].reshape(NE * NK, 128), axis=0, keepdims=True)
    lane = lax.broadcasted_iota(jnp.int32, (1, 128), 1)
    rr, rw, ww, waw = [
        jnp.broadcast_to(jnp.sum(jnp.where(lane == i, line, 0.0), axis=1, keepdims=True), (1, 128)) for i in range(4)
    ]
    alpha = rr / rw
    norm = alpha * alpha * ww - rr
    ratio = norm / rr
    ahead = 1.0 + ratio
    curve = ahead * ahead * rw - 2.0 * ahead * alpha * ww + alpha * alpha * waw
    small = (norm <= 1e-9 * rr) | (curve <= 0.0)
    step = jnp.where(small, alpha, norm / curve)
    ahead = jnp.where(small, 1.0, ahead)
    c_r = alpha + step * ahead
    c_w = -alpha * step
    scalars[...] = jnp.where(lane == 0, c_r, c_w)
    total = picked[0]
    for i in range(1, NK):
        total = total + picked[i]
    c_r = jnp.concatenate([c_r] * TL, axis=1)
    c_w = jnp.concatenate([c_w] * TL, axis=1)
    value = c_r * total[:LD] + c_w * total[LD:]
    for d in range(NE * NZC):
        out[d] = value


def mix(sums, picked):
    return pl.pallas_call(
        mix_body,
        out_shape=[
            jax.ShapeDtypeStruct((1, 128), jnp.float32),
            pltpu.HBM((NE * NZC, LD, COL), jnp.float32),
        ],
        compiler_params=params(4),
        name="mix",
    )(sums, picked)


def blend_body(scalars, rw, out):
    c_r = jnp.broadcast_to(scalars[0:1, 0:1], (CY, NZ))
    c_w = jnp.broadcast_to(scalars[0:1, 1:2], (CY, NZ))

    def one_plane(p, carry):
        out[p] = c_r * rw[0, p] + c_w * rw[1, p]
        return carry

    lax.fori_loop(0, PLANES, one_plane, 0, unroll=8)


def blend(scalars, rw):
    return pl.pallas_call(
        blend_body,
        out_shape=jax.ShapeDtypeStruct((PLANES, CY, NZ), jnp.float32),
        compiler_params=params(6),
        name="blend",
    )(scalars, rw)


def band_body(core, density, same, cross, out, acc):
    z = pl.program_id(0)

    @pl.when(z == 0)
    def _():
        acc[...] = jnp.zeros_like(acc)

    for half, values in ((0, same), (1, cross)):
        which = core[0] if half == 0 else 1 - core[0]
        start = pl.multiple_of(which * COL, 128)
        for m in range(0, NE, 2):
            v = values[m : m + 2, 0].reshape(16, COL)
            for i in range(EL):
                part = density[i, 8 * m : 8 * m + 16, pl.ds(start, COL)].astype(jnp.float32) * v
                total = part[:, :128]
                for t in range(1, TL):
                    total = total + part[:, 128 * t : 128 * (t + 1)]
                acc[i, 8 * m : 8 * m + 16] = acc[i, 8 * m : 8 * m + 16] + total

    @pl.when(z == NZC - 1)
    def _():
        for i in range(EL):
            out[i : i + 1, :] = jnp.sum(acc[i].T, axis=0, keepdims=True) * ORB**-0.5


def band(core, density, same, cross):
    values = pl.BlockSpec((NE, 1, LD, COL), lambda z, *_: (0, z, 0, 0))
    return pl.pallas_call(
        band_body,
        grid_spec=pltpu.PrefetchScalarGridSpec(
            num_scalar_prefetch=1,
            grid=(NZC,),
            in_specs=[pl.BlockSpec((EL, LAYERS, 2 * COL), lambda z, *_: (0, 0, z)), values, values],
            out_specs=pl.BlockSpec((EL, LAYERS), lambda z, *_: (0, 0)),
            scratch_shapes=[pltpu.VMEM((EL, LAYERS, 128), jnp.float32)],
        ),
        out_shape=jax.ShapeDtypeStruct((EL, LAYERS), jnp.float32),
        compiler_params=params(8),
        name="band",
    )(core, density, same, cross)


def shift_up(x, axis):
    return lax.ppermute(x, axis, [(i, i + 1) for i in range(lax.axis_size(axis) - 1)])


def shift_down(x, axis):
    return lax.ppermute(x, axis, [(i + 1, i) for i in range(lax.axis_size(axis) - 1)])


def one_step(density, quad_weights, orbital_cells, fixed_charge, gate_mask, gate_voltage):
    e = lax.axis_index(ENERGY).astype(jnp.int32)
    k = lax.axis_index(KPT).astype(jnp.int32)
    core = lax.axis_index(CORE).astype(jnp.int32)[None]
    where = jnp.stack([e, k])
    density = density.reshape(EL, LAYERS, ORB)

    own, other, xup, xdown, yup, ydown = occupancy_parts(
        e, k, gate_voltage, quad_weights.reshape(1, EL), density, fixed_charge, gate_mask
    )
    chips = NE * NZC
    pair = own.reshape(chips, 32, 128) + swap_cores(other.reshape(chips, 32, 128))
    parts = exchange(pair, CHIPS)
    xlow = shift_up(xup, ENERGY)
    xhigh = shift_down(xdown, ENERGY)
    ylow = shift_up(yup, KPT)
    yhigh = shift_down(ydown, KPT)
    parts, xlow, xhigh = lax.optimization_barrier((parts, xlow, xhigh))
    occ, corners = collect(where, parts)
    occ = exchange(occ, KPT)
    sums, rw = fields(
        where, gate_voltage, occ, orbital_cells, corners, fixed_charge, gate_mask, xlow, xhigh, ylow, yhigh
    )
    all_sums = exchange(sums, EVERY)
    picked = pick(where, orbital_cells, rw)
    picked = exchange(picked, KPT)
    scalars, values = mix(all_sums, picked)
    same = exchange(values, CHIPS)
    potential = blend(scalars, rw)
    cross = swap_cores(same)
    shape = (NE, NZC, LD, COL)
    shift = band(core, density, same.reshape(shape), cross.reshape(shape))
    return potential, shift.reshape(EL, 1, LAYERS)


def solution(mesh):
    split = Mesh(mesh.devices.reshape(4, 4, 4, 2), ("energy_0", "energy_1", "kpt_0", "kpt_1"))
    in_specs = (
        P(ENERGY, KPT, None, None),
        P(ENERGY, KPT),
        P(),
        P(ENERGY, KPT, None),
        P(ENERGY, KPT, None),
        P(ENERGY),
    )
    out_specs = (P(ENERGY, KPT, None), P(ENERGY, KPT, None))
    return jax.shard_map(one_step, mesh=split, in_specs=in_specs, out_specs=out_specs, check_vma=False)
```

time: 144 us -> 121 us (0.84)
  Pallas kernels: 45.6 us -> 33.5 us
  starting transfers between devices: 31.5 us -> 27.3 us
  local copies, waits for them, and re-layouts: 3.97 us -> 0.02 us
  other arithmetic: 4.76 us -> 1.27 us
  waiting for transfers between devices: 20 us -> 21.8 us
    pallas_call x1, Pallas kernels: 19.3 us -> 12.5 us  [fields(): pl.pallas_call(field_body, grid_spec=pltpu.PrefetchScalarGridSpec(num_sca...]
    all_to_all x3, starting transfers between devices: 24.1 us -> 19.8 us  [exchange(): return lax.all_to_all(x, axis, split_axis=0, concat_axis=0, tiled=True)]
    all_to_all x3, waiting for transfers between devices: 7.82 us -> 11.4 us  [exchange(): return lax.all_to_all(x, axis, split_axis=0, concat_axis=0, tiled=True)]
    pallas_call x1, Pallas kernels: 13.2 us -> 9.79 us  [pick(): pl.pallas_call(pick_body, grid_spec=pltpu.PrefetchScalarGridSpec(num_scal...]
    ppermute x4, waiting for transfers between devices: 9.57 us -> 6.66 us  [the longest x2 4.89 us: shift_up(): lax.ppermute(x, axis, [(i, i + 1) for i in range(lax.axis_size(axis) - 1)])]
    unnamed x30 -> x8, local copies, waits for them, and re-layouts: 2.57 us -> 0.02 us
    add x2 -> x1, other arithmetic: 3.62 us -> 1.19 us  [one_step(): own.reshape(chips, 32, 128) + swap_cores(other.reshape(chips, 32, 128))]
    pallas_call x1, Pallas kernels: 4.02 us -> 1.84 us  [band(): pl.pallas_call(band_body, grid_spec=pltpu.PrefetchScalarGridSpec(num_scal...]
  transfers between devices with their start and end apart: 9 -> 9, of which waited for: 5 -> 6; matrix products, arithmetic and copies ran while one was open for 4% -> 0% of each run, Pallas kernels for 11% -> 10%
where the time goes in v2:
time: 121 us; the launch traced here: 120 us
  blocking collectives  35.1 us (29%)
  Pallas kernels  33.5 us (28%)
  starting transfers between devices  27.3 us (23%)
  waiting for transfers between devices  21.8 us (18%)
  other arithmetic  1.27 us (1%)
    all_to_all x2, blocking collectives, exchange(): return lax.all_to_all(x, axis, split_axis=0, concat_axis=0, tiled=True)  35.1 us
    all_to_all x3, starting transfers between devices, exchange(): return lax.all_to_all(x, axis, split_axis=0, concat_axis=0, tiled=True)  19.8 us
    pallas_call x1, Pallas kernels, fields(): pl.pallas_call(field_body, grid_spec=pltpu.PrefetchScalarGridSpec(num_sca...  12.5 us
    all_to_all x3, waiting for transfers between devices, exchange(): return lax.all_to_all(x, axis, split_axis=0, concat_axis=0, tiled=True)  11.4 us
    pallas_call x1, Pallas kernels, pick(): pl.pallas_call(pick_body, grid_spec=pltpu.PrefetchScalarGridSpec(num_scal...  9.79 us
    pallas_call x1, Pallas kernels, occupancy_parts(): pl.pallas_call(occupancy_body, grid_spec=pltpu.PrefetchScalarGridSpec(num...  5.72 us
    ppermute x2, waiting for transfers between devices, shift_up(): lax.ppermute(x, axis, [(i, i + 1) for i in range(lax.axis_size(axis) - 1)])  4.89 us
    ppermute x2, starting transfers between devices, shift_up(): lax.ppermute(x, axis, [(i, i + 1) for i in range(lax.axis_size(axis) - 1)])  4.78 us
  transfers between devices with their start and end apart: 9, of which 6 were waited for; matrix products, arithmetic and copies ran while one was open for 0% of the time, Pallas kernels for 10%

profile of v2, /device:TPU:0, one launch (start us, length us, event | category | flops | bytes accessed | tf_op | source)
XLA Modules:
  0.0 119.7 jit_solution(10341390556243160349)
XLA Ops:
  0.6 5.7 %occupancy_parts.1 = (f32[16,4,32,128]{3,2,1,0:T(8,128)S(1)}, f32[16,4,32,128]{3,2,1,0:T(8,128)S(1)}, f32[3,16,256]{2,1,0:T(8,128)}, f32[3,16,256]{2,1,0:T(8,128...) custom-call(s32[1]{0:T(128)} %bitcast.energy, s32[1]{0:T(128)} %bitcast.1.kpt, f32[64]{0:T(128)} %volts.3, ...), custom_call_target="tpu_custom_call" | custom-call | tf_op jit(solution)/shard_map/occupancy_parts/pallas_call | solution.py:143
  6.4 0.1 collective-permute-start
  6.5 2.6 %collective-permute-done = f32[64,32,128]{2,1,0:T(8,128)S(1)} collective-permute-done((f32[64,32,128]{2,1,0:T(8,128)S(1)}, f32[64,32,128]{2,1,0:T(8,128)S(1)}, u32[]{:S(2)}, u32[]{:S(2)}) %collective-permute-start) | collective-permute-done | bytes 1048608 | tf_op jit(solution)/shard_map/ppermute | solution.py:34
  9.1 1.2 bitcast_add_fusion
  10.3 11.7 %all-to-all-start = ((f32[64,32,128]{2,1,0:T(8,128)}), f32[64,32,128]{2,1,0:T(8,128)S(1)}, u32[]{:S(2)}, u32[]{:S(2)}) async-start(f32[64,32,128]{2,1,0:T(8,128)} %bitcast_add_fusion), calls=%async_computation | async-start | bytes 2097152 | tf_op jit(solution)/shard_map/all_to_all | solution.py:38
  22.0 3.5 %collective-permute-start.1 = (f32[3,16,256]{2,1,0:T(8,128)}, f32[3,16,256]{2,1,0:T(8,128)S(1)}, u32[]{:S(2)}, u32[]{:S(2)}) collective-permute-start(f32[3,16,256]{2,1,0:T(8,128)} %get-tuple-element.19), channel_id=1, source_target_pairs={{0,8},{8,16},{16,24},{24,32},{32,40},{40,48},{48,56},{56,64},{64,7... | collective-permute-start | bytes 147464 | tf_op jit(solution)/shard_map/ppermute | solution.py:551
  25.5 1.3 %collective-permute-start.2 = (f32[3,16,256]{2,1,0:T(8,128)}, f32[3,16,256]{2,1,0:T(8,128)S(1)}, u32[]{:S(2)}, u32[]{:S(2)}) collective-permute-start(f32[3,16,256]{2,1,0:T(8,128)} %get-tuple-element.20), channel_id=1, source_target_pairs={{8,0},{16,8},{24,16},{32,24},{40,32},{48,40},{56,48},{64,56},{72,6... | collective-permute-start | bytes 147464 | tf_op jit(solution)/shard_map/ppermute | solution.py:555
  26.8 1.3 %collective-permute-start.3 = (f32[3,64,256]{2,1,0:T(8,128)S(1)}, f32[3,64,256]{2,1,0:T(8,128)S(1)}, u32[]{:S(2)}, u32[]{:S(2)}) collective-permute-start(f32[3,64,256]{2,1,0:T(8,128)S(1)} %get-tuple-element.26), channel_id=1, source_target_pairs={{0,1},{1,2},{2,3},{3,4},{4,5},{5,6},{6,7},{8,9},{9,10},{10,11},{11... | collective-permute-start | bytes 589832 | tf_op jit(solution)/shard_map/ppermute | solution.py:551
  28.1 1.3 %collective-permute-start.4 = (f32[3,64,256]{2,1,0:T(8,128)S(1)}, f32[3,64,256]{2,1,0:T(8,128)S(1)}, u32[]{:S(2)}, u32[]{:S(2)}) collective-permute-start(f32[3,64,256]{2,1,0:T(8,128)S(1)} %get-tuple-element.27), channel_id=1, source_target_pairs={{1,0},{2,1},{3,2},{4,3},{5,4},{6,5},{7,6},{9,8},{10,9},{11,10},{12... | collective-permute-start | bytes 589832 | tf_op jit(solution)/shard_map/ppermute | solution.py:555
  29.4 0.1 pad_add_fusion.where
  29.4 4.9 %collective-permute-done.1.xlow = f32[3,16,256]{2,1,0:T(8,128)S(1)} collective-permute-done((f32[3,16,256]{2,1,0:T(8,128)}, f32[3,16,256]{2,1,0:T(8,128)S(1)}, u32[]{:S(2)}, u32[]{:S(2)}) %collective-permute-start.1) | collective-permute-done | bytes 49184 | tf_op jit(solution)/shard_map/ppermute | solution.py:551
  34.3 1.8 %collective-permute-done.2.xhigh = f32[3,16,256]{2,1,0:T(8,128)S(1)} collective-permute-done((f32[3,16,256]{2,1,0:T(8,128)}, f32[3,16,256]{2,1,0:T(8,128)S(1)}, u32[]{:S(2)}, u32[]{:S(2)}) %collective-permute-start.2) | collective-permute-done | bytes 49184 | tf_op jit(solution)/shard_map/ppermute | solution.py:555
  36.1 5.4 %all-to-all-done.parts = f32[64,32,128]{2,1,0:T(8,128)S(1)} async-done(((f32[64,32,128]{2,1,0:T(8,128)}), f32[64,32,128]{2,1,0:T(8,128)S(1)}, u32[]{:S(2)}, u32[]{:S(2)}) %all-to-all-start) | async-done | bytes 1048608 | tf_op jit(solution)/shard_map/all_to_all | solution.py:38
  41.5 1.3 %collect.1 = (f32[8,32,128]{2,1,0:T(8,128)}, f32[2,2,256]{2,1,0:T(2,128)S(1)}) custom-call(s32[2]{0:T(128)S(1)} %pad_add_fusion.where, f32[64,32,128]{2,1,0:T(8,128)S(1)} %all-to-all-done.parts), custom_call_target="tpu_custom_call" | custom-call | tf_op jit(solution)/shard_map/collect/pallas_call | solution.py:191
  42.8 3.4 %all-to-all-start.1 = ((f32[8,32,128]{2,1,0:T(8,128)}), f32[8,32,128]{2,1,0:T(8,128)S(1)}, u32[]{:S(2)}, u32[]{:S(2)}) async-start(f32[8,32,128]{2,1,0:T(8,128)} %get-tuple-element.22), calls=%async_computation.1 | async-start | bytes 262144 | tf_op jit(solution)/shard_map/all_to_all | solution.py:38
  46.2 0.0 collective-permute-done.3.ylow
  46.2 0.0 collective-permute-done.4.yhigh
  46.2 6.0 %all-to-all-done.1.occ = f32[8,32,128]{2,1,0:T(8,128)S(1)} async-done(((f32[8,32,128]{2,1,0:T(8,128)}), f32[8,32,128]{2,1,0:T(8,128)S(1)}, u32[]{:S(2)}, u32[]{:S(2)}) %all-to-all-start.1) | async-done | bytes 131104 | tf_op jit(solution)/shard_map/all_to_all | solution.py:38
  52.2 0.0 copy-done
  52.2 0.0 copy-done.3
  52.2 12.5 %fields.1 = (f32[128,1,128]{2,1,0:T(1,128)}, f32[2,64,16,256]{3,2,1,0:T(8,128)}) custom-call(s32[2]{0:T(128)S(1)} %pad_add_fusion.where, f32[64]{0:T(128)S(1)} %copy-done.3, f32[8,32,128]{2,1,0:T(8,128)S(1)} %all-to-all-done.1.occ, s32[128,3072]{1,0:T(8,128)S(1)} %copy-done, s32[128,3072]{1,0:T(8,128)S(1)} %copy-done, s32[128,3072]{1,0:T(8,128)S(1)} %copy-done, ...), custom_call_target="tpu_custom_call" | custom-call | tf_op jit(solution)/shard_map/fields/pallas_call | solution.py:367
  64.8 4.8 %all-to-all-start.2 = ((f32[128,1,128]{2,1,0:T(1,128)}), f32[128,1,128]{2,1,0:T(1,128)S(1)}, u32[]{:S(2)}, u32[]{:S(2)}) async-start(f32[128,1,128]{2,1,0:T(1,128)} %get-tuple-element.28), calls=%async_computation.2 | async-start | bytes 131072 | tf_op jit(solution)/shard_map/all_to_all | solution.py:38
  69.5 9.8 %pick.1 = f32[8,16,384]{2,1,0:T(8,128)S(1)} custom-call(s32[2]{0:T(128)S(1)} %pad_add_fusion.where, s32[128,3072]{1,0:T(8,128)S(1)} %copy-done, f32[2,64,16,256]{3,2,1,0:T(8,128)} %get-tuple-element.29.rw_kept.rw), custom_call_target="tpu_custom_call" | custom-call | tf_op jit(solution)/shard_map/pick/pallas_call | solution.py:434
  79.3 0.0 copy-start.2
  79.4 0.0 all-to-all-done.2.sums
  79.4 10.7 %all_to_all.25.picked = f32[8,16,384]{2,1,0:T(8,128)S(1)} all-to-all(f32[8,16,384]{2,1,0:T(8,128)S(1)} %pick.1), channel_id=1, replica_groups=mesh['energy_0'=4,'energy_1'=4,'kpt_0'=4,'kpt_1'=2] {'kpt_0','kpt_1'}, dimensions={0} | all-to-all | bytes 393216 | tf_op jit(solution)/shard_map/all_to_all | solution.py:38
  90.1 1.1 mix.1
  91.2 24.4 %all_to_all.26 = f32[64,8,384]{2,1,0:T(8,128)S(1)} all-to-all(f32[64,8,384]{2,1,0:T(8,128)} %get-tuple-element.31), channel_id=1, replica_groups=mesh['energy_0'=4,'energy_1'=4,'kpt_0'=4,'kpt_1'=2] {'energy_0','energy_..., dimensions={0} | all-to-all | bytes 1572864 | tf_op jit(solution)/shard_map/all_to_all | solution.py:38
  115.6 0.0 collective-permute-start.5
  115.6 1.2 blend.1
  116.8 1.1 collective-permute-done.5
  117.9 1.8 %band.1 = f32[4,128]{1,0:T(4,128)} custom-call(s32[1]{0:T(128)} %bitcast.6.core, bf16[4,128,3072]{2,1,0:T(8,128)(2,1)S(1)} %bitcast.14, f32[16,4,8,384]{3,2,1,0:T(8,128)S(1)} %bitcast.15, f32[16,4,8,384]{3,2,1,0:T(8,128)S(1)} %bitcast.16), custom_call_target="tpu_custom_call" | custom-call | tf_op jit(solution)/shard_map/band/pallas_call | solution.py:535
  (5 shorter events, 0.0 us)
Async XLA Ops:
  6.4 2.7 %collective-permute-start = (f32[64,32,128]{2,1,0:T(8,128)S(1)}, f32[64,32,128]{2,1,0:T(8,128)S(1)}, u32[]{:S(2)}, u32[]{:S(2)}) collective-permute-start(f32[64,32,128]{2,1,0:T(8,128)S(1)} %bitcast.17), channel_id=1, source_target_pairs={{0,1},{1,0},{2,3},{3,2},{4,5},{5,4},{6,7},{7,6},{8,9},{9,8},{10,11... | collective-permute-start | bytes 3145736 | tf_op jit(solution)/shard_map/ppermute | solution.py:34
  10.3 41.9 %copy-start = (s32[128,3072]{1,0:T(8,128)S(1)}, s32[128,3072]{1,0:T(8,128)}, u32[]{:S(2)}) copy-start(s32[128,3072]{1,0:T(8,128)} %mine.3) | copy-start | bytes 4718596
  10.3 41.9 %copy-start.3 = (f32[64]{0:T(128)S(1)}, f32[64]{0:T(128)}, u32[]{:S(2)}) copy-start(f32[64]{0:T(128)} %volts.3) | copy-start | bytes 772
  10.3 31.2 %all-to-all-start = ((f32[64,32,128]{2,1,0:T(8,128)}), f32[64,32,128]{2,1,0:T(8,128)S(1)}, u32[]{:S(2)}, u32[]{:S(2)}) async-start(f32[64,32,128]{2,1,0:T(8,128)} %bitcast_add_fusion), calls=%async_computation | async-start | bytes 2097152 | tf_op jit(solution)/shard_map/all_to_all | solution.py:38
  22.0 12.4 %collective-permute-start.1 = (f32[3,16,256]{2,1,0:T(8,128)}, f32[3,16,256]{2,1,0:T(8,128)S(1)}, u32[]{:S(2)}, u32[]{:S(2)}) collective-permute-start(f32[3,16,256]{2,1,0:T(8,128)} %get-tuple-element.19), channel_id=1, source_target_pairs={{0,8},{8,16},{16,24},{24,32},{32,40},{40,48},{48,56},{56,64},{64,7... | collective-permute-start | bytes 147464 | tf_op jit(solution)/shard_map/ppermute | solution.py:551
  25.5 10.6 %collective-permute-start.2 = (f32[3,16,256]{2,1,0:T(8,128)}, f32[3,16,256]{2,1,0:T(8,128)S(1)}, u32[]{:S(2)}, u32[]{:S(2)}) collective-permute-start(f32[3,16,256]{2,1,0:T(8,128)} %get-tuple-element.20), channel_id=1, source_target_pairs={{8,0},{16,8},{24,16},{32,24},{40,32},{48,40},{56,48},{64,56},{72,6... | collective-permute-start | bytes 147464 | tf_op jit(solution)/shard_map/ppermute | solution.py:555
  26.8 19.4 %collective-permute-start.3 = (f32[3,64,256]{2,1,0:T(8,128)S(1)}, f32[3,64,256]{2,1,0:T(8,128)S(1)}, u32[]{:S(2)}, u32[]{:S(2)}) collective-permute-start(f32[3,64,256]{2,1,0:T(8,128)S(1)} %get-tuple-element.26), channel_id=1, source_target_pairs={{0,1},{1,2},{2,3},{3,4},{4,5},{5,6},{6,7},{8,9},{9,10},{10,11},{11... | collective-permute-start | bytes 589832 | tf_op jit(solution)/shard_map/ppermute | solution.py:551
  28.1 18.1 %collective-permute-start.4 = (f32[3,64,256]{2,1,0:T(8,128)S(1)}, f32[3,64,256]{2,1,0:T(8,128)S(1)}, u32[]{:S(2)}, u32[]{:S(2)}) collective-permute-start(f32[3,64,256]{2,1,0:T(8,128)S(1)} %get-tuple-element.27), channel_id=1, source_target_pairs={{1,0},{2,1},{3,2},{4,3},{5,4},{6,5},{7,6},{9,8},{10,9},{11,10},{12... | collective-permute-start | bytes 589832 | tf_op jit(solution)/shard_map/ppermute | solution.py:555
  42.8 9.4 %all-to-all-start.1 = ((f32[8,32,128]{2,1,0:T(8,128)}), f32[8,32,128]{2,1,0:T(8,128)S(1)}, u32[]{:S(2)}, u32[]{:S(2)}) async-start(f32[8,32,128]{2,1,0:T(8,128)} %get-tuple-element.22), calls=%async_computation.1 | async-start | bytes 262144 | tf_op jit(solution)/shard_map/all_to_all | solution.py:38
  64.8 14.6 %all-to-all-start.2 = ((f32[128,1,128]{2,1,0:T(1,128)}), f32[128,1,128]{2,1,0:T(1,128)S(1)}, u32[]{:S(2)}, u32[]{:S(2)}) async-start(f32[128,1,128]{2,1,0:T(1,128)} %get-tuple-element.28), calls=%async_computation.2 | async-start | bytes 131072 | tf_op jit(solution)/shard_map/all_to_all | solution.py:38
  79.3 36.2 %copy-start.2 = (f32[2,64,16,256]{3,2,1,0:T(8,128)S(1)}, f32[2,64,16,256]{3,2,1,0:T(8,128)}, u32[]{:S(2)}) copy-start(f32[2,64,16,256]{3,2,1,0:T(8,128)} %get-tuple-element.29.rw_kept.rw) | copy-start | bytes 6291460
  91.2 26.7 %copy-start.1 = (bf16[4,1,128,3072]{3,2,1,0:T(8,128)(2,1)S(1)}, bf16[4,1,128,3072]{3,2,1,0:T(8,128)(2,1)}, u32[]{:S(2)}) copy-start(bf16[4,1,128,3072]{3,2,1,0:T(8,128)(2,1)} %param.6) | copy-start | bytes 9437188
  115.6 2.3 %collective-permute-start.5 = (f32[64,8,384]{2,1,0:T(8,128)S(1)}, f32[64,8,384]{2,1,0:T(8,128)S(1)}, u32[]{:S(2)}, u32[]{:S(2)}) collective-permute-start(f32[64,8,384]{2,1,0:T(8,128)S(1)} %all_to_all.26), channel_id=1, source_target_pairs={{0,1},{1,0},{2,3},{3,2},{4,5},{5,4},{6,7},{7,6},{8,9},{9,8},{10,11... | collective-permute-start | bytes 2359304 | tf_op jit(solution)/shard_map/ppermute | solution.py:34

commit v3 on v2

v3 whole, which is shorter than its diff:
```python
import jax
import jax.numpy as jnp
from jax import lax
from jax.experimental import pallas as pl
from jax.experimental.pallas import tpu as pltpu
from jax.sharding import Mesh
from jax.sharding import PartitionSpec as P

ENERGY = ("energy_0", "energy_1")
KPT = ("kpt_0", "kpt_1")
CHIPS = ("energy_0", "energy_1", "kpt_0")
CORE = "kpt_1"
EVERY = ("energy_0", "energy_1", "kpt_0", "kpt_1")

NE = 16
NK = 8
NZC = 4
SUB = 8
LAYERS = 128
LD = 8
ORB = 3072
CY = 16
NY = 128
NZ = 256
PLANES = 64
EL = 4
W = 24
WC = 20
COL = ORB // NK
TL = COL // 128
PENALTY = 4.0


def swap_cores(x):
    return lax.ppermute(x, CORE, [(0, 1), (1, 0)])


def exchange(x, axis):
    return lax.all_to_all(x, axis, split_axis=0, concat_axis=0, tiled=True)


def in_hbm(x):
    return pltpu.with_memory_space_constraint(x, pltpu.HBM)


def params(mib):
    return pltpu.CompilerParams(vmem_limit_bytes=mib * 1024 * 1024)


def occupancy_body(energy, kpt, weights, density, volts_out, fixed, gate, own, other, fixed_ends, gate_ends, volts, arrivals):
    step = pl.program_id(0)
    e = energy[0]
    k = kpt[0]
    core = k % 2
    z = chip_order(step, kpt)
    ends = [pltpu.make_async_copy(volts_out, volts, arrivals.at[4])]
    for i, plane in enumerate((0, PLANES - 1)):
        ends.append(pltpu.make_async_copy(fixed.at[plane], fixed_ends.at[i], arrivals.at[2 * i]))
        ends.append(pltpu.make_async_copy(gate.at[plane], gate_ends.at[i], arrivals.at[2 * i + 1]))

    @pl.when(step == 0)
    def _():
        for copy in ends:
            copy.start()

    for half, out in ((0, own), (1, other)):
        which = core if half == 0 else 1 - core
        start = pl.multiple_of(which * COL, 128)
        zero = jnp.zeros((3, 128), jnp.float32)
        for i in range(0, NE, 2):
            total = None
            for n in range(EL):
                weight = jnp.broadcast_to(weights[0:1, n : n + 1], (16, COL))
                part = density[n, 8 * i : 8 * i + 16, pl.ds(start, COL)].astype(jnp.float32) * weight
                total = part if total is None else total + part
            for h in range(2):
                at = i + h
                for t in range(TL):
                    tile = total[8 * h : 8 * h + 8, 128 * t : 128 * (t + 1)]
                    out[at, 0, 8 * t : 8 * t + 8, :] = tile
                    if at + 1 < NE:
                        out[at + 1, 0, 24 + t : 25 + t, :] = tile[7:8]
                    if at > 0:
                        out[at - 1, 0, 27 + t : 28 + t, :] = tile[0:1]
        out[0, 0, 24:27, :] = zero
        out[NE - 1, 0, 27:30, :] = zero
        for i in range(NE):
            out[i, 0, 30:32, :] = zero[:2]

    @pl.when(step == 1)
    def _():
        for copy in ends:
            copy.wait()

    for dx in (-1, 1):
        for dy in (-1, 1):
            to_e = e + dx
            to_k = k + dy

            @pl.when((to_e >= 0) & (to_e < NE) & (to_k >= 0) & (to_k < NK) & (to_k // 2 == z))
            def _(dx=dx, dy=dy, to_e=to_e):
                i = 1 if dx == 1 else 0
                y = CY - 1 if dy == 1 else 0
                g = gate_ends[i, y : y + 1, :].astype(jnp.float32)
                line = fixed_ends[i, y : y + 1, :] + PENALTY * g * volts[(PLANES - 1) * i]
                other[to_e, 0, 30:31, :] = line[:, :128]
                other[to_e, 0, 31:32, :] = line[:, 128:]


def chip_order(step, kpt):
    return (kpt[0] // 2 + 2 + step) % NZC


def occupancy_parts(e, k, volts, weights, density, fixed, gate):
    shape = jax.ShapeDtypeStruct((NE, NZC, 32, 128), jnp.float32)
    block = pl.BlockSpec((NE, 1, 32, 128), lambda i, e, k: (0, chip_order(i, k), 0, 0))
    hbm = pl.BlockSpec(memory_space=pltpu.HBM)
    return pl.pallas_call(
        occupancy_body,
        grid_spec=pltpu.PrefetchScalarGridSpec(
            num_scalar_prefetch=2,
            grid=(NZC,),
            in_specs=[
                pl.BlockSpec((1, EL), lambda z, *_: (0, 0)),
                pl.BlockSpec((EL, LAYERS, 2 * COL), lambda i, e, k: (0, 0, chip_order(i, k))),
                hbm,
                hbm,
                hbm,
            ],
            out_specs=[block, block],
            scratch_shapes=[
                pltpu.VMEM((2, CY, NZ), jnp.float32),
                pltpu.VMEM((2, CY, NZ), jnp.int32),
                pltpu.SMEM((PLANES,), jnp.float32),
                pltpu.SemaphoreType.DMA((5,)),
            ],
        ),
        out_shape=[shape, shape],
        compiler_params=params(8),
        name="occupancy_parts",
    )(e[None], k[None], in_hbm(weights), in_hbm(density), in_hbm(volts), in_hbm(fixed), in_hbm(gate))


def edges_body(energy, volts_out, fixed, gate, cells, xup, xdown, yup, ydown, near, fixed_here, gate_here, volts, arrivals):
    copies = [
        pltpu.make_async_copy(volts_out, volts, arrivals.at[2]),
        pltpu.make_async_copy(fixed, fixed_here, arrivals.at[0]),
        pltpu.make_async_copy(gate, gate_here, arrivals.at[1]),
    ]
    later = []
    for n in range(3):
        start = pl.multiple_of(jnp.clip(energy[0] + n - 1, 0, NE - 1) * LD, LD)
        later.append(
            pltpu.make_async_copy(cells.at[pl.ds(start, LD)], near.at[pl.ds(n * LD, LD)], arrivals.at[3 + n])
        )
    for copy in copies + later:
        copy.start()
    for copy in copies:
        copy.wait()
    for out, planes in ((xup, (PLANES - 2, PLANES - 1)), (xdown, (0, 1))):
        for i, p in enumerate(planes):
            g = gate_here[p].astype(jnp.float32)
            out[i] = fixed_here[p] + PENALTY * g * volts[p]
            if p in (0, PLANES - 1):
                out[2] = g

    def one_plane(p, carry):
        volt = PENALTY * volts[p]
        for out, rows in ((yup, (CY - 2, CY - 1)), (ydown, (0, 1))):
            for i, y in enumerate(rows):
                g = gate_here[p, y : y + 1, :].astype(jnp.float32)
                out[i, pl.ds(p, 1), :] = fixed_here[p, y : y + 1, :] + volt * g
                if y in (0, CY - 1):
                    out[2, pl.ds(p, 1), :] = g
        return carry

    lax.fori_loop(0, PLANES, one_plane, 0, unroll=8)
    for copy in later:
        copy.wait()


def edges(e, volts, fixed, gate, cells):
    shapes = [(3, CY, NZ)] * 2 + [(3, PLANES, NZ)] * 2
    hbm = pl.BlockSpec(memory_space=pltpu.HBM)
    return pl.pallas_call(
        edges_body,
        grid_spec=pltpu.PrefetchScalarGridSpec(
            num_scalar_prefetch=1,
            grid=(1,),
            in_specs=[hbm, hbm, hbm, hbm],
            out_specs=[pl.BlockSpec(x, lambda i, *_: (0, 0, 0)) for x in shapes]
            + [pl.BlockSpec((3 * LD, ORB), lambda i, *_: (0, 0))],
            scratch_shapes=[
                pltpu.VMEM((PLANES, CY, NZ), jnp.float32),
                pltpu.VMEM((PLANES, CY, NZ), jnp.int32),
                pltpu.SMEM((PLANES,), jnp.float32),
                pltpu.SemaphoreType.DMA((6,)),
            ],
        ),
        out_shape=[jax.ShapeDtypeStruct(x, jnp.float32) for x in shapes]
        + [jax.ShapeDtypeStruct((3 * LD, ORB), jnp.int32)],
        compiler_params=params(8),
        name="edges",
    )(e[None], in_hbm(volts), in_hbm(fixed), in_hbm(gate), in_hbm(cells))


def collect_body(energy, kpt, parts, out, corners):
    e = energy[0]
    k = kpt[0]
    total = parts[0]
    for i in range(1, NE * NZC):
        total = total + parts[i]
    for n in range(NK):
        out[n] = total
    for i, dx in enumerate((-1, 1)):
        for j, dy in enumerate((-1, 1)):
            from_e = e + dx
            from_k = k + dy
            there = (from_e >= 0) & (from_e < NE) & (from_k >= 0) & (from_k < NK)
            source = jnp.where(there, from_e * NZC + from_k // 2, 0)
            lines = parts[source, 30:32, :]
            corners[i, j : j + 1, 0:128] = jnp.where(there, lines[0:1], 0.0)
            corners[i, j : j + 1, 128:256] = jnp.where(there, lines[1:2], 0.0)


def collect(e, k, parts):
    whole = lambda shape: pl.BlockSpec(shape, lambda i, *_: (0, 0, 0))
    shapes = [(NK, 32, 128), (2, 2, NZ)]
    return pl.pallas_call(
        collect_body,
        grid_spec=pltpu.PrefetchScalarGridSpec(
            num_scalar_prefetch=2,
            grid=(1,),
            in_specs=[whole((NE * NZC, 32, 128))],
            out_specs=[whole(x) for x in shapes],
        ),
        out_shape=[jax.ShapeDtypeStruct(x, jnp.float32) for x in shapes],
        compiler_params=params(4),
        name="collect",
    )(e[None], k[None], parts)


def split_parts(x):
    high = x.astype(jnp.bfloat16)
    low = (x - high.astype(jnp.float32)).astype(jnp.bfloat16)
    return high, low


def spread(line, rows):
    block = jnp.broadcast_to(line, (16, 128)).astype(jnp.bfloat16)
    return jnp.concatenate([block] * (rows // 16), axis=0)


def counting(rows):
    return lax.broadcasted_iota(jnp.int32, (rows, 128), 0).astype(jnp.float32).astype(jnp.bfloat16)


def tiles_of(line):
    return [line[:, 128 * t : 128 * (t + 1)] for t in range(line.shape[1] // 128)]


def marks(index, rows, counts):
    one = jnp.ones((), jnp.bfloat16)
    zero = jnp.zeros((), jnp.bfloat16)
    return jnp.concatenate([jnp.where(counts[:rows] == spread(t, rows), one, zero) for t in tiles_of(index)], axis=1)


def charge_of(cells, values, first_plane, planes, y0):
    plane = (cells >> 15) - first_plane
    dy = ((cells >> 8) & (NY - 1)) - y0
    near = (dy >= -2) & (dy < CY + 2) & (plane >= 0) & (plane < planes)
    row = jnp.where(near, plane * WC + jnp.where(dy >= 0, dy, dy + WC), -1).astype(jnp.float32)
    z = (cells & (NZ - 1)).astype(jnp.float32)
    rows = planes * WC
    padded = -(-rows // 16) * 16
    counts = counting(NZ)
    high = values.astype(jnp.bfloat16).astype(jnp.float32)
    low = values - high
    zero = jnp.zeros((), jnp.bfloat16)
    tops, bottoms = [], []
    for t, h, l in zip(tiles_of(row), tiles_of(high), tiles_of(low)):
        hit = counts[:padded] == spread(t, padded)
        tops.append(jnp.where(hit, spread(h, padded), zero))
        bottoms.append(jnp.where(hit, spread(l, padded), zero))
    left = jnp.concatenate([jnp.concatenate(tops, axis=1), jnp.concatenate(bottoms, axis=1)], axis=0)
    right = marks(z, NZ, counts)
    both = lax.dot_general(left, right, (((1,), (1,)), ((), ())), preferred_element_type=jnp.float32)
    return both[:padded] + both[padded:]


def in_plane(here):
    lane = lax.broadcasted_iota(jnp.int32, (W, NZ), 1)
    total = pltpu.roll(here, 1, 0) + pltpu.roll(here, W - 1, 0)
    total = total + jnp.where(lane == 0, 0.0, pltpu.roll(here, 1, 1))
    return total + jnp.where(lane == NZ - 1, 0.0, pltpu.roll(here, NZ - 1, 1))


def field_body(energy, kpt, occ, cells, corners, xlow, xhigh, ylow, yhigh, volts_out, fixed, gate,
               sums, fields_out, r_ext, g_ext, fixed_here, gate_here, volts, arrivals):
    e = energy[0]
    k = kpt[0]
    y0 = k * CY
    copies = [
        pltpu.make_async_copy(volts_out, volts, arrivals.at[2]),
        pltpu.make_async_copy(fixed, fixed_here, arrivals.at[0]),
        pltpu.make_async_copy(gate, gate_here, arrivals.at[1]),
    ]
    for copy in copies:
        copy.start()
    row = lax.broadcasted_iota(jnp.int32, (W, NZ), 0)
    y = jnp.where(row < CY + 4, row, row - W) + y0
    valid = jnp.where((y >= 0) & (y < NY), 1.0, 0.0)

    def values_of(index):
        return jnp.concatenate(
            [occ[c, pl.ds(index(t), 1), :] for c in range(NK) for t in range(TL)], axis=1
        )

    gap = jnp.zeros((4, NZ), jnp.float32)

    def keep(charge, planes, at):
        for p in range(planes):
            r_ext[at + p, 0:CY, :] = -charge[WC * p : WC * p + CY]
            r_ext[at + p, CY : CY + 2, :] = -charge[WC * p + CY : WC * p + CY + 2]
            r_ext[at + p, CY + 2 : W - 2, :] = gap
            r_ext[at + p, W - 2 : W, :] = -charge[WC * p + CY + 2 : WC * p + WC]

    for j in range(LD):
        charge = charge_of(cells[LD + j : LD + j + 1, :], values_of(lambda t: 8 * t + j), 0, SUB, y0)
        keep(charge, SUB, 2 + SUB * j)
    keep(charge_of(cells[LD - 1 : LD, :], values_of(lambda t: 24 + t), SUB - 2, 2, y0), 2, 0)
    keep(charge_of(cells[2 * LD : 2 * LD + 1, :], values_of(lambda t: 27 + t), 0, 2, y0), 2, PLANES + 2)

    for at, halo in ((0, xlow), (PLANES + 2, xhigh)):
        for i in range(2):
            r_ext[at + i, 0:CY, :] = r_ext[at + i, 0:CY, :] + halo[i]
    g_ext[1, 0:CY, :] = xlow[2]
    g_ext[PLANES + 2, 0:CY, :] = xhigh[2]
    sub = lax.broadcasted_iota(jnp.int32, (8, NZ), 0)
    none = jnp.zeros((8, NZ), jnp.float32)
    line = lambda x: jnp.broadcast_to(x, (8, NZ))
    for at, i in ((1, 0), (PLANES + 2, 1)):
        tile = jnp.where(sub == 0, line(corners[i, 1:2, :]), jnp.where(sub == 7, line(corners[i, 0:1, :]), none))
        r_ext[at, CY:W, :] = r_ext[at, CY:W, :] + tile
        g_ext[at, CY:W, :] = none
    for copy in copies:
        copy.wait()

    def load_plane(p, carry):
        at = pl.ds(p, 1)
        g = gate_here[p].astype(jnp.float32)
        g_ext[p + 2, 0:CY, :] = g
        r_ext[p + 2, 0:CY, :] = r_ext[p + 2, 0:CY, :] + (fixed_here[p] + PENALTY * g * volts[p])
        tile = jnp.where(sub == 0, line(yhigh[0, at, :]), jnp.where(sub == 1, line(yhigh[1, at, :]), none))
        tile = jnp.where(sub == 6, line(ylow[0, at, :]), jnp.where(sub == 7, line(ylow[1, at, :]), tile))
        r_ext[p + 2, CY:W, :] = r_ext[p + 2, CY:W, :] + tile
        tile = jnp.where(sub == 0, line(yhigh[2, at, :]), jnp.where(sub == 7, line(ylow[2, at, :]), none))
        g_ext[p + 2, CY:W, :] = tile
        return carry

    lax.fori_loop(0, PLANES, load_plane, 0, unroll=8)

    def image_plane(p):
        here = r_ext[p + 1]
        x = e * PLANES + p - 1
        inside = jnp.where((x >= 0) & (x < NE * PLANES), 1.0, 0.0)
        around = r_ext[p + 2] + r_ext[p] + in_plane(here)
        return ((6.0 + PENALTY * g_ext[p + 1]) * here - around) * (valid * inside)

    def sum_plane(p, carry):
        before, here, rr, rw, ww, waw = carry
        after = image_plane(p + 2)
        r = r_ext[p + 2, 0:CY, :]
        w = here[0:CY]
        image = ((6.0 + PENALTY * g_ext[p + 2]) * here - (before + after + in_plane(here)))[0:CY]
        fields_out[0, p] = r
        fields_out[1, p] = w
        return here, after, rr + r * r, rw + r * w, ww + w * w, waw + w * image

    zero = jnp.zeros((CY, NZ), jnp.float32)
    totals = lax.fori_loop(0, PLANES, sum_plane, (image_plane(0), image_plane(1)) + (zero,) * 4, unroll=8)[2:]
    lane = lax.broadcasted_iota(jnp.int32, (1, 128), 1)
    line = jnp.zeros((1, 128), jnp.float32)
    for i, total in enumerate(totals):
        line = line + jnp.where(lane == i, jnp.sum(total), 0.0)
    for d in range(NE * NK):
        sums[d] = line


def fields(e, k, volts, occ, cells, corners, fixed, gate, xlow, xhigh, ylow, yhigh):
    whole = lambda x: pl.BlockSpec(x.shape, lambda i, *_: (0,) * x.ndim)
    shapes = [
        jax.ShapeDtypeStruct((NE * NK, 1, 128), jnp.float32),
        jax.ShapeDtypeStruct((2, PLANES, CY, NZ), jnp.float32),
    ]
    return pl.pallas_call(
        field_body,
        grid_spec=pltpu.PrefetchScalarGridSpec(
            num_scalar_prefetch=2,
            grid=(1,),
            in_specs=[whole(x) for x in (occ, cells, corners, xlow, xhigh, ylow, yhigh)]
            + [pl.BlockSpec(memory_space=pltpu.HBM)] * 3,
            out_specs=[
                pl.BlockSpec((NE * NK, 1, 128), lambda i, *_: (0, 0, 0)),
                pl.BlockSpec((2, PLANES, CY, NZ), lambda i, *_: (0, 0, 0, 0)),
            ],
            scratch_shapes=[
                pltpu.VMEM((PLANES + 4, W, NZ), jnp.float32),
                pltpu.VMEM((PLANES + 4, W, NZ), jnp.float32),
                pltpu.VMEM((PLANES, CY, NZ), jnp.float32),
                pltpu.VMEM((PLANES, CY, NZ), jnp.int32),
                pltpu.SMEM((PLANES,), jnp.float32),
                pltpu.SemaphoreType.DMA((3,)),
            ],
        ),
        out_shape=shapes,
        compiler_params=params(16),
        name="fields",
    )(e[None], k[None], occ, cells, corners, xlow, xhigh, ylow, yhigh, in_hbm(volts), in_hbm(fixed), in_hbm(gate))


def lengths(sums):
    line = jnp.sum(sums[...].reshape(NE * NK, 128), axis=0, keepdims=True)
    lane = lax.broadcasted_iota(jnp.int32, (1, 128), 1)
    rr, rw, ww, waw = [
        jnp.broadcast_to(jnp.sum(jnp.where(lane == i, line, 0.0), axis=1, keepdims=True), (1, NZ)) for i in range(4)
    ]
    alpha = rr / rw
    norm = alpha * alpha * ww - rr
    ratio = norm / rr
    ahead = 1.0 + ratio
    curve = ahead * ahead * rw - 2.0 * ahead * alpha * ww + alpha * alpha * waw
    small = (norm <= 1e-9 * rr) | (curve <= 0.0)
    step = jnp.where(small, alpha, norm / curve)
    ahead = jnp.where(small, 1.0, ahead)
    return alpha + step * ahead, -alpha * step


def pick_body(kpt, sums, cells_near, rw, out, grid_out, grid_here, leaving):
    y0 = kpt[0] * CY
    wide = 2 * COL
    counts = counting(NZ)
    c_r, c_w = [jnp.broadcast_to(c, (SUB * CY, NZ)) for c in lengths(sums)]
    copies = []
    for j in range(LD):
        at = pl.ds(SUB * j, SUB)
        field = c_r * rw[0, at].reshape(SUB * CY, NZ) + c_w * rw[1, at].reshape(SUB * CY, NZ)
        grid_here[at] = field.reshape(SUB, CY, NZ)
        copies.append(pltpu.make_async_copy(grid_here.at[at], grid_out.at[at], leaving.at[j]))
        copies[-1].start()
        high, low = split_parts(field)
        for n in range(ORB // wide):
            cells = cells_near[LD + j : LD + j + 1, n * wide : (n + 1) * wide]
            dy = ((cells >> 8) & (NY - 1)) - y0
            row = jnp.where((dy >= 0) & (dy < CY), (cells >> 15) * CY + dy, -1)
            z = cells & (NZ - 1)
            right = marks(z.astype(jnp.float32), NZ, counts)
            lines = jnp.dot(high, right, preferred_element_type=jnp.float32)
            lines = lines + jnp.dot(low, right, preferred_element_type=jnp.float32)
            hit = lax.broadcasted_iota(jnp.int32, (SUB * CY, wide), 0) == row
            value = jnp.sum(jnp.where(hit, lines, 0.0), axis=0, keepdims=True)
            for h in range(2):
                out[2 * n + h, j : j + 1, :] = value[:, h * COL : (h + 1) * COL]
    for copy in copies:
        copy.wait()


def pick(k, sums, cells, rw):
    whole = lambda shape: pl.BlockSpec(shape, lambda i, *_: (0,) * len(shape))
    shape = jax.ShapeDtypeStruct((NK, LD, COL), jnp.float32)
    return pl.pallas_call(
        pick_body,
        grid_spec=pltpu.PrefetchScalarGridSpec(
            num_scalar_prefetch=1,
            grid=(1,),
            in_specs=[whole(sums.shape), whole(cells.shape), whole(rw.shape)],
            out_specs=[whole(shape.shape), pl.BlockSpec(memory_space=pltpu.HBM)],
            scratch_shapes=[pltpu.VMEM((PLANES, CY, NZ), jnp.float32), pltpu.SemaphoreType.DMA((LD,))],
        ),
        out_shape=[shape, pltpu.HBM((PLANES, CY, NZ), jnp.float32)],
        compiler_params=params(12),
        name="pick",
    )(k[None], sums, cells, rw)


def join_body(picked, out):
    total = picked[0]
    for i in range(1, NK):
        total = total + picked[i]
    for d in range(NE * NZC):
        out[d] = total


def join(picked):
    return pl.pallas_call(
        join_body,
        out_shape=jax.ShapeDtypeStruct((NE * NZC, LD, COL), jnp.float32),
        compiler_params=params(4),
        name="join",
    )(picked)


def band_body(which, density, values, before, out, acc):
    z = pl.program_id(0)
    start = pl.multiple_of(which[0] * COL, 128)

    @pl.when(z == 0)
    def _():
        acc[...] = jnp.zeros_like(acc)

    for m in range(0, NE, 2):
        v = values[m : m + 2, 0].reshape(16, COL)
        for i in range(EL):
            part = density[i, 8 * m : 8 * m + 16, pl.ds(start, COL)].astype(jnp.float32) * v
            total = part[:, :128]
            for t in range(1, TL):
                total = total + part[:, 128 * t : 128 * (t + 1)]
            acc[i, 8 * m : 8 * m + 16] = acc[i, 8 * m : 8 * m + 16] + total

    @pl.when(z == NZC - 1)
    def _():
        for i in range(EL):
            out[i : i + 1, :] = before[i : i + 1, :] + jnp.sum(acc[i].T, axis=0, keepdims=True) * ORB**-0.5


def band(which, density, values, before):
    small = pl.BlockSpec((EL, LAYERS), lambda z, *_: (0, 0))
    return pl.pallas_call(
        band_body,
        grid_spec=pltpu.PrefetchScalarGridSpec(
            num_scalar_prefetch=1,
            grid=(NZC,),
            in_specs=[
                pl.BlockSpec((EL, LAYERS, 2 * COL), lambda z, *_: (0, 0, z)),
                pl.BlockSpec((NE, 1, LD, COL), lambda z, *_: (0, z, 0, 0)),
                small,
            ],
            out_specs=small,
            scratch_shapes=[pltpu.VMEM((EL, LAYERS, 128), jnp.float32)],
        ),
        out_shape=jax.ShapeDtypeStruct((EL, LAYERS), jnp.float32),
        compiler_params=params(8),
        name="band",
    )(which, density, values, before)


def shift_up(x, axis):
    return lax.ppermute(x, axis, [(i, i + 1) for i in range(lax.axis_size(axis) - 1)])


def shift_down(x, axis):
    return lax.ppermute(x, axis, [(i + 1, i) for i in range(lax.axis_size(axis) - 1)])


def one_step(density, quad_weights, orbital_cells, fixed_charge, gate_mask, gate_voltage):
    e = lax.axis_index(ENERGY).astype(jnp.int32)
    k = lax.axis_index(KPT).astype(jnp.int32)
    core = lax.axis_index(CORE).astype(jnp.int32)[None]
    density = density.reshape(EL, LAYERS, ORB)

    own, other = occupancy_parts(e, k, gate_voltage, quad_weights.reshape(1, EL), density, fixed_charge, gate_mask)
    chips = NE * NZC
    received = swap_cores(other.reshape(chips, 32, 128))
    xup, xdown, yup, ydown, cells = edges(e, gate_voltage, fixed_charge, gate_mask, orbital_cells)
    pair = own.reshape(chips, 32, 128) + received
    parts = exchange(pair, CHIPS)
    xlow = shift_up(xup, ENERGY)
    xhigh = shift_down(xdown, ENERGY)
    ylow = shift_up(yup, KPT)
    yhigh = shift_down(ydown, KPT)
    parts, xlow, xhigh = lax.optimization_barrier((parts, xlow, xhigh))
    occ, corners = collect(e, k, parts)
    occ = exchange(occ, KPT)
    sums, rw = fields(
        e, k, gate_voltage, occ, cells, corners, fixed_charge, gate_mask, xlow, xhigh, ylow, yhigh
    )
    all_sums = exchange(sums, EVERY)
    picked, potential = pick(k, all_sums, cells, rw)
    picked = exchange(picked, KPT)
    same = exchange(join(picked), CHIPS)
    shape = (NE, NZC, LD, COL)
    cross = swap_cores(same)
    shift = band(core, density, same.reshape(shape), jnp.zeros((EL, LAYERS), jnp.float32))
    shift = band(1 - core, density, cross.reshape(shape), shift)
    return potential, shift.reshape(EL, 1, LAYERS)


def solution(mesh):
    split = Mesh(mesh.devices.reshape(4, 4, 4, 2), ("energy_0", "energy_1", "kpt_0", "kpt_1"))
    in_specs = (
        P(ENERGY, KPT, None, None),
        P(ENERGY, KPT),
        P(),
        P(ENERGY, KPT, None),
        P(ENERGY, KPT, None),
        P(ENERGY),
    )
    out_specs = (P(ENERGY, KPT, None), P(ENERGY, KPT, None))
    return jax.shard_map(one_step, mesh=split, in_specs=in_specs, out_specs=out_specs, check_vma=False)
```

time: 121 us -> 114 us (0.942)
  Pallas kernels: 33.5 us -> 21.9 us
  blocking collectives: 35.1 us -> 46.1 us
  starting transfers between devices: 27.3 us -> 22.6 us
  waiting for transfers between devices: 21.8 us -> 19.9 us
    all_to_all x2 -> x3, blocking collectives: 35.1 us -> 46.1 us  [exchange(): return lax.all_to_all(x, axis, split_axis=0, concat_axis=0, tiled=True)]
    pallas_call x1, Pallas kernels: 9.79 us -> 3.96 us  [pick(): pl.pallas_call(pick_body, grid_spec=pltpu.PrefetchScalarGridSpec(num_scal...]
    all_to_all x3 -> x2, starting transfers between devices: 19.8 us -> 14.9 us  [exchange(): return lax.all_to_all(x, axis, split_axis=0, concat_axis=0, tiled=True)]
    pallas_call x1, Pallas kernels: 12.5 us -> 9.13 us  [fields(): pl.pallas_call(field_body, grid_spec=pltpu.PrefetchScalarGridSpec(num_sca...]
    ppermute x2, waiting for transfers between devices: 4.89 us -> 2.71 us  [shift_up(): lax.ppermute(x, axis, [(i, i + 1) for i in range(lax.axis_size(axis) - 1)])]
    pallas_call x1, Pallas kernels: 5.72 us -> 3.73 us  [occupancy_parts(): pl.pallas_call(occupancy_body, grid_spec=pltpu.PrefetchScalarGridSpec(num...]
    all_to_all x3 -> x2, waiting for transfers between devices: 11.4 us -> 11.2 us  [exchange(): return lax.all_to_all(x, axis, split_axis=0, concat_axis=0, tiled=True)]
  transfers between devices with their start and end apart: 9 -> 8, of which waited for: 6 -> 6; matrix products, arithmetic and copies ran while one was open for 0% -> 0% of each run, Pallas kernels for 10% -> 3%
where the time goes in v3:
time: 114 us; the launch traced here: 112 us
  blocking collectives  46.1 us (40%)
  starting transfers between devices  22.6 us (20%)
  Pallas kernels  21.9 us (19%)
  waiting for transfers between devices  19.9 us (17%)
  other arithmetic  1.19 us (1%)
    all_to_all x3, blocking collectives, exchange(): return lax.all_to_all(x, axis, split_axis=0, concat_axis=0, tiled=True)  46.1 us
    all_to_all x2, starting transfers between devices, exchange(): return lax.all_to_all(x, axis, split_axis=0, concat_axis=0, tiled=True)  14.9 us
    all_to_all x2, waiting for transfers between devices, exchange(): return lax.all_to_all(x, axis, split_axis=0, concat_axis=0, tiled=True)  11.2 us
    pallas_call x1, Pallas kernels, fields(): pl.pallas_call(field_body, grid_spec=pltpu.PrefetchScalarGridSpec(num_sca...  9.13 us
    ppermute x2, starting transfers between devices, shift_up(): lax.ppermute(x, axis, [(i, i + 1) for i in range(lax.axis_size(axis) - 1)])  4.97 us
    ppermute x2, waiting for transfers between devices, swap_cores(): return lax.ppermute(x, CORE, [(0, 1), (1, 0)])  4.05 us
    pallas_call x1, Pallas kernels, pick(): pl.pallas_call(pick_body, grid_spec=pltpu.PrefetchScalarGridSpec(num_scal...  3.96 us
    pallas_call x1, Pallas kernels, occupancy_parts(): pl.pallas_call(occupancy_body, grid_spec=pltpu.PrefetchScalarGridSpec(num...  3.73 us
  transfers between devices with their start and end apart: 8, of which 6 were waited for; matrix products, arithmetic and copies ran while one was open for 0% of the time, Pallas kernels for 3%

profile of v3, /device:TPU:0, one launch (start us, length us, event | category | flops | bytes accessed | tf_op | source)
XLA Modules:
  0.0 112.4 jit_solution(8379527021249130447)
XLA Ops:
  0.6 3.7 %occupancy_parts.1 = (f32[16,4,32,128]{3,2,1,0:T(8,128)S(1)}, f32[16,4,32,128]{3,2,1,0:T(8,128)S(1)}) custom-call(s32[1]{0:T(128)} %bitcast.1.energy, s32[1]{0:T(128)} %bitcast.kpt, f32[1,4]{1,0:T(1,128)} %bitcast.20, bf16[4,128,3072]{2,1,0:T(8,128)(2,1)} %bitcast.13, f32[64]{0:T(128)} %volts_out.5, f32[64,16,256]{2,1,0:T(8,128)} %fixed.5, s32[64,16,256]{2,1,0:T(8,128)} %gate.5), custom_call_target="tpu_custom_call" | custom-call | tf_op jit(solution)/shard_map/occupancy_parts/pallas_call | solution.py:118
  4.4 0.1 collective-permute-start
  4.5 2.6 %collective-permute-done = f32[64,32,128]{2,1,0:T(8,128)S(1)} collective-permute-done((f32[64,32,128]{2,1,0:T(8,128)S(1)}, f32[64,32,128]{2,1,0:T(8,128)S(1)}, u32[]{:S(2)}, u32[]{:S(2)}) %collective-permute-start) | collective-permute-done | bytes 1048608 | tf_op jit(solution)/shard_map/ppermute | solution.py:35
  7.1 1.2 %bitcast_add_fusion = f32[64,32,128]{2,1,0:T(8,128)} fusion(f32[64,32,128]{2,1,0:T(8,128)S(1)} %collective-permute-done, f32[16,4,32,128]{3,2,1,0:T(8,128)S(1)} %get-tuple-element.18), kind=kLoop, calls=%fused_computation | loop fusion | flops 262144 | bytes 3145728 | tf_op jit(solution)/shard_map/add | solution.py:565
  8.3 11.5 %all-to-all-start = ((f32[64,32,128]{2,1,0:T(8,128)}), f32[64,32,128]{2,1,0:T(8,128)S(1)}, u32[]{:S(2)}, u32[]{:S(2)}) async-start(f32[64,32,128]{2,1,0:T(8,128)} %bitcast_add_fusion), calls=%async_computation | async-start | bytes 2097152 | tf_op jit(solution)/shard_map/all_to_all | solution.py:39
  19.9 2.0 %edges.1 = (f32[3,16,256]{2,1,0:T(8,128)S(1)}, f32[3,16,256]{2,1,0:T(8,128)S(1)}, f32[3,64,256]{2,1,0:T(8,128)S(1)}, f32[3,64,256]{2,1,0:T(8,128)S(1)}, s32[24,3072]{1,0:T(8,128)S(1)}) custom-call(s32[1]{0:T(128)} %bitcast.1.energy, f32[64]{0:T(128)} %volts_out.5, f32[64,16,256]{2,1,0:T(8,128)} %fixed.5, s32[64,16,256]{2,1,0:T(8,128)} %gate.5, s32[128,3072]{1,0:T(8,128)} %cells.1), custom_call_target="tpu_custom_call" | custom-call | tf_op jit(solution)/shard_map/edges/pallas_call | solution.py:185
  21.8 1.8 %collective-permute-start.3 = (f32[3,64,256]{2,1,0:T(8,128)S(1)}, f32[3,64,256]{2,1,0:T(8,128)S(1)}, u32[]{:S(2)}, u32[]{:S(2)}) collective-permute-start(f32[3,64,256]{2,1,0:T(8,128)S(1)} %get-tuple-element.28), channel_id=1, source_target_pairs={{0,1},{1,2},{2,3},{3,4},{4,5},{5,6},{6,7},{8,9},{9,10},{10,11},{11... | collective-permute-start | bytes 589832 | tf_op jit(solution)/shard_map/ppermute | solution.py:548
  23.6 1.3 %collective-permute-start.4 = (f32[3,64,256]{2,1,0:T(8,128)S(1)}, f32[3,64,256]{2,1,0:T(8,128)S(1)}, u32[]{:S(2)}, u32[]{:S(2)}) collective-permute-start(f32[3,64,256]{2,1,0:T(8,128)S(1)} %get-tuple-element.29), channel_id=1, source_target_pairs={{1,0},{2,1},{3,2},{4,3},{5,4},{6,5},{7,6},{9,8},{10,9},{11,10},{12... | collective-permute-start | bytes 589832 | tf_op jit(solution)/shard_map/ppermute | solution.py:552
  24.9 3.2 %collective-permute-start.1 = (f32[3,16,256]{2,1,0:T(8,128)S(1)}, f32[3,16,256]{2,1,0:T(8,128)S(1)}, u32[]{:S(2)}, u32[]{:S(2)}) collective-permute-start(f32[3,16,256]{2,1,0:T(8,128)S(1)} %get-tuple-element.20), channel_id=1, source_target_pairs={{0,8},{8,16},{16,24},{24,32},{32,40},{40,48},{48,56},{56,64},{64,7... | collective-permute-start | bytes 147464 | tf_op jit(solution)/shard_map/ppermute | solution.py:548
  28.1 1.3 %collective-permute-start.2 = (f32[3,16,256]{2,1,0:T(8,128)S(1)}, f32[3,16,256]{2,1,0:T(8,128)S(1)}, u32[]{:S(2)}, u32[]{:S(2)}) collective-permute-start(f32[3,16,256]{2,1,0:T(8,128)S(1)} %get-tuple-element.21), channel_id=1, source_target_pairs={{8,0},{16,8},{24,16},{32,24},{40,32},{48,40},{56,48},{64,56},{72,6... | collective-permute-start | bytes 147464 | tf_op jit(solution)/shard_map/ppermute | solution.py:552
  29.4 2.7 %collective-permute-done.1.xlow = f32[3,16,256]{2,1,0:T(8,128)S(1)} collective-permute-done((f32[3,16,256]{2,1,0:T(8,128)S(1)}, f32[3,16,256]{2,1,0:T(8,128)S(1)}, u32[]{:S(2)}, u32[]{:S(2)}) %collective-permute-start.1) | collective-permute-done | bytes 49184 | tf_op jit(solution)/shard_map/ppermute | solution.py:548
  32.1 2.0 %collective-permute-done.2.xhigh = f32[3,16,256]{2,1,0:T(8,128)S(1)} collective-permute-done((f32[3,16,256]{2,1,0:T(8,128)S(1)}, f32[3,16,256]{2,1,0:T(8,128)S(1)}, u32[]{:S(2)}, u32[]{:S(2)}) %collective-permute-start.2) | collective-permute-done | bytes 49184 | tf_op jit(solution)/shard_map/ppermute | solution.py:552
  34.1 5.2 %all-to-all-done.parts = f32[64,32,128]{2,1,0:T(8,128)S(1)} async-done(((f32[64,32,128]{2,1,0:T(8,128)}), f32[64,32,128]{2,1,0:T(8,128)S(1)}, u32[]{:S(2)}, u32[]{:S(2)}) %all-to-all-start) | async-done | bytes 1048608 | tf_op jit(solution)/shard_map/all_to_all | solution.py:39
  39.3 0.8 collect.1
  40.0 3.4 %all-to-all-start.1 = ((f32[8,32,128]{2,1,0:T(8,128)}), f32[8,32,128]{2,1,0:T(8,128)S(1)}, u32[]{:S(2)}, u32[]{:S(2)}) async-start(f32[8,32,128]{2,1,0:T(8,128)} %get-tuple-element.23), calls=%async_computation.1 | async-start | bytes 262144 | tf_op jit(solution)/shard_map/all_to_all | solution.py:39
  43.4 0.0 collective-permute-done.3.ylow
  43.4 0.0 collective-permute-done.4.yhigh
  43.4 6.0 %all-to-all-done.1.occ = f32[8,32,128]{2,1,0:T(8,128)S(1)} async-done(((f32[8,32,128]{2,1,0:T(8,128)}), f32[8,32,128]{2,1,0:T(8,128)S(1)}, u32[]{:S(2)}, u32[]{:S(2)}) %all-to-all-start.1) | async-done | bytes 131104 | tf_op jit(solution)/shard_map/all_to_all | solution.py:39
  49.4 9.1 %fields.1 = (f32[128,1,128]{2,1,0:T(1,128)S(1)}, f32[2,64,16,256]{3,2,1,0:T(8,128)S(1)}) custom-call(s32[1]{0:T(128)} %bitcast.1.energy, s32[1]{0:T(128)} %bitcast.kpt, f32[8,32,128]{2,1,0:T(8,128)S(1)} %all-to-all-done.1.occ, s32[24,3072]{1,0:T(8,128)S(1)} %get-tuple-element.24.cells.cells_near, f32[2,2,256]{2,1,0:T(2,128)S(1)} %get-tuple-element.25.corners, ...), custom_call_target="tpu_custom_call" | custom-call | tf_op jit(solution)/shard_map/fields/pallas_call | solution.py:396
  58.6 17.5 %all_to_all.25.sums = f32[128,1,128]{2,1,0:T(1,128)S(1)} all-to-all(f32[128,1,128]{2,1,0:T(1,128)S(1)} %get-tuple-element.30), channel_id=1, replica_groups=mesh['energy_0'=4,'energy_1'=4,'kpt_0'=4,'kpt_1'=2] {'energy_0','energy_..., dimensions={0} | all-to-all | bytes 131072 | tf_op jit(solution)/shard_map/all_to_all | solution.py:39
  76.1 0.0 copy-start
  76.1 4.0 %pick.1 = (f32[8,8,384]{2,1,0:T(8,128)S(1)}, f32[64,16,256]{2,1,0:T(8,128)}) custom-call(s32[1]{0:T(128)} %bitcast.kpt, f32[128,1,128]{2,1,0:T(1,128)S(1)} %all_to_all.25.sums, s32[24,3072]{1,0:T(8,128)S(1)} %get-tuple-element.24.cells.cells_near, f32[2,64,16,256]{3,2,1,0:T(8,128)S(1)} %get-tuple-element.31.rw), custom_call_target="tpu_custom_call" | custom-call | tf_op jit(solution)/shard_map/pick/pallas_call | solution.py:471
  80.1 8.2 %all_to_all.26.picked = f32[8,8,384]{2,1,0:T(8,128)S(1)} all-to-all(f32[8,8,384]{2,1,0:T(8,128)S(1)} %get-tuple-element.33), channel_id=1, replica_groups=mesh['energy_0'=4,'energy_1'=4,'kpt_0'=4,'kpt_1'=2] {'kpt_0','kpt_1'}, dimensions={0} | all-to-all | bytes 196608 | tf_op jit(solution)/shard_map/all_to_all | solution.py:39
  88.3 0.1 join.1
  88.3 20.4 %all_to_all.27 = f32[64,8,384]{2,1,0:T(8,128)S(1)} all-to-all(f32[64,8,384]{2,1,0:T(8,128)S(1)} %join.1), channel_id=1, replica_groups=mesh['energy_0'=4,'energy_1'=4,'kpt_0'=4,'kpt_1'=2] {'energy_0','energy_..., dimensions={0} | all-to-all | bytes 1572864 | tf_op jit(solution)/shard_map/all_to_all | solution.py:39
  108.7 0.0 collective-permute-start.5
  108.7 0.0 copy-done
  108.7 0.9 band.2.before
  109.6 1.4 %collective-permute-done.5 = f32[64,8,384]{2,1,0:T(8,128)S(1)} collective-permute-done((f32[64,8,384]{2,1,0:T(8,128)S(1)}, f32[64,8,384]{2,1,0:T(8,128)S(1)}, u32[]{:S(2)}, u32[]{:S(2)}) %collective-permute-start.5) | collective-permute-done | bytes 786464 | tf_op jit(solution)/shard_map/ppermute | solution.py:35
  111.0 1.4 %band.3 = f32[4,128]{1,0:T(4,128)} custom-call(s32[1]{0:T(128)S(6)} %sub.3.which, bf16[4,128,3072]{2,1,0:T(8,128)(2,1)S(1)} %bitcast.15, f32[16,4,8,384]{3,2,1,0:T(8,128)S(1)} %bitcast.17, f32[4,128]{1,0:T(4,128)S(1)} %band.2.before), custom_call_target="tpu_custom_call" | custom-call | tf_op jit(solution)/shard_map/band/pallas_call | solution.py:528
  (1 shorter events, 0.0 us)
Async XLA Ops:
  4.4 2.7 %collective-permute-start = (f32[64,32,128]{2,1,0:T(8,128)S(1)}, f32[64,32,128]{2,1,0:T(8,128)S(1)}, u32[]{:S(2)}, u32[]{:S(2)}) collective-permute-start(f32[64,32,128]{2,1,0:T(8,128)S(1)} %bitcast.18), channel_id=1, source_target_pairs={{0,1},{1,0},{2,3},{3,2},{4,5},{5,4},{6,7},{7,6},{8,9},{9,8},{10,11... | collective-permute-start | bytes 3145736 | tf_op jit(solution)/shard_map/ppermute | solution.py:35
  8.3 31.0 %all-to-all-start = ((f32[64,32,128]{2,1,0:T(8,128)}), f32[64,32,128]{2,1,0:T(8,128)S(1)}, u32[]{:S(2)}, u32[]{:S(2)}) async-start(f32[64,32,128]{2,1,0:T(8,128)} %bitcast_add_fusion), calls=%async_computation | async-start | bytes 2097152 | tf_op jit(solution)/shard_map/all_to_all | solution.py:39
  21.8 21.6 %collective-permute-start.3 = (f32[3,64,256]{2,1,0:T(8,128)S(1)}, f32[3,64,256]{2,1,0:T(8,128)S(1)}, u32[]{:S(2)}, u32[]{:S(2)}) collective-permute-start(f32[3,64,256]{2,1,0:T(8,128)S(1)} %get-tuple-element.28), channel_id=1, source_target_pairs={{0,1},{1,2},{2,3},{3,4},{4,5},{5,6},{6,7},{8,9},{9,10},{10,11},{11... | collective-permute-start | bytes 589832 | tf_op jit(solution)/shard_map/ppermute | solution.py:548
  23.6 19.8 %collective-permute-start.4 = (f32[3,64,256]{2,1,0:T(8,128)S(1)}, f32[3,64,256]{2,1,0:T(8,128)S(1)}, u32[]{:S(2)}, u32[]{:S(2)}) collective-permute-start(f32[3,64,256]{2,1,0:T(8,128)S(1)} %get-tuple-element.29), channel_id=1, source_target_pairs={{1,0},{2,1},{3,2},{4,3},{5,4},{6,5},{7,6},{9,8},{10,9},{11,10},{12... | collective-permute-start | bytes 589832 | tf_op jit(solution)/shard_map/ppermute | solution.py:552
  24.9 7.2 %collective-permute-start.1 = (f32[3,16,256]{2,1,0:T(8,128)S(1)}, f32[3,16,256]{2,1,0:T(8,128)S(1)}, u32[]{:S(2)}, u32[]{:S(2)}) collective-permute-start(f32[3,16,256]{2,1,0:T(8,128)S(1)} %get-tuple-element.20), channel_id=1, source_target_pairs={{0,8},{8,16},{16,24},{24,32},{32,40},{40,48},{48,56},{56,64},{64,7... | collective-permute-start | bytes 147464 | tf_op jit(solution)/shard_map/ppermute | solution.py:548
  28.1 6.0 %collective-permute-start.2 = (f32[3,16,256]{2,1,0:T(8,128)S(1)}, f32[3,16,256]{2,1,0:T(8,128)S(1)}, u32[]{:S(2)}, u32[]{:S(2)}) collective-permute-start(f32[3,16,256]{2,1,0:T(8,128)S(1)} %get-tuple-element.21), channel_id=1, source_target_pairs={{8,0},{16,8},{24,16},{32,24},{40,32},{48,40},{56,48},{64,56},{72,6... | collective-permute-start | bytes 147464 | tf_op jit(solution)/shard_map/ppermute | solution.py:552
  40.0 9.4 %all-to-all-start.1 = ((f32[8,32,128]{2,1,0:T(8,128)}), f32[8,32,128]{2,1,0:T(8,128)S(1)}, u32[]{:S(2)}, u32[]{:S(2)}) async-start(f32[8,32,128]{2,1,0:T(8,128)} %get-tuple-element.23), calls=%async_computation.1 | async-start | bytes 262144 | tf_op jit(solution)/shard_map/all_to_all | solution.py:39
  76.1 32.6 %copy-start = (bf16[4,1,128,3072]{3,2,1,0:T(8,128)(2,1)S(1)}, bf16[4,1,128,3072]{3,2,1,0:T(8,128)(2,1)}, u32[]{:S(2)}) copy-start(bf16[4,1,128,3072]{3,2,1,0:T(8,128)(2,1)} %param.6) | copy-start | bytes 9437188
  108.7 2.3 %collective-permute-start.5 = (f32[64,8,384]{2,1,0:T(8,128)S(1)}, f32[64,8,384]{2,1,0:T(8,128)S(1)}, u32[]{:S(2)}, u32[]{:S(2)}) collective-permute-start(f32[64,8,384]{2,1,0:T(8,128)S(1)} %all_to_all.27), channel_id=1, source_target_pairs={{0,1},{1,0},{2,3},{3,2},{4,5},{5,4},{6,7},{7,6},{8,9},{9,8},{10,11... | collective-permute-start | bytes 2359304 | tf_op jit(solution)/shard_map/ppermute | solution.py:35

commit v4 on v3

--- a/solution.py
+++ b/solution.py
@@ -29,6 +29,7 @@
 COL = ORB // NK
 TL = COL // 128
 PENALTY = 4.0
+AHEAD = 4
 
 
 def swap_cores(x):
@@ -47,96 +48,92 @@
     return pltpu.CompilerParams(vmem_limit_bytes=mib * 1024 * 1024)
 
 
-def occupancy_body(energy, kpt, weights, density, volts_out, fixed, gate, own, other, fixed_ends, gate_ends, volts, arrivals):
-    step = pl.program_id(0)
+def occupancy_body(energy, kpt, weights_out, density_out, volts_out, fixed, gate, own, other,
+                   weights, density, fixed_ends, gate_ends, volts, arrivals, blocks):
     e = energy[0]
     k = kpt[0]
     core = k % 2
-    z = chip_order(step, kpt)
-    ends = [pltpu.make_async_copy(volts_out, volts, arrivals.at[4])]
+    small = [
+        pltpu.make_async_copy(weights_out, weights, arrivals.at[0]),
+        pltpu.make_async_copy(volts_out, volts, arrivals.at[1]),
+    ]
     for i, plane in enumerate((0, PLANES - 1)):
-        ends.append(pltpu.make_async_copy(fixed.at[plane], fixed_ends.at[i], arrivals.at[2 * i]))
-        ends.append(pltpu.make_async_copy(gate.at[plane], gate_ends.at[i], arrivals.at[2 * i + 1]))
-
-    @pl.when(step == 0)
-    def _():
-        for copy in ends:
-            copy.start()
-
-    for half, out in ((0, own), (1, other)):
-        which = core if half == 0 else 1 - core
-        start = pl.multiple_of(which * COL, 128)
-        zero = jnp.zeros((3, 128), jnp.float32)
-        for i in range(0, NE, 2):
-            total = None
-            for n in range(EL):
-                weight = jnp.broadcast_to(weights[0:1, n : n + 1], (16, COL))
-                part = density[n, 8 * i : 8 * i + 16, pl.ds(start, COL)].astype(jnp.float32) * weight
-                total = part if total is None else total + part
-            for h in range(2):
-                at = i + h
-                for t in range(TL):
-                    tile = total[8 * h : 8 * h + 8, 128 * t : 128 * (t + 1)]
-                    out[at, 0, 8 * t : 8 * t + 8, :] = tile
-                    if at + 1 < NE:
-                        out[at + 1, 0, 24 + t : 25 + t, :] = tile[7:8]
-                    if at > 0:
-                        out[at - 1, 0, 27 + t : 28 + t, :] = tile[0:1]
-        out[0, 0, 24:27, :] = zero
-        out[NE - 1, 0, 27:30, :] = zero
-        for i in range(NE):
-            out[i, 0, 30:32, :] = zero[:2]
-
-    @pl.when(step == 1)
-    def _():
-        for copy in ends:
-            copy.wait()
+        small.append(pltpu.make_async_copy(fixed.at[plane], fixed_ends.at[i], arrivals.at[2 + 2 * i]))
+        small.append(pltpu.make_async_copy(gate.at[plane], gate_ends.at[i], arrivals.at[3 + 2 * i]))
+    large = [
+        pltpu.make_async_copy(density_out.at[:, :, pl.ds(2 * COL * z, 2 * COL)], density.at[z], blocks.at[z])
+        for z in range(NZC)
+    ]
+    for copy in small[:1] + large[:AHEAD] + small[1:]:
+        copy.start()
+    small[0].wait()
+    scale = [jnp.broadcast_to(weights[0:1, n : n + 1], (16, COL)) for n in range(EL)]
+    zero = jnp.zeros((3, 128), jnp.float32)
+    for z in range(NZC):
+        large[z].wait()
+        if z + AHEAD < NZC:
+            large[z + AHEAD].start()
+        for half, out in ((0, own), (1, other)):
+            which = core if half == 0 else 1 - core
+            start = pl.multiple_of(which * COL, 128)
+            for i in range(0, NE, 2):
+                total = None
+                for n in range(EL):
+                    part = density[z, n, 8 * i : 8 * i + 16, pl.ds(start, COL)].astype(jnp.float32) * scale[n]
+                    total = part if total is None else total + part
+                for h in range(2):
+                    at = i + h
+                    for t in range(TL):
+                        tile = total[8 * h : 8 * h + 8, 128 * t : 128 * (t + 1)]
+                        out[at, z, 8 * t : 8 * t + 8, :] = tile
+                        if at + 1 < NE:
+                            out[at + 1, z, 24 + t : 25 + t, :] = tile[7:8]
+                        if at > 0:
+                            out[at - 1, z, 27 + t : 28 + t, :] = tile[0:1]
+            out[0, z, 24:27, :] = zero
+            out[NE - 1, z, 27:30, :] = zero
+            for i in range(NE):
+                out[i, z, 30:32, :] = zero[:2]
+    for copy in small[1:]:
+        copy.wait()
 
     for dx in (-1, 1):
         for dy in (-1, 1):
             to_e = e + dx
             to_k = k + dy
 
-            @pl.when((to_e >= 0) & (to_e < NE) & (to_k >= 0) & (to_k < NK) & (to_k // 2 == z))
-            def _(dx=dx, dy=dy, to_e=to_e):
+            @pl.when((to_e >= 0) & (to_e < NE) & (to_k >= 0) & (to_k < NK))
+            def _(dx=dx, dy=dy, to_e=to_e, to_k=to_k):
                 i = 1 if dx == 1 else 0
                 y = CY - 1 if dy == 1 else 0
                 g = gate_ends[i, y : y + 1, :].astype(jnp.float32)
                 line = fixed_ends[i, y : y + 1, :] + PENALTY * g * volts[(PLANES - 1) * i]
-                other[to_e, 0, 30:31, :] = line[:, :128]
-                other[to_e, 0, 31:32, :] = line[:, 128:]
-
-
-def chip_order(step, kpt):
-    return (kpt[0] // 2 + 2 + step) % NZC
+                other[to_e, to_k // 2, 30:31, :] = line[:, :128]
+                other[to_e, to_k // 2, 31:32, :] = line[:, 128:]
 
 
 def occupancy_parts(e, k, volts, weights, density, fixed, gate):
-    shape = jax.ShapeDtypeStruct((NE, NZC, 32, 128), jnp.float32)
-    block = pl.BlockSpec((NE, 1, 32, 128), lambda i, e, k: (0, chip_order(i, k), 0, 0))
+    shape = (NE, NZC, 32, 128)
     hbm = pl.BlockSpec(memory_space=pltpu.HBM)
     return pl.pallas_call(
         occupancy_body,
         grid_spec=pltpu.PrefetchScalarGridSpec(
             num_scalar_prefetch=2,
-            grid=(NZC,),
-            in_specs=[
-                pl.BlockSpec((1, EL), lambda z, *_: (0, 0)),
-                pl.BlockSpec((EL, LAYERS, 2 * COL), lambda i, e, k: (0, 0, chip_order(i, k))),
-                hbm,
-                hbm,
-                hbm,
-            ],
-            out_specs=[block, block],
+            grid=(1,),
+            in_specs=[hbm] * 5,
+            out_specs=[pl.BlockSpec(shape, lambda i, *_: (0, 0, 0, 0))] * 2,
             scratch_shapes=[
+                pltpu.VMEM((1, EL), jnp.float32),
+                pltpu.VMEM((NZC, EL, LAYERS, 2 * COL), jnp.bfloat16),
                 pltpu.VMEM((2, CY, NZ), jnp.float32),
                 pltpu.VMEM((2, CY, NZ), jnp.int32),
                 pltpu.SMEM((PLANES,), jnp.float32),
-                pltpu.SemaphoreType.DMA((5,)),
+                pltpu.SemaphoreType.DMA((6,)),
+                pltpu.SemaphoreType.DMA((NZC,)),
             ],
         ),
-        out_shape=[shape, shape],
-        compiler_params=params(8),
+        out_shape=[jax.ShapeDtypeStruct(shape, jnp.float32)] * 2,
+        compiler_params=params(10),
         name="occupancy_parts",
     )(e[None], k[None], in_hbm(weights), in_hbm(density), in_hbm(volts), in_hbm(fixed), in_hbm(gate))
 
@@ -325,12 +322,8 @@
             r_ext[at + p, CY + 2 : W - 2, :] = gap
             r_ext[at + p, W - 2 : W, :] = -charge[WC * p + CY + 2 : WC * p + WC]
 
-    for j in range(LD):
-        charge = charge_of(cells[LD + j : LD + j + 1, :], values_of(lambda t: 8 * t + j), 0, SUB, y0)
-        keep(charge, SUB, 2 + SUB * j)
     keep(charge_of(cells[LD - 1 : LD, :], values_of(lambda t: 24 + t), SUB - 2, 2, y0), 2, 0)
     keep(charge_of(cells[2 * LD : 2 * LD + 1, :], values_of(lambda t: 27 + t), 0, 2, y0), 2, PLANES + 2)
-
     for at, halo in ((0, xlow), (PLANES + 2, xhigh)):
         for i in range(2):
             r_ext[at + i, 0:CY, :] = r_ext[at + i, 0:CY, :] + halo[i]
@@ -338,34 +331,33 @@
     g_ext[PLANES + 2, 0:CY, :] = xhigh[2]
     sub = lax.broadcasted_iota(jnp.int32, (8, NZ), 0)
     none = jnp.zeros((8, NZ), jnp.float32)
-    line = lambda x: jnp.broadcast_to(x, (8, NZ))
+    wide = lambda x: jnp.broadcast_to(x, (8, NZ))
     for at, i in ((1, 0), (PLANES + 2, 1)):
-        tile = jnp.where(sub == 0, line(corners[i, 1:2, :]), jnp.where(sub == 7, line(corners[i, 0:1, :]), none))
+        tile = jnp.where(sub == 0, wide(corners[i, 1:2, :]), jnp.where(sub == 7, wide(corners[i, 0:1, :]), none))
         r_ext[at, CY:W, :] = r_ext[at, CY:W, :] + tile
         g_ext[at, CY:W, :] = none
     for copy in copies:
         copy.wait()
 
-    def load_plane(p, carry):
-        at = pl.ds(p, 1)
+    def load_plane(p):
+        at = slice(p, p + 1)
         g = gate_here[p].astype(jnp.float32)
         g_ext[p + 2, 0:CY, :] = g
         r_ext[p + 2, 0:CY, :] = r_ext[p + 2, 0:CY, :] + (fixed_here[p] + PENALTY * g * volts[p])
-        tile = jnp.where(sub == 0, line(yhigh[0, at, :]), jnp.where(sub == 1, line(yhigh[1, at, :]), none))
-        tile = jnp.where(sub == 6, line(ylow[0, at, :]), jnp.where(sub == 7, line(ylow[1, at, :]), tile))
+        tile = jnp.where(sub == 0, wide(yhigh[0, at, :]), jnp.where(sub == 1, wide(yhigh[1, at, :]), none))
+        tile = jnp.where(sub == 6, wide(ylow[0, at, :]), jnp.where(sub == 7, wide(ylow[1, at, :]), tile))
         r_ext[p + 2, CY:W, :] = r_ext[p + 2, CY:W, :] + tile
-        tile = jnp.where(sub == 0, line(yhigh[2, at, :]), jnp.where(sub == 7, line(ylow[2, at, :]), none))
+        tile = jnp.where(sub == 0, wide(yhigh[2, at, :]), jnp.where(sub == 7, wide(ylow[2, at, :]), none))
         g_ext[p + 2, CY:W, :] = tile
-        return carry
-
-    lax.fori_loop(0, PLANES, load_plane, 0, unroll=8)
 
     def image_plane(p):
         here = r_ext[p + 1]
-        x = e * PLANES + p - 1
-        inside = jnp.where((x >= 0) & (x < NE * PLANES), 1.0, 0.0)
+        inside = valid
+        if p in (0, PLANES + 1):
+            x = e * PLANES + p - 1
+            inside = valid * jnp.where((x >= 0) & (x < NE * PLANES), 1.0, 0.0)
         around = r_ext[p + 2] + r_ext[p] + in_plane(here)
-        return ((6.0 + PENALTY * g_ext[p + 1]) * here - around) * (valid * inside)
+        return ((6.0 + PENALTY * g_ext[p + 1]) * here - around) * inside
 
     def sum_plane(p, carry):
         before, here, rr, rw, ww, waw = carry
@@ -377,11 +369,25 @@
         fields_out[1, p] = w
         return here, after, rr + r * r, rw + r * w, ww + w * w, waw + w * image
 
-    zero = jnp.zeros((CY, NZ), jnp.float32)
-    totals = lax.fori_loop(0, PLANES, sum_plane, (image_plane(0), image_plane(1)) + (zero,) * 4, unroll=8)[2:]
+    carry = None
+    done = 0
+    for j in range(LD + 1):
+        if j < LD:
+            charge = charge_of(cells[LD + j : LD + j + 1, :], values_of(lambda t: 8 * t + j), 0, SUB, y0)
+        ready = SUB * j - 2 if j < LD else PLANES
+        if j and carry is None:
+            zero = jnp.zeros((CY, NZ), jnp.float32)
+            carry = (image_plane(0), image_plane(1)) + (zero,) * 4
+        for p in range(done, ready):
+            carry = sum_plane(p, carry)
+        done = max(done, ready)
+        if j < LD:
+            keep(charge, SUB, 2 + SUB * j)
+            for p in range(SUB * j, SUB * j + SUB):
+                load_plane(p)
     lane = lax.broadcasted_iota(jnp.int32, (1, 128), 1)
     line = jnp.zeros((1, 128), jnp.float32)
-    for i, total in enumerate(totals):
+    for i, total in enumerate(carry[2:]):
         line = line + jnp.where(lane == i, jnp.sum(total), 0.0)
     for d in range(NE * NK):
         sums[d] = line
@@ -500,43 +506,31 @@
     )(picked)
 
 
-def band_body(which, density, values, before, out, acc):
-    z = pl.program_id(0)
-    start = pl.multiple_of(which[0] * COL, 128)
-
-    @pl.when(z == 0)
-    def _():
-        acc[...] = jnp.zeros_like(acc)
-
-    for m in range(0, NE, 2):
-        v = values[m : m + 2, 0].reshape(16, COL)
-        for i in range(EL):
-            part = density[i, 8 * m : 8 * m + 16, pl.ds(start, COL)].astype(jnp.float32) * v
-            total = part[:, :128]
-            for t in range(1, TL):
-                total = total + part[:, 128 * t : 128 * (t + 1)]
-            acc[i, 8 * m : 8 * m + 16] = acc[i, 8 * m : 8 * m + 16] + total
-
-    @pl.when(z == NZC - 1)
-    def _():
-        for i in range(EL):
-            out[i : i + 1, :] = before[i : i + 1, :] + jnp.sum(acc[i].T, axis=0, keepdims=True) * ORB**-0.5
+def band_body(which, density, values, before, out):
+    totals = [[None] * (NE // 2) for _ in range(EL)]
+    for m in range(NE // 2):
+        for z in range(NZC):
+            start = pl.multiple_of((2 * z + which[0]) * COL, 128)
+            v = values[2 * m : 2 * m + 2, z].reshape(16, COL)
+            for i in range(EL):
+                part = density[i, 16 * m : 16 * m + 16, pl.ds(start, COL)].astype(jnp.float32) * v
+                for t in range(TL):
+                    tile = part[:, 128 * t : 128 * (t + 1)]
+                    totals[i][m] = tile if totals[i][m] is None else totals[i][m] + tile
+    for i in range(EL):
+        total = jnp.concatenate(totals[i], axis=0)
+        out[i : i + 1, :] = before[i : i + 1, :] + jnp.sum(total.T, axis=0, keepdims=True) * ORB**-0.5
 
 
 def band(which, density, values, before):
-    small = pl.BlockSpec((EL, LAYERS), lambda z, *_: (0, 0))
+    whole = lambda x: pl.BlockSpec(x.shape, lambda i, *_: (0,) * x.ndim)
     return pl.pallas_call(
         band_body,
         grid_spec=pltpu.PrefetchScalarGridSpec(
             num_scalar_prefetch=1,
-            grid=(NZC,),
-            in_specs=[
-                pl.BlockSpec((EL, LAYERS, 2 * COL), lambda z, *_: (0, 0, z)),
-                pl.BlockSpec((NE, 1, LD, COL), lambda z, *_: (0, z, 0, 0)),
-                small,
-            ],
-            out_specs=small,
-            scratch_shapes=[pltpu.VMEM((EL, LAYERS, 128), jnp.float32)],
+            grid=(1,),
+            in_specs=[whole(density), whole(values), whole(before)],
+            out_specs=whole(before),
         ),
         out_shape=jax.ShapeDtypeStruct((EL, LAYERS), jnp.float32),
         compiler_params=params(8),

time: 114 us -> 111 us (0.974)
  Pallas kernels: 21.9 us -> 18.2 us
    pallas_call x1, Pallas kernels: 3.73 us -> 2.21 us  [occupancy_parts(): pl.pallas_call(occupancy_body, grid_spec=pltpu.PrefetchScalarGridSpec(num...]
    pallas_call x1, Pallas kernels: 9.13 us -> 7.84 us  [fields(): pl.pallas_call(field_body, grid_spec=pltpu.PrefetchScalarGridSpec(num_sca...]
where the time goes in v4:
time: 111 us; the launch traced here: 109 us
  blocking collectives  46.1 us (42%)
  starting transfers between devices  22.6 us (20%)
  waiting for transfers between devices  20.4 us (18%)
  Pallas kernels  18.2 us (16%)
  other arithmetic  1.19 us (1%)
    all_to_all x3, blocking collectives, exchange(): return lax.all_to_all(x, axis, split_axis=0, concat_axis=0, tiled=True)  46.1 us
    all_to_all x2, starting transfers between devices, exchange(): return lax.all_to_all(x, axis, split_axis=0, concat_axis=0, tiled=True)  14.9 us
    all_to_all x2, waiting for transfers between devices, exchange(): return lax.all_to_all(x, axis, split_axis=0, concat_axis=0, tiled=True)  11.2 us
    pallas_call x1, Pallas kernels, fields(): pl.pallas_call(field_body, grid_spec=pltpu.PrefetchScalarGridSpec(num_sca...  7.84 us
    ppermute x2, starting transfers between devices, shift_up(): lax.ppermute(x, axis, [(i, i + 1) for i in range(lax.axis_size(axis) - 1)])  4.97 us
    ppermute x2, waiting for transfers between devices, swap_cores(): return lax.ppermute(x, CORE, [(0, 1), (1, 0)])  4.49 us
    pallas_call x1, Pallas kernels, pick(): pl.pallas_call(pick_body, grid_spec=pltpu.PrefetchScalarGridSpec(num_scal...  3.97 us
    ppermute x2, waiting for transfers between devices, shift_up(): lax.ppermute(x, axis, [(i, i + 1) for i in range(lax.axis_size(axis) - 1)])  2.71 us
  transfers between devices with their start and end apart: 8, of which 6 were waited for; matrix products, arithmetic and copies ran while one was open for 0% of the time, Pallas kernels for 3%

profile of v4, /device:TPU:0, one launch (start us, length us, event | category | flops | bytes accessed | tf_op | source)
XLA Modules:
  0.0 109.2 jit_solution(3723547408204699296)
XLA Ops:
  0.6 2.2 %occupancy_parts.1 = (f32[16,4,32,128]{3,2,1,0:T(8,128)S(1)}, f32[16,4,32,128]{3,2,1,0:T(8,128)S(1)}) custom-call(s32[1]{0:T(128)} %bitcast.1.energy, s32[1]{0:T(128)} %bitcast.kpt, f32[1,4]{1,0:T(1,128)} %bitcast.20, bf16[4,128,3072]{2,1,0:T(8,128)(2,1)} %bitcast.13, f32[64]{0:T(128)} %volts_out.5, f32[64,16,256]{2,1,0:T(8,128)} %fixed.5, s32[64,16,256]{2,1,0:T(8,128)} %gate.5), custom_call_target="tpu_custom_call" | custom-call | tf_op jit(solution)/shard_map/occupancy_parts/pallas_call | solution.py:118
  2.9 0.1 collective-permute-start
  3.0 2.6 %collective-permute-done = f32[64,32,128]{2,1,0:T(8,128)S(1)} collective-permute-done((f32[64,32,128]{2,1,0:T(8,128)S(1)}, f32[64,32,128]{2,1,0:T(8,128)S(1)}, u32[]{:S(2)}, u32[]{:S(2)}) %collective-permute-start) | collective-permute-done | bytes 1048608 | tf_op jit(solution)/shard_map/ppermute | solution.py:36
  5.6 1.2 %bitcast_add_fusion = f32[64,32,128]{2,1,0:T(8,128)} fusion(f32[64,32,128]{2,1,0:T(8,128)S(1)} %collective-permute-done, f32[16,4,32,128]{3,2,1,0:T(8,128)S(1)} %get-tuple-element.18), kind=kLoop, calls=%fused_computation | loop fusion | flops 262144 | bytes 3145728 | tf_op jit(solution)/shard_map/add | solution.py:559
  6.8 11.5 %all-to-all-start = ((f32[64,32,128]{2,1,0:T(8,128)}), f32[64,32,128]{2,1,0:T(8,128)S(1)}, u32[]{:S(2)}, u32[]{:S(2)}) async-start(f32[64,32,128]{2,1,0:T(8,128)} %bitcast_add_fusion), calls=%async_computation | async-start | bytes 2097152 | tf_op jit(solution)/shard_map/all_to_all | solution.py:40
  18.3 2.0 %edges.1 = (f32[3,16,256]{2,1,0:T(8,128)S(1)}, f32[3,16,256]{2,1,0:T(8,128)S(1)}, f32[3,64,256]{2,1,0:T(8,128)S(1)}, f32[3,64,256]{2,1,0:T(8,128)S(1)}, s32[24,3072]{1,0:T(8,128)S(1)}) custom-call(s32[1]{0:T(128)} %bitcast.1.energy, f32[64]{0:T(128)} %volts_out.5, f32[64,16,256]{2,1,0:T(8,128)} %fixed.5, s32[64,16,256]{2,1,0:T(8,128)} %gate.5, s32[128,3072]{1,0:T(8,128)} %cells.1), custom_call_target="tpu_custom_call" | custom-call | tf_op jit(solution)/shard_map/edges/pallas_call | solution.py:182
  20.3 1.8 %collective-permute-start.3 = (f32[3,64,256]{2,1,0:T(8,128)S(1)}, f32[3,64,256]{2,1,0:T(8,128)S(1)}, u32[]{:S(2)}, u32[]{:S(2)}) collective-permute-start(f32[3,64,256]{2,1,0:T(8,128)S(1)} %get-tuple-element.28), channel_id=1, source_target_pairs={{0,1},{1,2},{2,3},{3,4},{4,5},{5,6},{6,7},{8,9},{9,10},{10,11},{11... | collective-permute-start | bytes 589832 | tf_op jit(solution)/shard_map/ppermute | solution.py:542
  22.1 1.3 %collective-permute-start.4 = (f32[3,64,256]{2,1,0:T(8,128)S(1)}, f32[3,64,256]{2,1,0:T(8,128)S(1)}, u32[]{:S(2)}, u32[]{:S(2)}) collective-permute-start(f32[3,64,256]{2,1,0:T(8,128)S(1)} %get-tuple-element.29), channel_id=1, source_target_pairs={{1,0},{2,1},{3,2},{4,3},{5,4},{6,5},{7,6},{9,8},{10,9},{11,10},{12... | collective-permute-start | bytes 589832 | tf_op jit(solution)/shard_map/ppermute | solution.py:546
  23.4 3.2 %collective-permute-start.1 = (f32[3,16,256]{2,1,0:T(8,128)S(1)}, f32[3,16,256]{2,1,0:T(8,128)S(1)}, u32[]{:S(2)}, u32[]{:S(2)}) collective-permute-start(f32[3,16,256]{2,1,0:T(8,128)S(1)} %get-tuple-element.20), channel_id=1, source_target_pairs={{0,8},{8,16},{16,24},{24,32},{32,40},{40,48},{48,56},{56,64},{64,7... | collective-permute-start | bytes 147464 | tf_op jit(solution)/shard_map/ppermute | solution.py:542
  26.6 1.3 %collective-permute-start.2 = (f32[3,16,256]{2,1,0:T(8,128)S(1)}, f32[3,16,256]{2,1,0:T(8,128)S(1)}, u32[]{:S(2)}, u32[]{:S(2)}) collective-permute-start(f32[3,16,256]{2,1,0:T(8,128)S(1)} %get-tuple-element.21), channel_id=1, source_target_pairs={{8,0},{16,8},{24,16},{32,24},{40,32},{48,40},{56,48},{64,56},{72,6... | collective-permute-start | bytes 147464 | tf_op jit(solution)/shard_map/ppermute | solution.py:546
  27.9 2.7 %collective-permute-done.1.xlow = f32[3,16,256]{2,1,0:T(8,128)S(1)} collective-permute-done((f32[3,16,256]{2,1,0:T(8,128)S(1)}, f32[3,16,256]{2,1,0:T(8,128)S(1)}, u32[]{:S(2)}, u32[]{:S(2)}) %collective-permute-start.1) | collective-permute-done | bytes 49184 | tf_op jit(solution)/shard_map/ppermute | solution.py:542
  30.6 2.0 %collective-permute-done.2.xhigh = f32[3,16,256]{2,1,0:T(8,128)S(1)} collective-permute-done((f32[3,16,256]{2,1,0:T(8,128)S(1)}, f32[3,16,256]{2,1,0:T(8,128)S(1)}, u32[]{:S(2)}, u32[]{:S(2)}) %collective-permute-start.2) | collective-permute-done | bytes 49184 | tf_op jit(solution)/shard_map/ppermute | solution.py:546
  32.6 5.2 %all-to-all-done.parts = f32[64,32,128]{2,1,0:T(8,128)S(1)} async-done(((f32[64,32,128]{2,1,0:T(8,128)}), f32[64,32,128]{2,1,0:T(8,128)S(1)}, u32[]{:S(2)}, u32[]{:S(2)}) %all-to-all-start) | async-done | bytes 1048608 | tf_op jit(solution)/shard_map/all_to_all | solution.py:40
  37.7 0.8 collect.1
  38.5 3.4 %all-to-all-start.1 = ((f32[8,32,128]{2,1,0:T(8,128)}), f32[8,32,128]{2,1,0:T(8,128)S(1)}, u32[]{:S(2)}, u32[]{:S(2)}) async-start(f32[8,32,128]{2,1,0:T(8,128)} %get-tuple-element.23), calls=%async_computation.1 | async-start | bytes 262144 | tf_op jit(solution)/shard_map/all_to_all | solution.py:40
  41.9 0.0 collective-permute-done.3.ylow
  41.9 0.0 collective-permute-done.4.yhigh
  41.9 6.0 %all-to-all-done.1.occ = f32[8,32,128]{2,1,0:T(8,128)S(1)} async-done(((f32[8,32,128]{2,1,0:T(8,128)}), f32[8,32,128]{2,1,0:T(8,128)S(1)}, u32[]{:S(2)}, u32[]{:S(2)}) %all-to-all-start.1) | async-done | bytes 131104 | tf_op jit(solution)/shard_map/all_to_all | solution.py:40
  47.9 7.8 %fields.1 = (f32[128,1,128]{2,1,0:T(1,128)S(1)}, f32[2,64,16,256]{3,2,1,0:T(8,128)S(1)}) custom-call(s32[1]{0:T(128)} %bitcast.1.energy, s32[1]{0:T(128)} %bitcast.kpt, f32[8,32,128]{2,1,0:T(8,128)S(1)} %all-to-all-done.1.occ, s32[24,3072]{1,0:T(8,128)S(1)} %get-tuple-element.24.cells.cells_near, f32[2,2,256]{2,1,0:T(2,128)S(1)} %get-tuple-element.25.corners, ...), custom_call_target="tpu_custom_call" | custom-call | tf_op jit(solution)/shard_map/fields/pallas_call | solution.py:402
  55.8 17.6 %all_to_all.25.sums = f32[128,1,128]{2,1,0:T(1,128)S(1)} all-to-all(f32[128,1,128]{2,1,0:T(1,128)S(1)} %get-tuple-element.30), channel_id=1, replica_groups=mesh['energy_0'=4,'energy_1'=4,'kpt_0'=4,'kpt_1'=2] {'energy_0','energy_..., dimensions={0} | all-to-all | bytes 131072 | tf_op jit(solution)/shard_map/all_to_all | solution.py:40
  73.3 0.0 copy-start
  73.3 4.0 %pick.1 = (f32[8,8,384]{2,1,0:T(8,128)S(1)}, f32[64,16,256]{2,1,0:T(8,128)}) custom-call(s32[1]{0:T(128)} %bitcast.kpt, f32[128,1,128]{2,1,0:T(1,128)S(1)} %all_to_all.25.sums, s32[24,3072]{1,0:T(8,128)S(1)} %get-tuple-element.24.cells.cells_near, f32[2,64,16,256]{3,2,1,0:T(8,128)S(1)} %get-tuple-element.31.rw), custom_call_target="tpu_custom_call" | custom-call | tf_op jit(solution)/shard_map/pick/pallas_call | solution.py:477
  77.3 8.2 %all_to_all.26.picked = f32[8,8,384]{2,1,0:T(8,128)S(1)} all-to-all(f32[8,8,384]{2,1,0:T(8,128)S(1)} %get-tuple-element.33), channel_id=1, replica_groups=mesh['energy_0'=4,'energy_1'=4,'kpt_0'=4,'kpt_1'=2] {'kpt_0','kpt_1'}, dimensions={0} | all-to-all | bytes 196608 | tf_op jit(solution)/shard_map/all_to_all | solution.py:40
  85.5 0.1 join.1
  85.5 20.4 %all_to_all.27 = f32[64,8,384]{2,1,0:T(8,128)S(1)} all-to-all(f32[64,8,384]{2,1,0:T(8,128)S(1)} %join.1), channel_id=1, replica_groups=mesh['energy_0'=4,'energy_1'=4,'kpt_0'=4,'kpt_1'=2] {'energy_0','energy_..., dimensions={0} | all-to-all | bytes 1572864 | tf_op jit(solution)/shard_map/all_to_all | solution.py:40
  105.9 0.0 collective-permute-start.5
  105.9 0.0 copy-done
  105.9 0.4 band.2.before
  106.3 1.8 %collective-permute-done.5 = f32[64,8,384]{2,1,0:T(8,128)S(1)} collective-permute-done((f32[64,8,384]{2,1,0:T(8,128)S(1)}, f32[64,8,384]{2,1,0:T(8,128)S(1)}, u32[]{:S(2)}, u32[]{:S(2)}) %collective-permute-start.5) | collective-permute-done | bytes 786464 | tf_op jit(solution)/shard_map/ppermute | solution.py:36
  108.2 1.0 band.3
  (1 shorter events, 0.0 us)
Async XLA Ops:
  2.9 2.7 %collective-permute-start = (f32[64,32,128]{2,1,0:T(8,128)S(1)}, f32[64,32,128]{2,1,0:T(8,128)S(1)}, u32[]{:S(2)}, u32[]{:S(2)}) collective-permute-start(f32[64,32,128]{2,1,0:T(8,128)S(1)} %bitcast.18), channel_id=1, source_target_pairs={{0,1},{1,0},{2,3},{3,2},{4,5},{5,4},{6,7},{7,6},{8,9},{9,8},{10,11... | collective-permute-start | bytes 3145736 | tf_op jit(solution)/shard_map/ppermute | solution.py:36
  6.8 31.0 %all-to-all-start = ((f32[64,32,128]{2,1,0:T(8,128)}), f32[64,32,128]{2,1,0:T(8,128)S(1)}, u32[]{:S(2)}, u32[]{:S(2)}) async-start(f32[64,32,128]{2,1,0:T(8,128)} %bitcast_add_fusion), calls=%async_computation | async-start | bytes 2097152 | tf_op jit(solution)/shard_map/all_to_all | solution.py:40
  20.3 21.6 %collective-permute-start.3 = (f32[3,64,256]{2,1,0:T(8,128)S(1)}, f32[3,64,256]{2,1,0:T(8,128)S(1)}, u32[]{:S(2)}, u32[]{:S(2)}) collective-permute-start(f32[3,64,256]{2,1,0:T(8,128)S(1)} %get-tuple-element.28), channel_id=1, source_target_pairs={{0,1},{1,2},{2,3},{3,4},{4,5},{5,6},{6,7},{8,9},{9,10},{10,11},{11... | collective-permute-start | bytes 589832 | tf_op jit(solution)/shard_map/ppermute | solution.py:542
  22.1 19.8 %collective-permute-start.4 = (f32[3,64,256]{2,1,0:T(8,128)S(1)}, f32[3,64,256]{2,1,0:T(8,128)S(1)}, u32[]{:S(2)}, u32[]{:S(2)}) collective-permute-start(f32[3,64,256]{2,1,0:T(8,128)S(1)} %get-tuple-element.29), channel_id=1, source_target_pairs={{1,0},{2,1},{3,2},{4,3},{5,4},{6,5},{7,6},{9,8},{10,9},{11,10},{12... | collective-permute-start | bytes 589832 | tf_op jit(solution)/shard_map/ppermute | solution.py:546
  23.4 7.2 %collective-permute-start.1 = (f32[3,16,256]{2,1,0:T(8,128)S(1)}, f32[3,16,256]{2,1,0:T(8,128)S(1)}, u32[]{:S(2)}, u32[]{:S(2)}) collective-permute-start(f32[3,16,256]{2,1,0:T(8,128)S(1)} %get-tuple-element.20), channel_id=1, source_target_pairs={{0,8},{8,16},{16,24},{24,32},{32,40},{40,48},{48,56},{56,64},{64,7... | collective-permute-start | bytes 147464 | tf_op jit(solution)/shard_map/ppermute | solution.py:542
  26.6 6.0 %collective-permute-start.2 = (f32[3,16,256]{2,1,0:T(8,128)S(1)}, f32[3,16,256]{2,1,0:T(8,128)S(1)}, u32[]{:S(2)}, u32[]{:S(2)}) collective-permute-start(f32[3,16,256]{2,1,0:T(8,128)S(1)} %get-tuple-element.21), channel_id=1, source_target_pairs={{8,0},{16,8},{24,16},{32,24},{40,32},{48,40},{56,48},{64,56},{72,6... | collective-permute-start | bytes 147464 | tf_op jit(solution)/shard_map/ppermute | solution.py:546
  38.5 9.4 %all-to-all-start.1 = ((f32[8,32,128]{2,1,0:T(8,128)}), f32[8,32,128]{2,1,0:T(8,128)S(1)}, u32[]{:S(2)}, u32[]{:S(2)}) async-start(f32[8,32,128]{2,1,0:T(8,128)} %get-tuple-element.23), calls=%async_computation.1 | async-start | bytes 262144 | tf_op jit(solution)/shard_map/all_to_all | solution.py:40
  73.3 32.6 %copy-start = (bf16[4,1,128,3072]{3,2,1,0:T(8,128)(2,1)S(1)}, bf16[4,1,128,3072]{3,2,1,0:T(8,128)(2,1)}, u32[]{:S(2)}) copy-start(bf16[4,1,128,3072]{3,2,1,0:T(8,128)(2,1)} %param.6) | copy-start | bytes 9437188
  105.9 2.3 %collective-permute-start.5 = (f32[64,8,384]{2,1,0:T(8,128)S(1)}, f32[64,8,384]{2,1,0:T(8,128)S(1)}, u32[]{:S(2)}, u32[]{:S(2)}) collective-permute-start(f32[64,8,384]{2,1,0:T(8,128)S(1)} %all_to_all.27), channel_id=1, source_target_pairs={{0,1},{1,0},{2,3},{3,2},{4,5},{5,4},{6,7},{7,6},{8,9},{9,8},{10,11... | collective-permute-start | bytes 2359304 | tf_op jit(solution)/shard_map/ppermute | solution.py:36

commit v5 on v4

--- a/solution.py
+++ b/solution.py
@@ -29,6 +29,7 @@
 COL = ORB // NK
 TL = COL // 128
 PENALTY = 4.0
+PIECES = 8
 AHEAD = 4
 
 
@@ -201,6 +202,35 @@
     )(e[None], in_hbm(volts), in_hbm(fixed), in_hbm(gate), in_hbm(cells))
 
 
+def pair_body(own, received, out, here, leaving):
+    copies = []
+    cut = NE * NZC // PIECES
+    for i in range(PIECES):
+        at = pl.ds(cut * i, cut)
+        here[at] = own[at] + received[at]
+        copies.append(pltpu.make_async_copy(here.at[at], out.at[at], leaving.at[i]))
+        copies[-1].start()
+    for copy in copies:
+        copy.wait()
+
+
+def add_pair(own, received):
+    whole = pl.BlockSpec(own.shape, lambda i: (0, 0, 0))
+    return pl.pallas_call(
+        pair_body,
+        grid_spec=pltpu.PrefetchScalarGridSpec(
+            num_scalar_prefetch=0,
+            grid=(1,),
+            in_specs=[whole, whole],
+            out_specs=pl.BlockSpec(memory_space=pltpu.HBM),
+            scratch_shapes=[pltpu.VMEM(own.shape, jnp.float32), pltpu.SemaphoreType.DMA((PIECES,))],
+        ),
+        out_shape=pltpu.HBM(own.shape, jnp.float32),
+        compiler_params=params(4),
+        name="add_pair",
+    )(own, received)
+
+
 def collect_body(energy, kpt, parts, out, corners):
     e = energy[0]
     k = kpt[0]
@@ -323,21 +353,20 @@
             r_ext[at + p, W - 2 : W, :] = -charge[WC * p + CY + 2 : WC * p + WC]
 
     keep(charge_of(cells[LD - 1 : LD, :], values_of(lambda t: 24 + t), SUB - 2, 2, y0), 2, 0)
-    keep(charge_of(cells[2 * LD : 2 * LD + 1, :], values_of(lambda t: 27 + t), 0, 2, y0), 2, PLANES + 2)
-    for at, halo in ((0, xlow), (PLANES + 2, xhigh)):
-        for i in range(2):
-            r_ext[at + i, 0:CY, :] = r_ext[at + i, 0:CY, :] + halo[i]
-    g_ext[1, 0:CY, :] = xlow[2]
-    g_ext[PLANES + 2, 0:CY, :] = xhigh[2]
     sub = lax.broadcasted_iota(jnp.int32, (8, NZ), 0)
     none = jnp.zeros((8, NZ), jnp.float32)
     wide = lambda x: jnp.broadcast_to(x, (8, NZ))
-    for at, i in ((1, 0), (PLANES + 2, 1)):
+
+    def outside(at, halo, i):
+        for n in range(2):
+            r_ext[at + n, 0:CY, :] = r_ext[at + n, 0:CY, :] + halo[n]
+        beside = at + 1 - i
         tile = jnp.where(sub == 0, wide(corners[i, 1:2, :]), jnp.where(sub == 7, wide(corners[i, 0:1, :]), none))
-        r_ext[at, CY:W, :] = r_ext[at, CY:W, :] + tile
-        g_ext[at, CY:W, :] = none
-    for copy in copies:
-        copy.wait()
+        g_ext[beside, 0:CY, :] = halo[2]
+        r_ext[beside, CY:W, :] = r_ext[beside, CY:W, :] + tile
+        g_ext[beside, CY:W, :] = none
+
+    outside(0, xlow, 0)
 
     def load_plane(p):
         at = slice(p, p + 1)
@@ -374,7 +403,12 @@
     for j in range(LD + 1):
         if j < LD:
             charge = charge_of(cells[LD + j : LD + j + 1, :], values_of(lambda t: 8 * t + j), 0, SUB, y0)
-        ready = SUB * j - 2 if j < LD else PLANES
+        else:
+            charge = charge_of(cells[2 * LD : 2 * LD + 1, :], values_of(lambda t: 27 + t), 0, 2, y0)
+        if j == 0:
+            for copy in copies:
+                copy.wait()
+        ready = SUB * j - 2
         if j and carry is None:
             zero = jnp.zeros((CY, NZ), jnp.float32)
             carry = (image_plane(0), image_plane(1)) + (zero,) * 4
@@ -385,6 +419,10 @@
             keep(charge, SUB, 2 + SUB * j)
             for p in range(SUB * j, SUB * j + SUB):
                 load_plane(p)
+    keep(charge, 2, PLANES + 2)
+    outside(PLANES + 2, xhigh, 1)
+    for p in range(done, PLANES):
+        carry = sum_plane(p, carry)
     lane = lax.broadcasted_iota(jnp.int32, (1, 128), 1)
     line = jnp.zeros((1, 128), jnp.float32)
     for i, total in enumerate(carry[2:]):
@@ -556,7 +594,7 @@
     chips = NE * NZC
     received = swap_cores(other.reshape(chips, 32, 128))
     xup, xdown, yup, ydown, cells = edges(e, gate_voltage, fixed_charge, gate_mask, orbital_cells)
-    pair = own.reshape(chips, 32, 128) + received
+    pair = add_pair(own.reshape(chips, 32, 128), received)
     parts = exchange(pair, CHIPS)
     xlow = shift_up(xup, ENERGY)
     xhigh = shift_down(xdown, ENERGY)

time: 111 us -> 110 us (level)
  other arithmetic: 1.19 us -> 0 us
    add x1 -> x0, other arithmetic: 1.19 us -> none  [one_step(): pair = own.reshape(chips, 32, 128) + received]
where the time goes in v5:
time: 110 us; the launch traced here: 109 us
  blocking collectives  46.1 us (42%)
  starting transfers between devices  22.6 us (21%)
  waiting for transfers between devices  20.4 us (19%)
  Pallas kernels  19 us (17%)
    all_to_all x3, blocking collectives, exchange(): return lax.all_to_all(x, axis, split_axis=0, concat_axis=0, tiled=True)  46.1 us
    all_to_all x2, starting transfers between devices, exchange(): return lax.all_to_all(x, axis, split_axis=0, concat_axis=0, tiled=True)  14.9 us
    all_to_all x2, waiting for transfers between devices, exchange(): return lax.all_to_all(x, axis, split_axis=0, concat_axis=0, tiled=True)  11.2 us
    pallas_call x1, Pallas kernels, fields(): pl.pallas_call(field_body, grid_spec=pltpu.PrefetchScalarGridSpec(num_sca...  7.54 us
    ppermute x2, starting transfers between devices, shift_up(): lax.ppermute(x, axis, [(i, i + 1) for i in range(lax.axis_size(axis) - 1)])  4.97 us
    ppermute x2, waiting for transfers between devices, swap_cores(): return lax.ppermute(x, CORE, [(0, 1), (1, 0)])  4.48 us
    pallas_call x1, Pallas kernels, pick(): pl.pallas_call(pick_body, grid_spec=pltpu.PrefetchScalarGridSpec(num_scal...  3.95 us
    ppermute x2, waiting for transfers between devices, shift_up(): lax.ppermute(x, axis, [(i, i + 1) for i in range(lax.axis_size(axis) - 1)])  2.71 us
  transfers between devices with their start and end apart: 8, of which 6 were waited for; matrix products, arithmetic and copies ran while one was open for 0% of the time, Pallas kernels for 3%

profile of v5, /device:TPU:0, one launch (start us, length us, event | category | flops | bytes accessed | tf_op | source)
XLA Modules:
  0.0 108.8 jit_solution(698238918814899444)
XLA Ops:
  0.6 2.2 %occupancy_parts.1 = (f32[16,4,32,128]{3,2,1,0:T(8,128)S(1)}, f32[16,4,32,128]{3,2,1,0:T(8,128)S(1)}) custom-call(s32[1]{0:T(128)} %bitcast.1.energy, s32[1]{0:T(128)} %bitcast.kpt, f32[1,4]{1,0:T(1,128)} %bitcast.20, bf16[4,128,3072]{2,1,0:T(8,128)(2,1)} %bitcast.12, f32[64]{0:T(128)} %volts_out.5, f32[64,16,256]{2,1,0:T(8,128)} %fixed.5, s32[64,16,256]{2,1,0:T(8,128)} %gate.5), custom_call_target="tpu_custom_call" | custom-call | tf_op jit(solution)/shard_map/occupancy_parts/pallas_call | solution.py:119
  2.9 0.1 collective-permute-start
  3.0 2.6 %collective-permute-done.received = f32[64,32,128]{2,1,0:T(8,128)S(1)} collective-permute-done((f32[64,32,128]{2,1,0:T(8,128)S(1)}, f32[64,32,128]{2,1,0:T(8,128)S(1)}, u32[]{:S(2)}, u32[]{:S(2)}) %collective-permute-start) | collective-permute-done | bytes 1048608 | tf_op jit(solution)/shard_map/ppermute | solution.py:37
  5.6 1.0 add_pair.1
  6.6 11.6 %all-to-all-start = ((f32[64,32,128]{2,1,0:T(8,128)}), f32[64,32,128]{2,1,0:T(8,128)S(1)}, u32[]{:S(2)}, u32[]{:S(2)}) async-start(f32[64,32,128]{2,1,0:T(8,128)} %add_pair.1), calls=%async_computation | async-start | bytes 2097152 | tf_op jit(solution)/shard_map/all_to_all | solution.py:41
  18.2 2.0 %edges.1 = (f32[3,16,256]{2,1,0:T(8,128)S(1)}, f32[3,16,256]{2,1,0:T(8,128)S(1)}, f32[3,64,256]{2,1,0:T(8,128)S(1)}, f32[3,64,256]{2,1,0:T(8,128)S(1)}, s32[24,3072]{1,0:T(8,128)S(1)}) custom-call(s32[1]{0:T(128)} %bitcast.1.energy, f32[64]{0:T(128)} %volts_out.5, f32[64,16,256]{2,1,0:T(8,128)} %fixed.5, s32[64,16,256]{2,1,0:T(8,128)} %gate.5, s32[128,3072]{1,0:T(8,128)} %cells.1), custom_call_target="tpu_custom_call" | custom-call | tf_op jit(solution)/shard_map/edges/pallas_call | solution.py:183
  20.2 1.8 %collective-permute-start.3 = (f32[3,64,256]{2,1,0:T(8,128)S(1)}, f32[3,64,256]{2,1,0:T(8,128)S(1)}, u32[]{:S(2)}, u32[]{:S(2)}) collective-permute-start(f32[3,64,256]{2,1,0:T(8,128)S(1)} %get-tuple-element.28), channel_id=1, source_target_pairs={{0,1},{1,2},{2,3},{3,4},{4,5},{5,6},{6,7},{8,9},{9,10},{10,11},{11... | collective-permute-start | bytes 589832 | tf_op jit(solution)/shard_map/ppermute | solution.py:580
  21.9 1.3 %collective-permute-start.4 = (f32[3,64,256]{2,1,0:T(8,128)S(1)}, f32[3,64,256]{2,1,0:T(8,128)S(1)}, u32[]{:S(2)}, u32[]{:S(2)}) collective-permute-start(f32[3,64,256]{2,1,0:T(8,128)S(1)} %get-tuple-element.29), channel_id=1, source_target_pairs={{1,0},{2,1},{3,2},{4,3},{5,4},{6,5},{7,6},{9,8},{10,9},{11,10},{12... | collective-permute-start | bytes 589832 | tf_op jit(solution)/shard_map/ppermute | solution.py:584
  23.2 3.2 %collective-permute-start.1 = (f32[3,16,256]{2,1,0:T(8,128)S(1)}, f32[3,16,256]{2,1,0:T(8,128)S(1)}, u32[]{:S(2)}, u32[]{:S(2)}) collective-permute-start(f32[3,16,256]{2,1,0:T(8,128)S(1)} %get-tuple-element.20), channel_id=1, source_target_pairs={{0,8},{8,16},{16,24},{24,32},{32,40},{40,48},{48,56},{56,64},{64,7... | collective-permute-start | bytes 147464 | tf_op jit(solution)/shard_map/ppermute | solution.py:580
  26.5 1.3 %collective-permute-start.2 = (f32[3,16,256]{2,1,0:T(8,128)S(1)}, f32[3,16,256]{2,1,0:T(8,128)S(1)}, u32[]{:S(2)}, u32[]{:S(2)}) collective-permute-start(f32[3,16,256]{2,1,0:T(8,128)S(1)} %get-tuple-element.21), channel_id=1, source_target_pairs={{8,0},{16,8},{24,16},{32,24},{40,32},{48,40},{56,48},{64,56},{72,6... | collective-permute-start | bytes 147464 | tf_op jit(solution)/shard_map/ppermute | solution.py:584
  27.8 2.7 %collective-permute-done.1.xlow = f32[3,16,256]{2,1,0:T(8,128)S(1)} collective-permute-done((f32[3,16,256]{2,1,0:T(8,128)S(1)}, f32[3,16,256]{2,1,0:T(8,128)S(1)}, u32[]{:S(2)}, u32[]{:S(2)}) %collective-permute-start.1) | collective-permute-done | bytes 49184 | tf_op jit(solution)/shard_map/ppermute | solution.py:580
  30.5 2.0 %collective-permute-done.2.xhigh = f32[3,16,256]{2,1,0:T(8,128)S(1)} collective-permute-done((f32[3,16,256]{2,1,0:T(8,128)S(1)}, f32[3,16,256]{2,1,0:T(8,128)S(1)}, u32[]{:S(2)}, u32[]{:S(2)}) %collective-permute-start.2) | collective-permute-done | bytes 49184 | tf_op jit(solution)/shard_map/ppermute | solution.py:584
  32.4 5.2 %all-to-all-done.parts = f32[64,32,128]{2,1,0:T(8,128)S(1)} async-done(((f32[64,32,128]{2,1,0:T(8,128)}), f32[64,32,128]{2,1,0:T(8,128)S(1)}, u32[]{:S(2)}, u32[]{:S(2)}) %all-to-all-start) | async-done | bytes 1048608 | tf_op jit(solution)/shard_map/all_to_all | solution.py:41
  37.6 0.8 collect.1
  38.4 3.4 %all-to-all-start.1 = ((f32[8,32,128]{2,1,0:T(8,128)}), f32[8,32,128]{2,1,0:T(8,128)S(1)}, u32[]{:S(2)}, u32[]{:S(2)}) async-start(f32[8,32,128]{2,1,0:T(8,128)} %get-tuple-element.23), calls=%async_computation.1 | async-start | bytes 262144 | tf_op jit(solution)/shard_map/all_to_all | solution.py:41
  41.8 0.0 collective-permute-done.3.ylow
  41.8 0.0 collective-permute-done.4.yhigh
  41.8 6.0 %all-to-all-done.1.occ = f32[8,32,128]{2,1,0:T(8,128)S(1)} async-done(((f32[8,32,128]{2,1,0:T(8,128)}), f32[8,32,128]{2,1,0:T(8,128)S(1)}, u32[]{:S(2)}, u32[]{:S(2)}) %all-to-all-start.1) | async-done | bytes 131104 | tf_op jit(solution)/shard_map/all_to_all | solution.py:41
  47.8 7.5 %fields.1 = (f32[128,1,128]{2,1,0:T(1,128)S(1)}, f32[2,64,16,256]{3,2,1,0:T(8,128)S(1)}) custom-call(s32[1]{0:T(128)} %bitcast.1.energy, s32[1]{0:T(128)} %bitcast.kpt, f32[8,32,128]{2,1,0:T(8,128)S(1)} %all-to-all-done.1.occ, s32[24,3072]{1,0:T(8,128)S(1)} %get-tuple-element.24.cells.cells_near, f32[2,2,256]{2,1,0:T(2,128)S(1)} %get-tuple-element.25.corners, ...), custom_call_target="tpu_custom_call" | custom-call | tf_op jit(solution)/shard_map/fields/pallas_call | solution.py:440
  55.3 17.6 %all_to_all.25.sums = f32[128,1,128]{2,1,0:T(1,128)S(1)} all-to-all(f32[128,1,128]{2,1,0:T(1,128)S(1)} %get-tuple-element.30), channel_id=1, replica_groups=mesh['energy_0'=4,'energy_1'=4,'kpt_0'=4,'kpt_1'=2] {'energy_0','energy_..., dimensions={0} | all-to-all | bytes 131072 | tf_op jit(solution)/shard_map/all_to_all | solution.py:41
  72.9 0.0 copy-start
  72.9 3.9 %pick.1 = (f32[8,8,384]{2,1,0:T(8,128)S(1)}, f32[64,16,256]{2,1,0:T(8,128)}) custom-call(s32[1]{0:T(128)} %bitcast.kpt, f32[128,1,128]{2,1,0:T(1,128)S(1)} %all_to_all.25.sums, s32[24,3072]{1,0:T(8,128)S(1)} %get-tuple-element.24.cells.cells_near, f32[2,64,16,256]{3,2,1,0:T(8,128)S(1)} %get-tuple-element.31.rw), custom_call_target="tpu_custom_call" | custom-call | tf_op jit(solution)/shard_map/pick/pallas_call | solution.py:515
  76.9 8.2 %all_to_all.26.picked = f32[8,8,384]{2,1,0:T(8,128)S(1)} all-to-all(f32[8,8,384]{2,1,0:T(8,128)S(1)} %get-tuple-element.33), channel_id=1, replica_groups=mesh['energy_0'=4,'energy_1'=4,'kpt_0'=4,'kpt_1'=2] {'kpt_0','kpt_1'}, dimensions={0} | all-to-all | bytes 196608 | tf_op jit(solution)/shard_map/all_to_all | solution.py:41
  85.0 0.1 join.1
  85.1 20.4 %all_to_all.27 = f32[64,8,384]{2,1,0:T(8,128)S(1)} all-to-all(f32[64,8,384]{2,1,0:T(8,128)S(1)} %join.1), channel_id=1, replica_groups=mesh['energy_0'=4,'energy_1'=4,'kpt_0'=4,'kpt_1'=2] {'energy_0','energy_..., dimensions={0} | all-to-all | bytes 1572864 | tf_op jit(solution)/shard_map/all_to_all | solution.py:41
  105.5 0.0 collective-permute-start.5
  105.5 0.0 copy-done
  105.5 0.4 band.2.before
  105.9 1.8 %collective-permute-done.5 = f32[64,8,384]{2,1,0:T(8,128)S(1)} collective-permute-done((f32[64,8,384]{2,1,0:T(8,128)S(1)}, f32[64,8,384]{2,1,0:T(8,128)S(1)}, u32[]{:S(2)}, u32[]{:S(2)}) %collective-permute-start.5) | collective-permute-done | bytes 786464 | tf_op jit(solution)/shard_map/ppermute | solution.py:37
  107.7 1.0 band.3
  (1 shorter events, 0.0 us)
Async XLA Ops:
  2.9 2.7 %collective-permute-start = (f32[64,32,128]{2,1,0:T(8,128)S(1)}, f32[64,32,128]{2,1,0:T(8,128)S(1)}, u32[]{:S(2)}, u32[]{:S(2)}) collective-permute-start(f32[64,32,128]{2,1,0:T(8,128)S(1)} %bitcast.18), channel_id=1, source_target_pairs={{0,1},{1,0},{2,3},{3,2},{4,5},{5,4},{6,7},{7,6},{8,9},{9,8},{10,11... | collective-permute-start | bytes 3145736 | tf_op jit(solution)/shard_map/ppermute | solution.py:37
  6.6 31.0 %all-to-all-start = ((f32[64,32,128]{2,1,0:T(8,128)}), f32[64,32,128]{2,1,0:T(8,128)S(1)}, u32[]{:S(2)}, u32[]{:S(2)}) async-start(f32[64,32,128]{2,1,0:T(8,128)} %add_pair.1), calls=%async_computation | async-start | bytes 2097152 | tf_op jit(solution)/shard_map/all_to_all | solution.py:41
  20.2 21.6 %collective-permute-start.3 = (f32[3,64,256]{2,1,0:T(8,128)S(1)}, f32[3,64,256]{2,1,0:T(8,128)S(1)}, u32[]{:S(2)}, u32[]{:S(2)}) collective-permute-start(f32[3,64,256]{2,1,0:T(8,128)S(1)} %get-tuple-element.28), channel_id=1, source_target_pairs={{0,1},{1,2},{2,3},{3,4},{4,5},{5,6},{6,7},{8,9},{9,10},{10,11},{11... | collective-permute-start | bytes 589832 | tf_op jit(solution)/shard_map/ppermute | solution.py:580
  21.9 19.8 %collective-permute-start.4 = (f32[3,64,256]{2,1,0:T(8,128)S(1)}, f32[3,64,256]{2,1,0:T(8,128)S(1)}, u32[]{:S(2)}, u32[]{:S(2)}) collective-permute-start(f32[3,64,256]{2,1,0:T(8,128)S(1)} %get-tuple-element.29), channel_id=1, source_target_pairs={{1,0},{2,1},{3,2},{4,3},{5,4},{6,5},{7,6},{9,8},{10,9},{11,10},{12... | collective-permute-start | bytes 589832 | tf_op jit(solution)/shard_map/ppermute | solution.py:584
  23.2 7.2 %collective-permute-start.1 = (f32[3,16,256]{2,1,0:T(8,128)S(1)}, f32[3,16,256]{2,1,0:T(8,128)S(1)}, u32[]{:S(2)}, u32[]{:S(2)}) collective-permute-start(f32[3,16,256]{2,1,0:T(8,128)S(1)} %get-tuple-element.20), channel_id=1, source_target_pairs={{0,8},{8,16},{16,24},{24,32},{32,40},{40,48},{48,56},{56,64},{64,7... | collective-permute-start | bytes 147464 | tf_op jit(solution)/shard_map/ppermute | solution.py:580
  26.5 6.0 %collective-permute-start.2 = (f32[3,16,256]{2,1,0:T(8,128)S(1)}, f32[3,16,256]{2,1,0:T(8,128)S(1)}, u32[]{:S(2)}, u32[]{:S(2)}) collective-permute-start(f32[3,16,256]{2,1,0:T(8,128)S(1)} %get-tuple-element.21), channel_id=1, source_target_pairs={{8,0},{16,8},{24,16},{32,24},{40,32},{48,40},{56,48},{64,56},{72,6... | collective-permute-start | bytes 147464 | tf_op jit(solution)/shard_map/ppermute | solution.py:584
  38.4 9.4 %all-to-all-start.1 = ((f32[8,32,128]{2,1,0:T(8,128)}), f32[8,32,128]{2,1,0:T(8,128)S(1)}, u32[]{:S(2)}, u32[]{:S(2)}) async-start(f32[8,32,128]{2,1,0:T(8,128)} %get-tuple-element.23), calls=%async_computation.1 | async-start | bytes 262144 | tf_op jit(solution)/shard_map/all_to_all | solution.py:41
  72.9 32.6 %copy-start = (bf16[4,1,128,3072]{3,2,1,0:T(8,128)(2,1)S(1)}, bf16[4,1,128,3072]{3,2,1,0:T(8,128)(2,1)}, u32[]{:S(2)}) copy-start(bf16[4,1,128,3072]{3,2,1,0:T(8,128)(2,1)} %param.6) | copy-start | bytes 9437188
  105.5 2.3 %collective-permute-start.5 = (f32[64,8,384]{2,1,0:T(8,128)S(1)}, f32[64,8,384]{2,1,0:T(8,128)S(1)}, u32[]{:S(2)}, u32[]{:S(2)}) collective-permute-start(f32[64,8,384]{2,1,0:T(8,128)S(1)} %all_to_all.27), channel_id=1, source_target_pairs={{0,1},{1,0},{2,3},{3,2},{4,5},{5,4},{6,7},{7,6},{8,9},{9,8},{10,11... | collective-permute-start | bytes 2359304 | tf_op jit(solution)/shard_map/ppermute | solution.py:37
